TPU v7x, 32 devices: a whole 2x2x4 slice. The times are simulated.
32 devices in a mesh: slab: 8 (over z, y), sub: 4 (over x, core).
Axes of the slice: x: 2, y: 2, z: 4, core: 2. Of those that a mesh axis runs over, the one named last changes fastest.
Arguments:
- populations: float32 [19, 8, 128, 128], P(None, 'slab', 'sub'), may hold values from 0.5 to 1.5
- marker_cell: int32 [8, 4, 256, 128], P('slab', 'sub'), may hold values from 0 to 4095
- marker_count: int32 [8, 4, 256], P('slab', 'sub'), may hold values from 1 to 128
- particle_count: int32 [8, 4], P('slab', 'sub'), may hold values from 32 to 256, as said below
- particle_id: int32 [8, 4, 256], P('slab', 'sub'), may hold values from 0 to 2047, as said below
- owner_table: int32 [4, 8], P('sub'), may hold values from 0 to 7, as said below
- particle_velocity: float32 [8, 4, 3, 256], P('slab', 'sub'), may hold values from -0.3 to 0.3
- pair_list: int32 [8, 4, 256, 4], P('slab', 'sub'), may hold values from 0 to 255, as said below
- pair_gap: float32 [8, 4, 256, 4], P('slab', 'sub'), may hold values from 0.25 to 4
- self_coupling: bfloat16 [128, 128], replicated, may hold values from -2 to 16
- pair_coupling: bfloat16 [128, 128], replicated, may hold values from -1 to 6
Outputs:
- read: float32 [19, 8, 128, 128], P(None, 'slab', 'sub')
- marker_force: bfloat16 [8, 4, 256, 3, 128], P('slab', 'sub')
Inputs may be any that keep to these rules, and one draw needn't show every extreme that they name: `particle_count`: A holder's live particles fill its first slots; in every sub index some holder has 256 live particles. `particle_id`: live slots of one sub index hold distinct ids; a live slot's particle is owned by slab index owner_table[j, id // 256] of the same sub index j. At most 32 live particles of one holder belong to one owner, and in every draw some holder sends exactly 32 to every owner. Dead slots hold arbitrary ids. `owner_table`: each row is a permutation of the slab indices. `pair_list`: A spot never names itself.
All inputs are finite; a program needn't handle non-finite values.
Results may differ from a plain program's by a relative error of at most 0.0053.
Values may be sent and summed in bfloat16 or wider, within the bound.
No kernel may reach another device: no remote copies, remote signals or barrier semaphores. Data moves between devices by JAX's collectives and lax.ppermute only.
A program may use at most 64 MiB of HBM per device.

v0:
```python
import math

import jax
import jax.numpy as jnp
from jax import lax
from jax.sharding import PartitionSpec as P

lattice_dirs = [
    (0, 0, 0),
    (1, 0, 0),
    (-1, 0, 0),
    (0, 1, 0),
    (0, -1, 0),
    (0, 0, 1),
    (0, 0, -1),
    (1, 1, 0),
    (-1, -1, 0),
    (1, -1, 0),
    (-1, 1, 0),
    (1, 0, 1),
    (-1, 0, -1),
    (1, 0, -1),
    (-1, 0, 1),
    (0, 1, 1),
    (0, -1, -1),
    (0, 1, -1),
    (0, -1, 1),
]
lattice_weights = [1.0 / 3.0] + [1.0 / 18.0] * 6 + [1.0 / 36.0] * 12
opposite_of = [0, 2, 1, 4, 3, 6, 5, 8, 7, 10, 9, 12, 11, 14, 13, 16, 15, 18, 17]
relax_rate = 1.25
forward_x = [1, 7, 9, 11, 13]
backward_x = [2, 8, 10, 12, 14]
marker_block_most = 4096


def shifted(value, axis, steps):
    count = lax.axis_size(axis)
    pairs = [(source, (source + steps) % count) for source in range(count)]
    return lax.ppermute(value, axis, pairs)


def extended(block, sides, width):
    for axis, dim in sides:
        count = lax.axis_size(axis)
        forward = [(i, i + 1) for i in range(count - 1)]
        backward = [(target, source) for source, target in forward]
        low = lax.ppermute(
            lax.slice_in_dim(block, block.shape[dim] - width, None, axis=dim), axis, forward
        )
        high = lax.ppermute(lax.slice_in_dim(block, 0, width, axis=dim), axis, backward)
        block = jnp.concatenate([low, block, high], axis=dim)
    return block


def moments(populations):
    dirs_table = jnp.array(lattice_dirs, jnp.float32)
    density = jnp.sum(populations, axis=0)
    moment = jnp.einsum("ic,i...->c...", dirs_table, populations, precision=lax.Precision.HIGHEST)
    return (density, moment)


def collide(populations, density, moment, body_force):
    dirs_table = jnp.array(lattice_dirs, jnp.float32)
    weight_col = jnp.array(lattice_weights, jnp.float32).reshape(
        (19,) + (1,) * (populations.ndim - 1)
    )
    velocity = (moment + 0.5 * body_force) / density
    along = jnp.einsum("ic,c...->i...", dirs_table, velocity, precision=lax.Precision.HIGHEST)
    push = jnp.einsum("ic,c...->i...", dirs_table, body_force, precision=lax.Precision.HIGHEST)
    speed_sq = jnp.sum(velocity * velocity, axis=0)
    work_rate = jnp.sum(velocity * body_force, axis=0)
    equilibrium = weight_col * density * (1.0 + 3.0 * along + 4.5 * along * along - 1.5 * speed_sq)
    source = (1.0 - 0.5 * relax_rate) * weight_col * (3.0 * (push - work_rate) + 9.0 * along * push)
    return populations - relax_rate * (populations - equilibrium) + source


def lubricate(owned, partner_index, partner_gap, self_coupling, pair_coupling):
    marker_width = owned.shape[-1]
    partners = owned[partner_index]
    weighted = jnp.sum(partners.astype(jnp.float32) / partner_gap[:, :, None, None], axis=1).astype(
        jnp.bfloat16
    )
    direct = jnp.dot(
        owned.reshape(-1, marker_width), self_coupling, preferred_element_type=jnp.float32
    )
    coupled = jnp.dot(
        weighted.reshape(-1, marker_width), pair_coupling, preferred_element_type=jnp.float32
    )
    return (direct + coupled).astype(jnp.bfloat16).reshape(owned.shape)


def cell_picks(cells, row_total, cell_depth, pick_type):
    row_pick = (cells // cell_depth)[:, None] == jnp.arange(row_total, dtype=jnp.int32)[None, :]
    depth_pick = (cells % cell_depth)[:, None] == jnp.arange(cell_depth, dtype=jnp.int32)[None, :]
    return (row_pick.astype(pick_type), depth_pick)


def sample_markers(flow_field, flat_cells, row_total, cell_depth, block_size):

    def sample_block(cells):
        row_pick, depth_pick = cell_picks(cells, row_total, cell_depth, jnp.float32)
        picked_rows = jnp.dot(
            row_pick,
            flow_field,
            precision=lax.Precision.HIGHEST,
            preferred_element_type=jnp.float32,
        ).reshape(block_size, 3, cell_depth)
        return jnp.sum(jnp.where(depth_pick[:, None, :], picked_rows, 0.0), axis=2)

    return lax.map(sample_block, flat_cells.reshape(-1, block_size)).reshape(-1, 3)


def spread_markers(force_terms, flat_cells, row_total, cell_depth, block_size):

    def spread_block(total, operands):
        cells, terms = operands
        row_pick, depth_pick = cell_picks(cells, row_total, cell_depth, jnp.bfloat16)
        placed = jnp.where(depth_pick[:, None, :], terms[:, :, None], jnp.zeros((), jnp.bfloat16))
        placed = placed.reshape(block_size, 3 * cell_depth)
        part_sum = lax.dot_general(
            row_pick, placed, (((0,), (0,)), ((), ())), preferred_element_type=jnp.float32
        )
        return (total + part_sum, None)

    start = jnp.zeros((row_total, 3 * cell_depth), jnp.float32)
    total, unused = lax.scan(
        spread_block,
        start,
        (flat_cells.reshape(-1, block_size), force_terms.reshape(-1, block_size, 3)),
    )
    return total


def stream_block(padded, collided, sub_position, sub_total):
    planes, rows_y = (collided.shape[1], collided.shape[2])
    outputs = []
    for number in range(19):
        step_x, step_y, step_z = lattice_dirs[number]
        moved = padded[
            number, 1 - step_x : 1 - step_x + planes, 1 - step_y : 1 - step_y + rows_y, :
        ]
        moved = jnp.roll(moved, step_z, axis=2)
        if step_y != 0:
            edge_row = 0 if step_y == 1 else rows_y - 1
            wall_device = sub_position == (0 if step_y == 1 else sub_total - 1)
            at_wall = (jnp.arange(rows_y) == edge_row)[None, :, None] & wall_device
            moved = jnp.where(at_wall, collided[opposite_of[number]], moved)
        outputs.append(moved)
    return jnp.stack(outputs)


def per_device(
    populations,
    marker_cell,
    marker_count,
    particle_count,
    particle_id,
    owner_table,
    particle_velocity,
    pair_list,
    pair_gap,
    self_coupling,
    pair_coupling,
):
    slab_count = lax.axis_size("slab")
    cell_index = marker_cell[0, 0]
    slot_count, marker_width = cell_index.shape
    capacity = slot_count // slab_count
    buffer_rows = slab_count * capacity
    cell_depth = populations.shape[3]
    row_total = populations.shape[1] * populations.shape[2]
    marker_total = slot_count * marker_width
    block_size = math.gcd(marker_total, marker_block_most)
    density, moment = moments(populations)
    fluid_flow = (moment / density).reshape(3, row_total, cell_depth)
    flow_field = jnp.transpose(fluid_flow, (1, 0, 2)).reshape(row_total, 3 * cell_depth)
    flat_cells = cell_index.reshape(-1)
    sampled = sample_markers(flow_field, flat_cells, row_total, cell_depth, block_size)
    sampled = jnp.transpose(sampled.reshape(slot_count, marker_width, 3), (0, 2, 1))
    slot_index = jnp.arange(slot_count, dtype=jnp.int32)
    alive_slot = slot_index < particle_count[0, 0]
    marker_index = jnp.arange(marker_width, dtype=jnp.int32)
    live_marker = alive_slot[:, None] & (marker_index[None, :] < marker_count[0, 0][:, None])
    target_speed = jnp.transpose(particle_velocity[0, 0])[:, :, None]
    slip_value = jnp.where(live_marker[:, None, :], target_speed - sampled, 0.0).astype(
        jnp.bfloat16
    )
    identities = particle_id[0, 0]
    slab_range = jnp.arange(slab_count, dtype=jnp.int32)
    range_match = (identities // slot_count)[:, None] == slab_range[None, :]
    owner_slab = jnp.sum(jnp.where(range_match, owner_table[0][None, :], 0), axis=1)
    chosen = ((owner_slab[:, None] == slab_range[None, :]) & alive_slot[:, None]).astype(jnp.int32)
    earlier = jnp.cumsum(chosen, axis=0) - chosen
    position = jnp.sum(earlier * chosen, axis=1)
    send_row = jnp.where(alive_slot, owner_slab * capacity + position, buffer_rows)
    out_slip = (
        jnp.zeros((buffer_rows, 3, marker_width), jnp.bfloat16)
        .at[send_row]
        .set(slip_value, mode="drop")
    )
    out_spot = (
        jnp.full((buffer_rows,), -1, jnp.int32)
        .at[send_row]
        .set(identities % slot_count, mode="drop")
    )
    got_slip, got_spot = (
        lax.all_to_all(
            out_slip.reshape(slab_count, capacity, 3, marker_width),
            "slab",
            split_axis=0,
            concat_axis=0,
            tiled=True,
        ),
        lax.all_to_all(
            out_spot.reshape(slab_count, capacity), "slab", split_axis=0, concat_axis=0, tiled=True
        ),
    )
    got_spot = got_spot.reshape(-1)
    landing = jnp.where(got_spot >= 0, got_spot, slot_count)
    owned = (
        jnp.zeros((slot_count, 3, marker_width), jnp.bfloat16)
        .at[landing]
        .set(got_slip.reshape(-1, 3, marker_width), mode="drop")
    )
    correction = lubricate(owned, pair_list[0, 0], pair_gap[0, 0], self_coupling, pair_coupling)
    reply_rows = correction[jnp.minimum(landing, slot_count - 1)]
    returned = lax.all_to_all(
        reply_rows.reshape(slab_count, capacity, 3, marker_width),
        "slab",
        split_axis=0,
        concat_axis=0,
        tiled=True,
    )
    own_rows = returned.reshape(buffer_rows, 3, marker_width)[
        jnp.minimum(send_row, buffer_rows - 1)
    ]
    marker_force = jnp.where(live_marker[:, None, :], own_rows, 0.0)
    force_terms = jnp.transpose(marker_force, (0, 2, 1)).reshape(marker_total, 3)
    force_rows = spread_markers(force_terms, flat_cells, row_total, cell_depth, block_size)
    body_force = jnp.transpose(force_rows.reshape(row_total, 3, cell_depth), (1, 0, 2)).reshape(
        moment.shape
    )
    collided = collide(populations, density, moment, body_force)
    forward_rows = jnp.array(forward_x, jnp.int32)
    backward_rows = jnp.array(backward_x, jnp.int32)
    ahead = shifted(collided[forward_rows].astype(jnp.bfloat16), "slab", 1).astype(jnp.float32)
    behind = shifted(collided[backward_rows].astype(jnp.bfloat16), "slab", -1).astype(jnp.float32)
    low_plane = jnp.zeros_like(collided).at[forward_rows].set(ahead)
    high_plane = jnp.zeros_like(collided).at[backward_rows].set(behind)
    widened = jnp.concatenate([low_plane, collided, high_plane], axis=1)
    padded = extended(widened, (("sub", 2),), 1)
    read = stream_block(padded, collided, lax.axis_index("sub"), lax.axis_size("sub"))
    return (read, marker_force[None, None])


def solution(mesh):
    placed = (
        P(None, "slab", "sub", None),
        P("slab", "sub", None, None),
        P("slab", "sub", None),
        P("slab", "sub"),
        P("slab", "sub", None),
        P("sub", None),
        P("slab", "sub", None, None),
        P("slab", "sub", None, None),
        P("slab", "sub", None, None),
        P(),
        P(),
    )
    return jax.shard_map(
        per_device,
        mesh=mesh,
        in_specs=placed,
        out_specs=(P(None, "slab", "sub", None), P("slab", "sub", None, None, None)),
        check_vma=False,
    )
```

profile of v0, /device:TPU:1, one launch (start us, length us, event | category | flops | bytes accessed | tf_op | source)
XLA Modules:
  0.0 161.1 jit_solution(8945607689649256846)
XLA Ops:
  3.7 1.4 scatter_custom_fusion
  5.8 6.4 %all-to-all-start = ((s32[8,1,32]{2,1,0:T(1,128)}), s32[8,1,32]{2,1,0:T(1,128)S(1)}, u32[]{:S(2)}, u32[]{:S(2)}) async-start(s32[8,1,32]{2,1,0:T(1,128)} %all_to_all.12), calls=%async_computation | async-start | bytes 8192 | tf_op jit(solution)/shard_map/all_to_all | solution.py:215
  14.0 2.1 %broadcast_divide_fusion = (f32[3,32,128]{2,0,1:T(4,128)S(1)}, f32[3,32,128]{2,0,1:T(4,128)}) fusion(f32[32,128]{1,0:T(8,128)S(1)} %reduce_sum.66, f32[19,3,1]{0,1,2:T(4,128)} %constant.229, f32[19,32,128]{2,1,0:T(8,128)} %bitcast.213), kind=kOutput, calls=%fused_computation.93 | convolution fusion | flops 2813952 | bytes 426212 | tf_op jit(solution)/shard_map/ic,i...->c.../dot_general | solution.py:59
  16.1 1.6 reshape_reshape_squeeze.4
  17.7 37.7 %while.25 = (s32[]{:T(128)}, f32[8,4096,3]{1,2,0:T(4,128)S(1)}, s32[8,4096]{1,0:T(8,128)}, f32[32,384]{1,0:T(8,128)S(1)}, s32[]{:T(128)}) while((s32[]{:T(128)}, f32[8,4096,3]{1,2,0:T(4,128)S(1)}, s32[8,4096]{1,0:T(8,128)}, f32[32,384]{1,0:T(8,128)S(1)}, s32[]{:T(128)}) %tuple.101), condition=%wide.region_8.9_spmd, body=%wide.region_6.8_spmd.sunk | while | flops 607846400 | bytes 13975621 | solution.py:111
  18.7 2.7 %fusion.56 = f32[4096,384]{0,1:T(8,128)S(1)} fusion(f32[32,384]{1,0:T(8,128)S(1)} %get-tuple-element.300, s32[4096]{0:T(1024)S(1)} %get-tuple-element.279), kind=kOutput, calls=%fused_computation.13.clone.1 | convolution fusion | flops 604110848 | bytes 6356992 | tf_op jit(solution)/shard_map/while/body/eval_jaxpr/dot_general | solution.py:103
  23.4 2.7 %fusion.56 = f32[4096,384]{0,1:T(8,128)S(1)} fusion(f32[32,384]{1,0:T(8,128)S(1)} %get-tuple-element.300, s32[4096]{0:T(1024)S(1)} %get-tuple-element.279), kind=kOutput, calls=%fused_computation.13.clone.1 | convolution fusion | flops 604110848 | bytes 6356992 | tf_op jit(solution)/shard_map/while/body/eval_jaxpr/dot_general | solution.py:103
  28.1 2.7 %fusion.56 = f32[4096,384]{0,1:T(8,128)S(1)} fusion(f32[32,384]{1,0:T(8,128)S(1)} %get-tuple-element.300, s32[4096]{0:T(1024)S(1)} %get-tuple-element.279), kind=kOutput, calls=%fused_computation.13.clone.1 | convolution fusion | flops 604110848 | bytes 6356992 | tf_op jit(solution)/shard_map/while/body/eval_jaxpr/dot_general | solution.py:103
  32.8 2.7 %fusion.56 = f32[4096,384]{0,1:T(8,128)S(1)} fusion(f32[32,384]{1,0:T(8,128)S(1)} %get-tuple-element.300, s32[4096]{0:T(1024)S(1)} %get-tuple-element.279), kind=kOutput, calls=%fused_computation.13.clone.1 | convolution fusion | flops 604110848 | bytes 6356992 | tf_op jit(solution)/shard_map/while/body/eval_jaxpr/dot_general | solution.py:103
  37.5 2.7 %fusion.56 = f32[4096,384]{0,1:T(8,128)S(1)} fusion(f32[32,384]{1,0:T(8,128)S(1)} %get-tuple-element.300, s32[4096]{0:T(1024)S(1)} %get-tuple-element.279), kind=kOutput, calls=%fused_computation.13.clone.1 | convolution fusion | flops 604110848 | bytes 6356992 | tf_op jit(solution)/shard_map/while/body/eval_jaxpr/dot_general | solution.py:103
  42.2 2.7 %fusion.56 = f32[4096,384]{0,1:T(8,128)S(1)} fusion(f32[32,384]{1,0:T(8,128)S(1)} %get-tuple-element.300, s32[4096]{0:T(1024)S(1)} %get-tuple-element.279), kind=kOutput, calls=%fused_computation.13.clone.1 | convolution fusion | flops 604110848 | bytes 6356992 | tf_op jit(solution)/shard_map/while/body/eval_jaxpr/dot_general | solution.py:103
  46.9 2.7 %fusion.56 = f32[4096,384]{0,1:T(8,128)S(1)} fusion(f32[32,384]{1,0:T(8,128)S(1)} %get-tuple-element.300, s32[4096]{0:T(1024)S(1)} %get-tuple-element.279), kind=kOutput, calls=%fused_computation.13.clone.1 | convolution fusion | flops 604110848 | bytes 6356992 | tf_op jit(solution)/shard_map/while/body/eval_jaxpr/dot_general | solution.py:103
  51.6 2.7 %fusion.56 = f32[4096,384]{0,1:T(8,128)S(1)} fusion(f32[32,384]{1,0:T(8,128)S(1)} %get-tuple-element.300, s32[4096]{0:T(1024)S(1)} %get-tuple-element.279), kind=kOutput, calls=%fused_computation.13.clone.1 | convolution fusion | flops 604110848 | bytes 6356992 | tf_op jit(solution)/shard_map/while/body/eval_jaxpr/dot_general | solution.py:103
  56.0 7.3 %scatter_fusion = bf16[256,3,128]{2,1,0:T(4,128)(2,1)S(1)} fusion(bf16[256,3,128]{2,1,0:T(4,128)(2,1)S(1)} %broadcast.570.clone, s32[256]{0:T(256)S(1)} %bitcast.229, bf16[256,3,128]{2,1,0:T(4,128)(2,1)S(1)} %fusion.19), kind=kCustom, calls=%fused_computation.6 | custom fusion | bytes 590848 | tf_op jit(solution)/shard_map/scatter | solution.py:200
  64.3 5.4 %all-to-all-start.1 = ((bf16[8,32,3,128]{3,1,2,0:T(8,128)(2,1)}), bf16[8,32,3,128]{3,1,2,0:T(8,128)(2,1)S(1)}, u32[]{:S(2)}, u32[]{:S(2)}) async-start(bf16[8,32,3,128]{3,1,2,0:T(8,128)(2,1)} %copy.353), calls=%async_computation.1 | async-start | bytes 393216 | tf_op jit(solution)/shard_map/all_to_all | solution.py:208
  71.2 5.2 %all-to-all-done.1 = bf16[8,32,3,128]{3,1,2,0:T(8,128)(2,1)S(1)} async-done(((bf16[8,32,3,128]{3,1,2,0:T(8,128)(2,1)}), bf16[8,32,3,128]{3,1,2,0:T(8,128)(2,1)S(1)}, u32[]{:S(2)}, u32[]{:S(2)}) %all-to-all-start.1) | async-done | bytes 196640 | tf_op jit(solution)/shard_map/all_to_all | solution.py:208
  76.6 7.3 %scatter_fusion.1 = bf16[256,3,128]{2,1,0:T(4,128)(2,1)S(1)} fusion(bf16[256,3,128]{2,1,0:T(4,128)(2,1)S(1)} %broadcast.570, s32[256]{0:T(256)S(1)} %bitcast.230, bf16[256,3,128]{2,1,0:T(4,128)(2,1)S(1)} %bitcast.217), kind=kCustom, calls=%fused_computation.7 | custom fusion | bytes 590848 | tf_op jit(solution)/shard_map/scatter | solution.py:224
  84.1 3.6 %gather_fusion = bf16[1024,3,128]{2,1,0:T(4,128)(2,1)S(1)} fusion(bf16[256,3,128]{2,1,0:T(4,128)(2,1)S(1)} %scatter_fusion.1, s32[1024]{0:T(1024)S(1)} %broadcast_clamp_fusion), kind=kCustom, calls=%fused_computation | custom fusion | bytes 1576960 | tf_op jit(solution)/shard_map/gather | solution.py:80
  87.7 1.7 %fusion.7 = bf16[256,3,128]{2,1,0:T(4,128)(2,1)S(1)} fusion(f32[256,4]{1,0:T(8,128)S(1)} %copy.356, bf16[1024,3,128]{2,1,0:T(4,128)(2,1)S(1)} %gather_fusion), kind=kLoop, calls=%fused_computation.41 | loop fusion | flops 1081344 | bytes 987136 | tf_op jit(solution)/shard_map/reduce_sum | solution.py:81
  91.7 4.2 %all-to-all-start.2 = ((bf16[8,32,3,128]{3,1,2,0:T(8,128)(2,1)}), bf16[8,32,3,128]{3,1,2,0:T(8,128)(2,1)S(1)}, u32[]{:S(2)}, u32[]{:S(2)}) async-start(bf16[8,32,3,128]{3,1,2,0:T(8,128)(2,1)} %copy.357), calls=%async_computation.2 | async-start | bytes 393216 | tf_op jit(solution)/shard_map/all_to_all | solution.py:228
  97.6 4.9 %all-to-all-done.2 = bf16[8,32,3,128]{3,1,2,0:T(8,128)(2,1)S(1)} async-done(((bf16[8,32,3,128]{3,1,2,0:T(8,128)(2,1)}), bf16[8,32,3,128]{3,1,2,0:T(8,128)(2,1)S(1)}, u32[]{:S(2)}, u32[]{:S(2)}) %all-to-all-start.2) | async-done | bytes 196640 | tf_op jit(solution)/shard_map/all_to_all | solution.py:228
  105.5 28.6 %while.26 = (s32[]{:T(128)}, f32[32,384]{1,0:T(8,128)S(1)}, s32[8,4096]{1,0:T(8,128)}, bf16[8,4096,3]{1,2,0:T(4,128)(2,1)}, s32[]{:T(128)}, /*index=5*/s32[]{:T(128)}) while((s32[]{:T(128)}, f32[32,384]{1,0:T(8,128)S(1)}, s32[8,4096]{1,0:T(8,128)}, bf16[8,4096,3]{1,2,0:T(4,128)(2,1)}, s32[]{:T(128)}, /*index=5*/s32[]{:T(128)}) %tuple.98), condition=%wide.region_13.14_spmd.clone, body=%wide.region_12.13_spmd.clone.sunk | while | flops 102993920 | bytes 7626839 | solution.py:127
  111.7 1.0 convolution_add_fusion.3
  118.8 1.0 convolution_add_fusion.3
  126.0 1.0 convolution_add_fusion.3
  133.1 1.0 convolution_add_fusion.3
  134.3 1.3 fusion.21
  136.5 1.2 fusion.41
  140.2 4.2 %collective-permute-start.1 = (bf16[5,1,32,128]{3,2,0,1:T(8,128)(2,1)S(1)}, bf16[5,1,32,128]{3,2,0,1:T(8,128)(2,1)S(1)}, u32[]{:S(2)}, u32[]{:S(2)}) collective-permute-start(bf16[5,1,32,128]{3,2,0,1:T(8,128)(2,1)S(1)} %bitcast.224), channel_id=1, source_target_pairs={{0,28},{4,0},{8,4},{12,8},{16,12},{20,16},{24,20},{28,24},{1,29},{... | collective-permute-start | bytes 122888 | tf_op jit(solution)/shard_map/ppermute | solution.py:40
  147.0 6.7 %collective-permute-start.2 = (f32[19,3,1,128]{3,2,1,0:T(1,128)S(1)}, f32[19,3,1,128]{3,2,1,0:T(1,128)S(1)}, u32[]{:S(2)}, u32[]{:S(2)}) collective-permute-start(f32[19,3,1,128]{3,2,1,0:T(1,128)S(1)} %get-tuple-element.205), channel_id=1, source_target_pairs={{0,1},{1,2},{2,3},{4,5},{5,6},{6,7},{8,9},{9,10},{10,11},{12,13},{... | collective-permute-start | bytes 87560 | tf_op jit(solution)/shard_map/ppermute | solution.py:48
  153.7 1.9 %collective-permute-start.3 = (f32[19,3,1,128]{3,2,1,0:T(1,128)S(1)}, f32[19,3,1,128]{3,2,1,0:T(1,128)S(1)}, u32[]{:S(2)}, u32[]{:S(2)}) collective-permute-start(f32[19,3,1,128]{3,2,1,0:T(1,128)S(1)} %get-tuple-element.204), channel_id=1, source_target_pairs={{1,0},{2,1},{3,2},{5,4},{6,5},{7,6},{9,8},{10,9},{11,10},{13,12},{... | collective-permute-start | bytes 87560 | tf_op jit(solution)/shard_map/ppermute | solution.py:51
  155.9 3.0 %collective-permute-done.3 = f32[19,3,1,128]{3,2,1,0:T(1,128)S(1)} collective-permute-done((f32[19,3,1,128]{3,2,1,0:T(1,128)S(1)}, f32[19,3,1,128]{3,2,1,0:T(1,128)S(1)}, u32[]{:S(2)}, u32[]{:S(2)}) %collective-permute-start.3) | collective-permute-done | bytes 29216 | tf_op jit(solution)/shard_map/ppermute | solution.py:51
  (216 shorter events, 63.6 us)
Async XLA Ops:
  0.6 88.9 %copy-start = (bf16[128,128]{1,0:T(8,128)(2,1)S(1)}, bf16[128,128]{1,0:T(8,128)(2,1)}, u32[]{:S(2)}) copy-start(bf16[128,128]{1,0:T(8,128)(2,1)} %param.29) | copy-start | bytes 98308
  5.8 58.5 %all-to-all-start = ((s32[8,1,32]{2,1,0:T(1,128)}), s32[8,1,32]{2,1,0:T(1,128)S(1)}, u32[]{:S(2)}, u32[]{:S(2)}) async-start(s32[8,1,32]{2,1,0:T(1,128)} %all_to_all.12), calls=%async_computation | async-start | bytes 8192 | tf_op jit(solution)/shard_map/all_to_all | solution.py:215
  14.0 2.1 %copy-start.3 = (f32[32,128]{1,0:T(8,128)}, f32[32,128]{1,0:T(8,128)S(1)}, u32[]{:S(2)}) copy-start(f32[32,128]{1,0:T(8,128)S(1)} %reduce_sum.66) | copy-start | bytes 49156
  17.7 37.7 %copy-start.9 = (f32[1,1,3,256]{3,1,2,0:T(1,128)S(1)}, f32[1,1,3,256]{3,1,2,0:T(1,128)}, u32[]{:S(2)}) copy-start(f32[1,1,3,256]{3,1,2,0:T(1,128)} %param.26) | copy-start | bytes 9220
  17.7 38.2 %copy-start.8 = (s32[1,1,256,4]{2,3,1,0:T(4,128)S(1)}, s32[1,1,256,4]{2,3,1,0:T(4,128)}, u32[]{:S(2)}) copy-start(s32[1,1,256,4]{2,3,1,0:T(4,128)} %param.27) | copy-start | bytes 12292
  56.0 13.8 %copy-start.7 = (f32[1,1,256,4]{2,3,1,0:T(4,128)S(1)}, f32[1,1,256,4]{2,3,1,0:T(4,128)}, u32[]{:S(2)}) copy-start(f32[1,1,256,4]{2,3,1,0:T(4,128)} %param.28) | copy-start | bytes 12292
  64.3 12.1 %all-to-all-start.1 = ((bf16[8,32,3,128]{3,1,2,0:T(8,128)(2,1)}), bf16[8,32,3,128]{3,1,2,0:T(8,128)(2,1)S(1)}, u32[]{:S(2)}, u32[]{:S(2)}) async-start(bf16[8,32,3,128]{3,1,2,0:T(8,128)(2,1)} %copy.353), calls=%async_computation.1 | async-start | bytes 393216 | tf_op jit(solution)/shard_map/all_to_all | solution.py:208
  76.5 13.2 %copy-start.4 = (bf16[128,128]{1,0:T(8,128)(2,1)S(1)}, bf16[128,128]{1,0:T(8,128)(2,1)}, u32[]{:S(2)}) copy-start(bf16[128,128]{1,0:T(8,128)(2,1)} %param.30) | copy-start | bytes 98308
  87.7 9.3 %copy-start.10 = (s32[5]{0:T(128)S(1)}, s32[5]{0:T(128)}, u32[]{:S(2)}) copy-start(s32[5]{0:T(128)} %constant.227) | copy-start | bytes 64
  87.7 9.3 %copy-start.12 = (s32[5]{0:T(128)S(1)}, s32[5]{0:T(128)}, u32[]{:S(2)}) copy-start(s32[5]{0:T(128)} %constant.225) | copy-start | bytes 64
  91.7 10.8 %all-to-all-start.2 = ((bf16[8,32,3,128]{3,1,2,0:T(8,128)(2,1)}), bf16[8,32,3,128]{3,1,2,0:T(8,128)(2,1)S(1)}, u32[]{:S(2)}, u32[]{:S(2)}) async-start(bf16[8,32,3,128]{3,1,2,0:T(8,128)(2,1)} %copy.357), calls=%async_computation.2 | async-start | bytes 393216 | tf_op jit(solution)/shard_map/all_to_all | solution.py:228
  105.5 32.2 %copy-start.1 = (f32[19,1,32,128]{3,2,1,0:T(8,128)S(1)}, f32[19,1,32,128]{3,2,1,0:T(8,128)}, u32[]{:S(2)}) copy-start(f32[19,1,32,128]{3,2,1,0:T(8,128)} %param.20) | copy-start | bytes 933892
  134.2 10.2 %copy-start.2 = (bf16[1,1,256,3,128]{4,3,2,1,0:T(4,128)(2,1)S(1)}, bf16[1,1,256,3,128]{4,3,2,1,0:T(4,128)(2,1)}, u32[]{:S(2)}) copy-start(bf16[1,1,256,3,128]{4,3,2,1,0:T(4,128)(2,1)} %bitcast_select_fusion) | copy-start | bytes 589828
  134.2 11.0 %copy-start.13 = (s32[5]{0:T(128)S(1)}, s32[5]{0:T(128)}, u32[]{:S(2)}) copy-start(s32[5]{0:T(128)} %constant.225) | copy-start | bytes 64
  134.2 11.9 %copy-start.11 = (s32[5]{0:T(128)S(1)}, s32[5]{0:T(128)}, u32[]{:S(2)}) copy-start(s32[5]{0:T(128)} %constant.227) | copy-start | bytes 64
  134.2 21.4 %copy-start.5 = (pred[32]{0:T(512)(128)(4,1)S(1)}, pred[32]{0:T(512)(128)(4,1)}, u32[]{:S(2)}) copy-start(pred[32]{0:T(512)(128)(4,1)} %compare_and_fusion.1) | copy-start | bytes 100
  136.5 22.4 %copy-start.6 = (pred[32]{0:T(512)(128)(4,1)S(1)}, pred[32]{0:T(512)(128)(4,1)}, u32[]{:S(2)}) copy-start(pred[32]{0:T(512)(128)(4,1)} %compare_and_fusion) | copy-start | bytes 100
  139.4 5.7 %collective-permute-start = (bf16[5,1,32,128]{3,2,0,1:T(8,128)(2,1)S(1)}, bf16[5,1,32,128]{3,2,0,1:T(8,128)(2,1)S(1)}, u32[]{:S(2)}, u32[]{:S(2)}) collective-permute-start(bf16[5,1,32,128]{3,2,0,1:T(8,128)(2,1)S(1)} %bitcast.225), channel_id=1, source_target_pairs={{0,4},{4,8},{8,12},{12,16},{16,20},{20,24},{24,28},{28,0},{1,5},{5... | collective-permute-start | bytes 122888 | tf_op jit(solution)/shard_map/ppermute | solution.py:40
  140.2 5.8 %collective-permute-start.1 = (bf16[5,1,32,128]{3,2,0,1:T(8,128)(2,1)S(1)}, bf16[5,1,32,128]{3,2,0,1:T(8,128)(2,1)S(1)}, u32[]{:S(2)}, u32[]{:S(2)}) collective-permute-start(bf16[5,1,32,128]{3,2,0,1:T(8,128)(2,1)S(1)} %bitcast.224), channel_id=1, source_target_pairs={{0,28},{4,0},{8,4},{12,8},{16,12},{20,16},{24,20},{28,24},{1,29},{... | collective-permute-start | bytes 122888 | tf_op jit(solution)/shard_map/ppermute | solution.py:40
  147.0 8.6 %collective-permute-start.2 = (f32[19,3,1,128]{3,2,1,0:T(1,128)S(1)}, f32[19,3,1,128]{3,2,1,0:T(1,128)S(1)}, u32[]{:S(2)}, u32[]{:S(2)}) collective-permute-start(f32[19,3,1,128]{3,2,1,0:T(1,128)S(1)} %get-tuple-element.205), channel_id=1, source_target_pairs={{0,1},{1,2},{2,3},{4,5},{5,6},{6,7},{8,9},{9,10},{10,11},{12,13},{... | collective-permute-start | bytes 87560 | tf_op jit(solution)/shard_map/ppermute | solution.py:48
  153.7 5.2 %collective-permute-start.3 = (f32[19,3,1,128]{3,2,1,0:T(1,128)S(1)}, f32[19,3,1,128]{3,2,1,0:T(1,128)S(1)}, u32[]{:S(2)}, u32[]{:S(2)}) collective-permute-start(f32[19,3,1,128]{3,2,1,0:T(1,128)S(1)} %get-tuple-element.204), channel_id=1, source_target_pairs={{1,0},{2,1},{3,2},{5,4},{6,5},{7,6},{9,8},{10,9},{11,10},{13,12},{... | collective-permute-start | bytes 87560 | tf_op jit(solution)/shard_map/ppermute | solution.py:51
  160.3 0.7 copy-start.14
where the time goes:
time: 163 us; the launch traced here: 161 us
  local copies, waits for them, and re-layouts  53.7 us (33%)
  matrix products  34.5 us (21%)
  starting transfers between devices  28.8 us (18%)
  other arithmetic  28.2 us (17%)
  waiting for transfers between devices  13.1 us (8%)
  between operations  1.85 us (1%)
    dot_general x8, matrix products, sample_block(): jnp.dot(row_pick, flow_field, precision=lax.Precision.HIGHEST, preferred_...  21.3 us
    dynamic_slice x16, local copies, waits for them, and re-layouts, sample_markers(): lax.map(sample_block, flat_cells.reshape(-1, block_size)).reshape(-1, 3)  14.8 us
    dot_general x8, matrix products, spread_block(): lax.dot_general(row_pick, placed, (((0,), (0,)), ((), ())), preferred_ele...  8.26 us
    scatter x1, local copies, waits for them, and re-layouts, per_device(): out_slip = jnp.zeros((buffer_rows, 3, marker_width), jnp.bfloat16).at[sen...  7.3 us
    scatter x1, local copies, waits for them, and re-layouts, per_device(): owned = jnp.zeros((slot_count, 3, marker_width), jnp.bfloat16).at[landing...  7.3 us
    ppermute x1, starting transfers between devices, extended(): lax.ppermute(lax.slice_in_dim(block, block.shape[dim] - width, None, axis...  6.68 us
    all_to_all x1, starting transfers between devices, per_device(): lax.all_to_all(out_spot.reshape(slab_count, capacity), 'slab', split_axis...  6.37 us
    broadcast_in_dim x8, local copies, waits for them, and re-layouts, spread_block(): jnp.where(depth_pick[:, None, :], terms[:, :, None], jnp.zeros((), jnp.bf...  6.21 us
  transfers between devices with their start and end apart: 7, of which 3 were waited for; matrix products, arithmetic and copies ran while one was open for 36% of the time, Pallas kernels for 0%

commit v1 on v0

v1 whole, which is shorter than its diff:
```python
import functools

import jax
import jax.numpy as jnp
from jax import lax
from jax.experimental import pallas as pl
from jax.experimental.pallas import tpu as pltpu
from jax.sharding import PartitionSpec as P

lattice_dirs = [
    (0, 0, 0),
    (1, 0, 0),
    (-1, 0, 0),
    (0, 1, 0),
    (0, -1, 0),
    (0, 0, 1),
    (0, 0, -1),
    (1, 1, 0),
    (-1, -1, 0),
    (1, -1, 0),
    (-1, 1, 0),
    (1, 0, 1),
    (-1, 0, -1),
    (1, 0, -1),
    (-1, 0, 1),
    (0, 1, 1),
    (0, -1, -1),
    (0, 1, -1),
    (0, -1, 1),
]
lattice_weights = [1.0 / 3.0] + [1.0 / 18.0] * 6 + [1.0 / 36.0] * 12
opposite_of = [0, 2, 1, 4, 3, 6, 5, 8, 7, 10, 9, 12, 11, 14, 13, 16, 15, 18, 17]
relax_rate = 1.25
forward_x = [1, 7, 9, 11, 13]
backward_x = [2, 8, 10, 12, 14]
upward_y = [3, 15, 17, 7, 10]
downward_y = [4, 16, 18, 9, 8]
BF = jnp.bfloat16
F32 = jnp.float32


def iota(shape, dim, dtype=F32):
    value = lax.broadcasted_iota(jnp.int32, shape, dim)
    return value if dtype == jnp.int32 else value.astype(F32).astype(dtype)


def dot_nt(a, b):
    return lax.dot_general(a, b, (((1,), (1,)), ((), ())), preferred_element_type=F32)


def dot_nn(a, b):
    return jnp.dot(a, b, preferred_element_type=F32)


def moments_of(pops):
    density = pops[0]
    moment = [None, None, None]
    for number in range(19):
        if number:
            density = density + pops[number]
        for axis in range(3):
            step = lattice_dirs[number][axis]
            if step == 0:
                continue
            if moment[axis] is None:
                moment[axis] = pops[number] if step == 1 else -pops[number]
            elif step == 1:
                moment[axis] = moment[axis] + pops[number]
            else:
                moment[axis] = moment[axis] - pops[number]
    return density, moment


def one_hot_rows(row, count, kind=BF):
    tall = jnp.broadcast_to(row, (16, row.shape[1])).astype(kind)
    one, zero = jnp.ones((), kind), jnp.zeros((), kind)
    parts = []
    for start in range(0, count, 16):
        number = iota((16, row.shape[1]), 0, F32) + float(start)
        parts.append(jnp.where(number.astype(kind) == tall, one, zero))
    return jnp.concatenate(parts, axis=0)


def sample_kernel(
    slab_count,
    packed,
    count_ref,
    table_ref,
    pops_ref,
    cell_ref,
    marker_count_ref,
    id_ref,
    velocity_ref,
    slip_ref,
    *rest,
):
    if packed:
        cols_ref, z_ref, y_ref, sampled_ref = rest
    else:
        spot_ref, cols_ref, z_ref, y_ref, sampled_ref = rest
    slots, width = cell_ref.shape
    rows, depth = pops_ref.shape[1:]
    capacity = slots // slab_count

    density, moment = moments_of([pops_ref[number] for number in range(19)])
    flow = jnp.concatenate([part / density for part in moment], axis=0)
    high = flow.astype(BF)
    low = (flow - high.astype(F32)).astype(BF)
    flow_pair = jnp.concatenate([high, low], axis=1)

    cells = cell_ref[...]
    z_ref[...] = (cells % depth).astype(F32)
    y_ref[...] = (cells // depth).astype(F32)

    group = 8

    def sample_group(step, carry):
        base = pl.multiple_of(step * group, group)
        z_rows = z_ref[pl.ds(base, group), :]
        y_rows = y_ref[pl.ds(base, group), :]
        parts = [[], [], []]
        for first in range(0, group, 2):
            picks = jnp.concatenate(
                [one_hot_rows(z_rows[s : s + 1], depth) for s in (first, first + 1)], axis=1
            )
            picked = dot_nn(flow_pair, jnp.concatenate([picks, picks], axis=0))
            for s in (first, first + 1):
                off = (s - first) * width
                mask = iota((rows, width), 0) == y_rows[s : s + 1]
                for c in range(3):
                    block = picked[c * rows : (c + 1) * rows, off : off + width]
                    parts[c].append(
                        jnp.sum(jnp.where(mask, block, 0.0), axis=0, keepdims=True)
                    )
        for c in range(3):
            sampled_ref[c, pl.ds(base, group), :] = jnp.concatenate(parts[c], axis=0)
        return carry

    lax.fori_loop(0, slots // group, sample_group, 0)

    lane = iota((1, slots), 1, jnp.int32)
    alive = lane < count_ref[0]
    identity = id_ref[...]
    block = identity // slots
    spot = (identity % slots).astype(F32)

    def look_up(b, owner):
        return jnp.where(block == b, table_ref[b], owner)

    owner = lax.fori_loop(0, slab_count, look_up, jnp.zeros((1, slots), jnp.int32))
    owner = jnp.where(alive, owner, -1)
    owner_f = owner.astype(F32)
    chosen = jnp.where(iota((slab_count, slots), 0) == owner_f, 1.0, 0.0)
    before = jnp.where(
        iota((slots, slots), 0) < iota((slots, slots), 1), 1.0, 0.0
    ).astype(BF)
    earlier = dot_nn(chosen.astype(BF), before)
    position = jnp.sum(chosen * earlier, axis=0, keepdims=True)
    send_row = jnp.where(alive, owner_f * float(capacity) + position, -1.0)

    count = jnp.where(alive, marker_count_ref[...], 0).astype(F32)
    velocity = velocity_ref[...]
    stack = jnp.concatenate(
        [velocity, count, send_row, jnp.zeros((3, slots), F32)], axis=0
    )
    cols = jnp.transpose(stack)
    cols_ref[...] = cols
    live = iota((slots, width), 1) < cols[:, 3:4]
    slips = []
    for c in range(3):
        slips.append(jnp.where(live, cols[:, c : c + 1] - sampled_ref[c], 0.0).astype(BF))
    place = jnp.where(iota((slots, slots), 0) == send_row, 1.0, 0.0).astype(BF)
    sent = dot_nn(place, jnp.concatenate(slips, axis=1)).astype(BF)
    where_to = jnp.where(iota((width, slots), 0) == position, 1.0, 0.0).astype(BF)
    if packed:
        for c in range(3):
            slip_ref[:, c * capacity : (c + 1) * capacity, :] = sent[
                :, c * width : (c + 1) * width
            ].reshape(slab_count, capacity, width)
        taken = (iota((slab_count * 16, slots), 0, jnp.int32) // 16).astype(F32) == owner_f
        marks = dot_nt(jnp.where(taken, spot + 1.0, 0.0).astype(BF), where_to)
        slip_ref[:, 3 * capacity :, :] = marks.astype(BF).reshape(slab_count, 16, width)
    else:
        for c in range(3):
            slip_ref[c] = sent[:, c * width : (c + 1) * width]
        marks = dot_nt((chosen * (spot + 1.0)).astype(BF), where_to)
        spot_ref[...] = marks.astype(BF)


def owner_kernel(
    slab_count,
    packed,
    *refs,
):
    if packed:
        got_ref, list_ref, gap_ref, self_ref, pair_ref, out_ref = refs
        width = got_ref.shape[2]
        slots = list_ref.shape[0]
        capacity = slots // slab_count
        got = jnp.concatenate(
            [
                got_ref[:, c * capacity : (c + 1) * capacity, :].reshape(slots, width)
                for c in range(3)
            ],
            axis=1,
        )
        per_tile = width // capacity
        lane = iota((8, width), 1, jnp.int32)
        tiles = []
        for start in range(0, slab_count, per_tile):
            total = jnp.zeros((8, width), F32)
            for source in range(start, min(start + per_tile, slab_count)):
                mark = got_ref[source, 3 * capacity : 3 * capacity + 16, :].astype(F32)[:8]
                off = (source - start) * capacity
                if off:
                    mark = pltpu.roll(mark, off, 1)
                mine = (lane >= off) & (lane < off + capacity)
                total = jnp.where(mine, mark, total)
            tiles.append(total)
        spots = jnp.concatenate(tiles, axis=1) - 1.0
    else:
        got_ref, spot_ref, list_ref, gap_ref, self_ref, pair_ref, out_ref = refs
        width = got_ref.shape[2]
        slots = list_ref.shape[0]
        got = jnp.concatenate([got_ref[c] for c in range(3)], axis=1)
        spots = jnp.broadcast_to(spot_ref[...].astype(F32), (8, slots)) - 1.0

    spot_row = spots[:1]
    spot_col = jnp.transpose(spots)[:, :1]
    land = jnp.where(iota((slots, slots), 0) == spot_row, 1.0, 0.0).astype(BF)
    reply = jnp.where(iota((slots, slots), 1) == spot_col, 1.0, 0.0).astype(BF)
    partner = list_ref[...].astype(F32)
    inverse = 1.0 / gap_ref[...]
    column = iota((slots, slots), 1)
    weight = jnp.zeros((slots, slots), F32)
    for k in range(list_ref.shape[1]):
        weight = weight + jnp.where(column == partner[:, k : k + 1], inverse[:, k : k + 1], 0.0)
    high = weight.astype(BF)
    low = (weight - high.astype(F32)).astype(BF)

    owned = dot_nn(land, got).astype(BF)
    near = (dot_nn(high, owned) + dot_nn(low, owned)).astype(BF)
    coupling = jnp.concatenate([self_ref[...], pair_ref[...]], axis=0)
    fixed = []
    for c in range(3):
        cut = slice(c * width, (c + 1) * width)
        both = jnp.concatenate([owned[:, cut], near[:, cut]], axis=1)
        fixed.append(dot_nn(both, coupling).astype(BF))
    replies = dot_nn(reply, jnp.concatenate(fixed, axis=1)).astype(BF)
    for c in range(3):
        cut = replies[:, c * width : (c + 1) * width]
        if packed:
            out_ref[:, c * capacity : (c + 1) * capacity, :] = cut.reshape(
                slab_count, capacity, width
            )
        else:
            out_ref[c] = cut


def spread_kernel(
    slab_count,
    packed,
    back_ref,
    cols_ref,
    cell_ref,
    pops_ref,
    force_out_ref,
    collided_ref,
    up_ref,
    down_ref,
    ahead_ref,
    behind_ref,
    z_ref,
    y_ref,
    force_ref,
):
    slots, width = cell_ref.shape
    rows, depth = pops_ref.shape[1:]
    capacity = slots // slab_count
    if packed:
        back = jnp.concatenate(
            [
                back_ref[:, c * capacity : (c + 1) * capacity, :].reshape(slots, width)
                for c in range(3)
            ],
            axis=1,
        )
    else:
        back = jnp.concatenate([back_ref[c] for c in range(3)], axis=1)
    cols = cols_ref[...]
    fetch = jnp.where(iota((slots, slots), 1) == cols[:, 4:5], 1.0, 0.0).astype(BF)
    own = dot_nn(fetch, back)
    live = iota((slots, width), 1) < cols[:, 3:4]
    for c in range(3):
        masked = jnp.where(live, own[:, c * width : (c + 1) * width], 0.0)
        force_ref[c] = masked
        force_out_ref[c] = masked.astype(BF)

    cells = cell_ref[...]
    z_ref[...] = (cells % depth).astype(F32)
    y_ref[...] = (cells // depth).astype(F32)

    group = 16

    def spread_group(step, total):
        base = pl.multiple_of(step * group, group)
        z_rows = z_ref[pl.ds(base, group), :]
        y_rows = y_ref[pl.ds(base, group), :]
        f_rows = [force_ref[c, pl.ds(base, group), :] for c in range(3)]
        picks, terms = [], []
        for s in range(group):
            picks.append(one_hot_rows(z_rows[s : s + 1], depth))
            tall = jnp.broadcast_to(y_rows[s : s + 1], (16, width)).astype(BF)
            parts = []
            for c in range(3):
                value = jnp.broadcast_to(f_rows[c][s : s + 1], (16, width)).astype(BF)
                for start in range(0, rows, 16):
                    number = (iota((16, width), 0) + float(start)).astype(BF)
                    parts.append(jnp.where(number == tall, value, jnp.zeros((), BF)))
            terms.append(jnp.concatenate(parts, axis=0))
        return total + dot_nt(jnp.concatenate(terms, axis=1), jnp.concatenate(picks, axis=1))

    total = lax.fori_loop(
        0, slots // group, spread_group, jnp.zeros((3 * rows, depth), F32)
    )

    force = [total[c * rows : (c + 1) * rows] for c in range(3)]
    pops = [pops_ref[number] for number in range(19)]
    density, moment = moments_of(pops)
    velocity = [(moment[c] + 0.5 * force[c]) / density for c in range(3)]
    speed_sq = velocity[0] * velocity[0] + velocity[1] * velocity[1] + velocity[2] * velocity[2]
    work_rate = velocity[0] * force[0] + velocity[1] * force[1] + velocity[2] * force[2]
    base_term = 1.0 - 1.5 * speed_sq
    for number in range(19):
        step = lattice_dirs[number]
        along, push = None, None
        for c in range(3):
            if step[c] == 0:
                continue
            v, f = (velocity[c], force[c]) if step[c] == 1 else (-velocity[c], -force[c])
            along = v if along is None else along + v
            push = f if push is None else push + f
        weight = lattice_weights[number]
        if along is None:
            equilibrium = weight * density * base_term
            source = ((1.0 - 0.5 * relax_rate) * weight * -3.0) * work_rate
        else:
            equilibrium = weight * density * (base_term + 3.0 * along + 4.5 * along * along)
            source = ((1.0 - 0.5 * relax_rate) * weight) * (
                3.0 * (push - work_rate) + 9.0 * along * push
            )
        value = pops[number] - relax_rate * (pops[number] - equilibrium) + source
        collided_ref[number] = value
        if number in forward_x:
            ahead_ref[forward_x.index(number)] = value.astype(BF)
        if number in backward_x:
            behind_ref[backward_x.index(number)] = value.astype(BF)
        if number in upward_y:
            at = upward_y.index(number)
            up_ref[at : at + 1, :] = value[rows - 1 :]
        if number in downward_y:
            at = downward_y.index(number)
            down_ref[at : at + 1, :] = value[:1]
    up_ref[5:, :] = jnp.zeros((3, depth), F32)
    down_ref[5:, :] = jnp.zeros((3, depth), F32)


def stream_kernel(
    sub_ref, collided_ref, low_ref, high_ref, ahead_ref, behind_ref, corner_f, corner_b, read_ref
):
    rows, depth = collided_ref.shape[1:]
    row = iota((rows, depth), 0, jnp.int32)
    at_low, at_high = sub_ref[0] == 0, sub_ref[0] == sub_ref[1] - 1
    low_wall = jnp.where(at_low, 1, 0)
    high_wall = jnp.where(at_high, 1, 0)
    for number in range(19):
        step_x, step_y, step_z = lattice_dirs[number]
        if step_x == 1:
            moved = ahead_ref[forward_x.index(number)].astype(F32)
        elif step_x == -1:
            moved = behind_ref[backward_x.index(number)].astype(F32)
        else:
            moved = collided_ref[number]
        if step_y != 0:
            rolled = pltpu.roll(moved, 1 if step_y == 1 else rows - 1, 0)
            edge_row = 0 if step_y == 1 else rows - 1
            if step_x == 0:
                at = (upward_y if step_y == 1 else downward_y).index(number)
                edge = (low_ref if step_y == 1 else high_ref)[at : at + 1, :]
            else:
                at = 0 if step_y == 1 else 1
                edge = (corner_f if step_x == 1 else corner_b)[at : at + 1, :]
            moved = jnp.where(row == edge_row, edge, rolled)
        if step_z != 0:
            moved = pltpu.roll(moved, 1 if step_z == 1 else depth - 1, 1)
        if step_y != 0:
            wall = low_wall if step_y == 1 else high_wall
            at_wall = (row == edge_row) & (wall == 1)
            moved = jnp.where(at_wall, collided_ref[opposite_of[number]], moved)
        read_ref[number] = moved


def whole(memory=pltpu.VMEM):
    return pl.BlockSpec(memory_space=memory)


def ring(value, axis, steps):
    count = lax.axis_size(axis)
    return lax.ppermute(value, axis, [(i, (i + steps) % count) for i in range(count)])


def per_device(
    populations,
    marker_cell,
    marker_count,
    particle_count,
    particle_id,
    owner_table,
    particle_velocity,
    pair_list,
    pair_gap,
    self_coupling,
    pair_coupling,
):
    slab_count = lax.axis_size("slab")
    slots, width = marker_cell.shape[2:]
    planes, rows, depth = populations.shape[1:]
    assert planes == 1 and slots <= 256 and slots % slab_count == 0
    capacity = slots // slab_count
    assert capacity <= width
    packed = capacity % 16 == 0 and width % capacity == 0
    pops = populations.reshape(19, rows, depth)
    cells = marker_cell.reshape(slots, width)
    shape = jax.ShapeDtypeStruct

    if packed:
        sample_out = [shape((slab_count, 3 * capacity + 16, width), BF)]
    else:
        sample_out = [shape((3, slots, width), BF), shape((slab_count, width), BF)]
    sample_out.append(shape((slots, 8), F32))
    results = pl.pallas_call(
        functools.partial(sample_kernel, slab_count, packed),
        out_shape=sample_out,
        in_specs=[whole(pltpu.SMEM)] * 2 + [whole()] * 5,
        out_specs=[whole()] * len(sample_out),
        scratch_shapes=[
            pltpu.VMEM((slots, width), F32),
            pltpu.VMEM((slots, width), F32),
            pltpu.VMEM((3, slots, width), F32),
        ],
        name="sample",
    )(
        particle_count.reshape(1),
        owner_table.reshape(slab_count),
        pops,
        cells,
        marker_count.reshape(1, slots),
        particle_id.reshape(1, slots),
        particle_velocity.reshape(3, slots),
    )
    cols = results[-1]

    def exchange(value):
        return lax.all_to_all(value, "slab", split_axis=0, concat_axis=0, tiled=True)

    def by_owner(value):
        value = value.reshape(3, slab_count, capacity, width)
        return jnp.transpose(value, (1, 0, 2, 3)).reshape(slab_count, 3 * capacity, width)

    def by_component(value):
        value = value.reshape(slab_count, 3, capacity, width)
        return jnp.transpose(value, (1, 0, 2, 3)).reshape(3, slots, width)

    if packed:
        arrived = [exchange(results[0])]
        reply_shape = shape((slab_count, 3 * capacity, width), BF)
    else:
        slip = jnp.concatenate([by_owner(results[0]), results[1][:, None, :]], axis=1)
        got = exchange(slip)
        arrived = [
            by_component(got[:, : 3 * capacity]),
            got[:, 3 * capacity, :capacity].reshape(1, slots),
        ]
        reply_shape = shape((3, slots, width), BF)
    reply = pl.pallas_call(
        functools.partial(owner_kernel, slab_count, packed),
        out_shape=reply_shape,
        in_specs=[whole()] * (len(arrived) + 4),
        out_specs=whole(),
        name="owner",
    )(
        *arrived,
        pair_list.reshape(slots, -1),
        pair_gap.reshape(slots, -1),
        self_coupling,
        pair_coupling,
    )
    back = exchange(reply) if packed else by_component(exchange(by_owner(reply)))

    marker_force, collided, up, down, ahead, behind = pl.pallas_call(
        functools.partial(spread_kernel, slab_count, packed),
        out_shape=[
            shape((3, slots, width), BF),
            shape((19, rows, depth), F32),
            shape((8, depth), F32),
            shape((8, depth), F32),
            shape((5, rows, depth), BF),
            shape((5, rows, depth), BF),
        ],
        in_specs=[whole()] * 4,
        out_specs=[whole()] * 6,
        scratch_shapes=[
            pltpu.VMEM((slots, width), F32),
            pltpu.VMEM((slots, width), F32),
            pltpu.VMEM((3, slots, width), F32),
        ],
        name="spread",
    )(back, cols, cells, pops)

    low = ring(up, "sub", 1)
    high = ring(down, "sub", -1)
    ahead = ring(ahead, "slab", 1)
    behind = ring(behind, "slab", -1)
    corner_f = ring(jnp.concatenate([low[3:4], high[3:4]]), "slab", 1)
    corner_b = ring(jnp.concatenate([low[4:5], high[4:5]]), "slab", -1)
    place = jnp.stack([lax.axis_index("sub"), jnp.int32(lax.axis_size("sub"))]).astype(jnp.int32)
    read = pl.pallas_call(
        stream_kernel,
        out_shape=shape((19, rows, depth), F32),
        in_specs=[whole(pltpu.SMEM)] + [whole()] * 7,
        out_specs=whole(),
        name="stream",
    )(place, collided, low, high, ahead, behind, corner_f, corner_b)
    marker_force = jnp.transpose(marker_force, (1, 0, 2))[None, None]
    return (read.reshape(19, 1, rows, depth), marker_force)


def solution(mesh):
    placed = (
        P(None, "slab", "sub", None),
        P("slab", "sub", None, None),
        P("slab", "sub", None),
        P("slab", "sub"),
        P("slab", "sub", None),
        P("sub", None),
        P("slab", "sub", None, None),
        P("slab", "sub", None, None),
        P("slab", "sub", None, None),
        P(),
        P(),
    )
    return jax.shard_map(
        per_device,
        mesh=mesh,
        in_specs=placed,
        out_specs=(P(None, "slab", "sub", None), P("slab", "sub", None, None, None)),
        check_vma=False,
    )
```

time: 163 us -> 68.1 us (0.42)
  the two profiles are of different devices: /device:TPU:1 before, /device:TPU:0 now
where the time goes in v1:
time: 68.1 us; the launch traced here: 67.6 us
  Pallas kernels  22.6 us (33%)
  starting transfers between devices  15.3 us (22%)
  blocking collectives  11.8 us (17%)
  waiting for transfers between devices  10.4 us (15%)
  local copies, waits for them, and re-layouts  5.4 us (8%)
  between operations  1.37 us (2%)
    all_to_all x1, blocking collectives, exchange(): lax.all_to_all(value, 'slab', split_axis=0, concat_axis=0, tiled=True)  11.8 us
    pallas_call x1, Pallas kernels, per_device(): pl.pallas_call(functools.partial(sample_kernel, slab_count, packed), out_...  10.3 us
    ppermute x6, starting transfers between devices, ring(): lax.ppermute(value, axis, [(i, (i + steps) % count) for i in range(count)])  7.86 us
    pallas_call x1, Pallas kernels, per_device(): pl.pallas_call(functools.partial(spread_kernel, slab_count, packed), out_...  7.55 us
    all_to_all x1, starting transfers between devices, exchange(): lax.all_to_all(value, 'slab', split_axis=0, concat_axis=0, tiled=True)  7.44 us
    all_to_all x1, waiting for transfers between devices, exchange(): lax.all_to_all(value, 'slab', split_axis=0, concat_axis=0, tiled=True)  6.83 us
    unnamed x23, local copies, waits for them, and re-layouts  5.39 us
    ppermute x6, waiting for transfers between devices, ring(): lax.ppermute(value, axis, [(i, (i + steps) % count) for i in range(count)])  3.61 us
  transfers between devices with their start and end apart: 7, of which 3 were waited for; matrix products, arithmetic and copies ran while one was open for 3% of the time, Pallas kernels for 0%

profile of v1, /device:TPU:0, one launch (start us, length us, event | category | flops | bytes accessed | tf_op | source)
XLA Modules:
  0.0 67.6 jit_solution(7568893990120973833)
XLA Ops:
  0.6 1.3 %copy.18 = f32[1,1,3,256]{3,2,1,0:T(4,128)} copy(f32[1,1,3,256]{3,1,2,0:T(1,128)} %param.17) | data formatting | bytes 6144
  2.6 10.3 %sample.1 = (bf16[8,112,128]{2,1,0:T(8,128)(2,1)}, f32[256,8]{1,0:T(8,128)}) custom-call(s32[1]{0:T(128)} %bitcast.18.count_ref, s32[8]{0:T(128)} %bitcast.29, f32[19,32,128]{2,1,0:T(8,128)} %bitcast.19, s32[256,128]{1,0:T(8,128)} %bitcast.21, s32[1,256]{1,0:T(1,128)} %bitcast.27, s32[1,256]{1,0:T(1,128)} %bitcast.28, f32[3,256]{1,0:T(4,128)} %bitcast.26), custom_call_target="tpu_custom_call" | custom-call | tf_op jit(solution)/shard_map/sample/pallas_call | solution.py:441
  12.8 7.4 %all-to-all-start = ((bf16[8,112,128]{2,1,0:T(8,128)(2,1)}), bf16[8,112,128]{2,1,0:T(8,128)(2,1)S(1)}, u32[]{:S(2)}, u32[]{:S(2)}) async-start(bf16[8,112,128]{2,1,0:T(8,128)(2,1)} %get-tuple-element.10), calls=%async_computation | async-start | bytes 458752 | tf_op jit(solution)/shard_map/all_to_all | solution.py:464
  20.3 0.0 copy-start.6
  20.3 0.8 %copy.13 = s32[1,1,256,4]{3,2,1,0:T(8,128)} copy(s32[1,1,256,4]{2,3,1,0:T(4,128)S(1)} %copy-done.5) | data formatting | bytes 8192 | tf_op args[7]
  21.1 0.0 copy-done.6
  21.1 0.8 %copy.14 = f32[1,1,256,4]{3,2,1,0:T(8,128)} copy(f32[1,1,256,4]{2,3,1,0:T(4,128)S(1)} %copy-done.6) | data formatting | bytes 8192 | tf_op args[8]
  21.9 6.8 %all-to-all-done.refs_0_ = bf16[8,112,128]{2,1,0:T(8,128)(2,1)S(1)} async-done(((bf16[8,112,128]{2,1,0:T(8,128)(2,1)}), bf16[8,112,128]{2,1,0:T(8,128)(2,1)S(1)}, u32[]{:S(2)}, u32[]{:S(2)}) %all-to-all-start) | async-done | bytes 229408 | tf_op jit(solution)/shard_map/all_to_all | solution.py:464
  28.7 0.7 %copy-done = bf16[8,112,128]{2,1,0:T(8,128)(2,1)} copy-done((bf16[8,112,128]{2,1,0:T(8,128)(2,1)}, bf16[8,112,128]{2,1,0:T(8,128)(2,1)S(1)}, u32[]{:S(2)}) %copy-start) | copy-done | bytes 229400
  29.4 3.0 %owner.1 = bf16[8,96,128]{2,1,0:T(8,128)(2,1)} custom-call(bf16[8,112,128]{2,1,0:T(8,128)(2,1)} %copy-done, s32[256,4]{1,0:T(8,128)} %bitcast.23, f32[256,4]{1,0:T(8,128)} %bitcast.24, bf16[128,128]{1,0:T(8,128)(2,1)} %refs_3_.1, bf16[128,128]{1,0:T(8,128)(2,1)} %refs_4_.1), custom_call_target="tpu_custom_call" | custom-call | tf_op jit(solution)/shard_map/owner/pallas_call | solution.py:485
  32.4 11.8 %all_to_all.10.back_ref = bf16[8,96,128]{2,1,0:T(8,128)(2,1)} all-to-all(bf16[8,96,128]{2,1,0:T(8,128)(2,1)} %owner.1), channel_id=1, replica_groups=mesh['slab'=8,'sub'=4] {'slab'}, dimensions={0} | all-to-all | bytes 393216 | tf_op jit(solution)/shard_map/all_to_all | solution.py:464
  44.2 7.5 %spread.1 = (bf16[3,256,128]{2,1,0:T(8,128)(2,1)}, f32[19,32,128]{2,1,0:T(8,128)}, f32[8,128]{1,0:T(8,128)}, f32[8,128]{1,0:T(8,128)}, bf16[5,32,128]{2,1,0:T(8,128)(2,1)}, /*index=5*/bf16[5,32,128]{2,1,0:T(8,128)(2,1)}) custom-call(bf16[8,96,128]{2,1,0:T(8,128)(2,1)} %all_to_all.10.back_ref, f32[256,8]{1,0:T(8,128)} %get-tuple-element.11.cols_ref, ...), custom_call_target="tpu_custom_call" | custom-call | tf_op jit(solution)/shard_map/spread/pallas_call | solution.py:500
  51.7 0.0 collective-permute-start
  51.7 0.7 copy-done.9
  52.4 1.1 %collective-permute-start.1 = (f32[8,128]{1,0:T(8,128)S(1)}, f32[8,128]{1,0:T(8,128)S(1)}, u32[]{:S(2)}, u32[]{:S(2)}) collective-permute-start(f32[8,128]{1,0:T(8,128)S(1)} %copy-done.9), channel_id=1, source_target_pairs={{0,3},{1,0},{2,1},{3,2},{4,7},{5,4},{6,5},{7,6},{8,11},{9,8},{10,9... | collective-permute-start | bytes 12296 | tf_op jit(solution)/shard_map/ppermute | solution.py:409
  53.5 0.2 collective-permute-start.2
  53.6 4.6 %collective-permute-start.3 = (bf16[5,32,128]{2,1,0:T(8,128)(2,1)}, bf16[5,32,128]{2,1,0:T(8,128)(2,1)S(1)}, u32[]{:S(2)}, u32[]{:S(2)}) collective-permute-start(bf16[5,32,128]{2,1,0:T(8,128)(2,1)} %get-tuple-element.16), channel_id=1, source_target_pairs={{0,28},{4,0},{8,4},{12,8},{16,12},{20,16},{24,20},{28,24},{1,29},{... | collective-permute-start | bytes 122888 | tf_op jit(solution)/shard_map/ppermute | solution.py:409
  58.2 0.0 collective-permute-done.low_ref
  58.2 0.0 collective-permute-done.1.high_ref
  58.2 0.5 copy-done.3
  58.8 0.0 collective-permute-start.5
  58.8 0.0 copy-done.4
  58.8 2.1 %collective-permute-start.4 = (f32[2,128]{1,0:T(2,128)S(1)}, f32[2,128]{1,0:T(2,128)S(1)}, u32[]{:S(2)}, u32[]{:S(2)}) collective-permute-start(f32[2,128]{1,0:T(2,128)S(1)} %pad_maximum_fusion), channel_id=1, source_target_pairs={{0,4},{4,8},{8,12},{12,16},{16,20},{20,24},{24,28},{28,0},{1,5},{5... | collective-permute-start | bytes 3080 | tf_op jit(solution)/shard_map/ppermute | solution.py:409
  60.9 0.6 pad_add_fusion.sub_ref
  61.5 0.8 %collective-permute-done.5.corner_b = f32[2,128]{1,0:T(2,128)S(1)} collective-permute-done((f32[2,128]{1,0:T(2,128)S(1)}, f32[2,128]{1,0:T(2,128)S(1)}, u32[]{:S(2)}, u32[]{:S(2)}) %collective-permute-start.5) | collective-permute-done | bytes 1056 | tf_op jit(solution)/shard_map/ppermute | solution.py:409
  62.4 2.8 %collective-permute-done.4.corner_f = f32[2,128]{1,0:T(2,128)S(1)} collective-permute-done((f32[2,128]{1,0:T(2,128)S(1)}, f32[2,128]{1,0:T(2,128)S(1)}, u32[]{:S(2)}, u32[]{:S(2)}) %collective-permute-start.4) | collective-permute-done | bytes 1056 | tf_op jit(solution)/shard_map/ppermute | solution.py:409
  65.1 0.0 collective-permute-done.2.ahead_ref
  65.1 0.0 collective-permute-done.3.behind_ref
  65.1 0.5 copy-done.8
  65.7 0.0 copy-done.1
  65.7 0.0 copy-done.2
  65.8 1.8 %stream.1 = f32[19,32,128]{2,1,0:T(8,128)} custom-call(s32[2]{0:T(128)} %pad_add_fusion.sub_ref, f32[19,32,128]{2,1,0:T(8,128)} %get-tuple-element.12.collided_ref, f32[8,128]{1,0:T(8,128)} %copy-done.3, f32[8,128]{1,0:T(8,128)} %copy-done.4, bf16[5,32,128]{2,1,0:T(8,128)(2,1)} %copy-done.1, bf16[5,32,128]{2,1,0:T(8,128)(2,1)} %copy-done.2, ...), custom_call_target="tpu_custom_call" | custom-call | tf_op jit(solution)/shard_map/stream/pallas_call | solution.py:527
  (15 shorter events, 0.0 us)
Async XLA Ops:
  12.8 7.4 %copy-start.5 = (s32[1,1,256,4]{2,3,1,0:T(4,128)S(1)}, s32[1,1,256,4]{2,3,1,0:T(4,128)}, u32[]{:S(2)}) copy-start(s32[1,1,256,4]{2,3,1,0:T(4,128)} %param.18) | copy-start | bytes 12292
  12.8 15.9 %all-to-all-start = ((bf16[8,112,128]{2,1,0:T(8,128)(2,1)}), bf16[8,112,128]{2,1,0:T(8,128)(2,1)S(1)}, u32[]{:S(2)}, u32[]{:S(2)}) async-start(bf16[8,112,128]{2,1,0:T(8,128)(2,1)} %get-tuple-element.10), calls=%async_computation | async-start | bytes 458752 | tf_op jit(solution)/shard_map/all_to_all | solution.py:464
  20.3 0.8 %copy-start.6 = (f32[1,1,256,4]{2,3,1,0:T(4,128)S(1)}, f32[1,1,256,4]{2,3,1,0:T(4,128)}, u32[]{:S(2)}) copy-start(f32[1,1,256,4]{2,3,1,0:T(4,128)} %param.19) | copy-start | bytes 12292
  28.7 0.7 %copy-start = (bf16[8,112,128]{2,1,0:T(8,128)(2,1)}, bf16[8,112,128]{2,1,0:T(8,128)(2,1)S(1)}, u32[]{:S(2)}) copy-start(bf16[8,112,128]{2,1,0:T(8,128)(2,1)S(1)} %all-to-all-done.refs_0_) | copy-start | bytes 688132
  51.7 0.7 %copy-start.9 = (f32[8,128]{1,0:T(8,128)S(1)}, f32[8,128]{1,0:T(8,128)}, u32[]{:S(2)}) copy-start(f32[8,128]{1,0:T(8,128)} %get-tuple-element.14) | copy-start | bytes 12292
  51.7 6.5 %collective-permute-start = (f32[8,128]{1,0:T(8,128)}, f32[8,128]{1,0:T(8,128)S(1)}, u32[]{:S(2)}, u32[]{:S(2)}) collective-permute-start(f32[8,128]{1,0:T(8,128)} %get-tuple-element.13), channel_id=1, source_target_pairs={{0,1},{1,2},{2,3},{3,0},{4,5},{5,6},{6,7},{7,4},{8,9},{9,10},{10,1... | collective-permute-start | bytes 12296 | tf_op jit(solution)/shard_map/ppermute | solution.py:409
  52.4 5.8 %collective-permute-start.1 = (f32[8,128]{1,0:T(8,128)S(1)}, f32[8,128]{1,0:T(8,128)S(1)}, u32[]{:S(2)}, u32[]{:S(2)}) collective-permute-start(f32[8,128]{1,0:T(8,128)S(1)} %copy-done.9), channel_id=1, source_target_pairs={{0,3},{1,0},{2,1},{3,2},{4,7},{5,4},{6,5},{7,6},{8,11},{9,8},{10,9... | collective-permute-start | bytes 12296 | tf_op jit(solution)/shard_map/ppermute | solution.py:409
  53.5 11.7 %collective-permute-start.2 = (bf16[5,32,128]{2,1,0:T(8,128)(2,1)}, bf16[5,32,128]{2,1,0:T(8,128)(2,1)S(1)}, u32[]{:S(2)}, u32[]{:S(2)}) collective-permute-start(bf16[5,32,128]{2,1,0:T(8,128)(2,1)} %get-tuple-element.15), channel_id=1, source_target_pairs={{0,4},{4,8},{8,12},{12,16},{16,20},{20,24},{24,28},{28,0},{1,5},{5... | collective-permute-start | bytes 122888 | tf_op jit(solution)/shard_map/ppermute | solution.py:409
  53.6 11.5 %collective-permute-start.3 = (bf16[5,32,128]{2,1,0:T(8,128)(2,1)}, bf16[5,32,128]{2,1,0:T(8,128)(2,1)S(1)}, u32[]{:S(2)}, u32[]{:S(2)}) collective-permute-start(bf16[5,32,128]{2,1,0:T(8,128)(2,1)} %get-tuple-element.16), channel_id=1, source_target_pairs={{0,28},{4,0},{8,4},{12,8},{16,12},{20,16},{24,20},{28,24},{1,29},{... | collective-permute-start | bytes 122888 | tf_op jit(solution)/shard_map/ppermute | solution.py:409
  58.2 0.6 copy-start.3
  58.2 0.6 copy-start.4
  58.8 3.6 %collective-permute-start.5 = (f32[2,128]{1,0:T(2,128)S(1)}, f32[2,128]{1,0:T(2,128)S(1)}, u32[]{:S(2)}, u32[]{:S(2)}) collective-permute-start(f32[2,128]{1,0:T(2,128)S(1)} %pad_maximum_fusion.1), channel_id=1, source_target_pairs={{0,28},{4,0},{8,4},{12,8},{16,12},{20,16},{24,20},{28,24},{1,29},{... | collective-permute-start | bytes 3080 | tf_op jit(solution)/shard_map/ppermute | solution.py:409
  58.8 6.3 %collective-permute-start.4 = (f32[2,128]{1,0:T(2,128)S(1)}, f32[2,128]{1,0:T(2,128)S(1)}, u32[]{:S(2)}, u32[]{:S(2)}) collective-permute-start(f32[2,128]{1,0:T(2,128)S(1)} %pad_maximum_fusion), channel_id=1, source_target_pairs={{0,4},{4,8},{8,12},{12,16},{16,20},{20,24},{24,28},{28,0},{1,5},{5... | collective-permute-start | bytes 3080 | tf_op jit(solution)/shard_map/ppermute | solution.py:409
  62.3 2.8 %copy-start.7 = (f32[2,128]{1,0:T(2,128)}, f32[2,128]{1,0:T(2,128)S(1)}, u32[]{:S(2)}) copy-start(f32[2,128]{1,0:T(2,128)S(1)} %collective-permute-done.5.corner_b) | copy-start | bytes 3076
  65.1 0.6 copy-start.8
  65.1 0.6 copy-start.1
  65.1 0.6 copy-start.2

commit v2 on v1

--- a/solution.py
+++ b/solution.py
@@ -1,4 +1,5 @@
 import functools
+import math
 
 import jax
 import jax.numpy as jnp
@@ -35,6 +36,9 @@
 backward_x = [2, 8, 10, 12, 14]
 upward_y = [3, 15, 17, 7, 10]
 downward_y = [4, 16, 18, 9, 8]
+sample_unroll = 64
+spread_unroll = 64
+kernel_memory = 16 << 20
 BF = jnp.bfloat16
 F32 = jnp.float32
 
@@ -79,6 +83,25 @@
         number = iota((16, row.shape[1]), 0, F32) + float(start)
         parts.append(jnp.where(number.astype(kind) == tall, one, zero))
     return jnp.concatenate(parts, axis=0)
+
+
+def fold_rows(blocks):
+    row = iota(blocks[0].shape, 0, jnp.int32)
+    half = 4
+    while half:
+        merged = []
+        for s in range(half):
+            a, b = blocks[s], blocks[s + half]
+            merged.append(
+                jnp.where(
+                    (row & half) == 0,
+                    a + pltpu.roll(a, 8 - half, 0),
+                    b + pltpu.roll(b, half, 0),
+                )
+            )
+        blocks = merged
+        half //= 2
+    return blocks[0]
 
 
 def sample_kernel(
@@ -112,28 +135,32 @@
     z_ref[...] = (cells % depth).astype(F32)
     y_ref[...] = (cells // depth).astype(F32)
 
-    group = 8
+    group = math.gcd(slots, sample_unroll)
 
     def sample_group(step, carry):
         base = pl.multiple_of(step * group, group)
-        z_rows = z_ref[pl.ds(base, group), :]
-        y_rows = y_ref[pl.ds(base, group), :]
-        parts = [[], [], []]
-        for first in range(0, group, 2):
-            picks = jnp.concatenate(
-                [one_hot_rows(z_rows[s : s + 1], depth) for s in (first, first + 1)], axis=1
-            )
-            picked = dot_nn(flow_pair, jnp.concatenate([picks, picks], axis=0))
-            for s in (first, first + 1):
-                off = (s - first) * width
-                mask = iota((rows, width), 0) == y_rows[s : s + 1]
-                for c in range(3):
-                    block = picked[c * rows : (c + 1) * rows, off : off + width]
-                    parts[c].append(
-                        jnp.sum(jnp.where(mask, block, 0.0), axis=0, keepdims=True)
-                    )
-        for c in range(3):
-            sampled_ref[c, pl.ds(base, group), :] = jnp.concatenate(parts[c], axis=0)
+        for eight in range(0, group, 8):
+            z_rows = z_ref[pl.ds(base + eight, 8), :]
+            y_rows = y_ref[pl.ds(base + eight, 8), :]
+            parts = [[], [], []]
+            for first in range(0, 8, 2):
+                picks = jnp.concatenate(
+                    [one_hot_rows(z_rows[s : s + 1], depth) for s in (first, first + 1)], axis=1
+                )
+                picked = dot_nn(flow_pair, jnp.concatenate([picks, picks], axis=0))
+                for s in (first, first + 1):
+                    cut = slice((s - first) * width, (s - first + 1) * width)
+                    tall = jnp.broadcast_to(y_rows[s : s + 1], (8, width))
+                    found = [jnp.zeros((8, width), F32)] * 3
+                    for start in range(0, rows, 8):
+                        mask = iota((8, width), 0) + float(start) == tall
+                        for c in range(3):
+                            at = c * rows + start
+                            found[c] = jnp.where(mask, picked[at : at + 8, cut], found[c])
+                    for c in range(3):
+                        parts[c].append(found[c])
+            for c in range(3):
+                sampled_ref[c, pl.ds(base + eight, 8), :] = fold_rows(parts[c])
         return carry
 
     lax.fori_loop(0, slots // group, sample_group, 0)
@@ -159,7 +186,7 @@
     send_row = jnp.where(alive, owner_f * float(capacity) + position, -1.0)
 
     count = jnp.where(alive, marker_count_ref[...], 0).astype(F32)
-    velocity = velocity_ref[...]
+    velocity = jnp.concatenate([velocity_ref[c] for c in range(3)], axis=0)
     stack = jnp.concatenate(
         [velocity, count, send_row, jnp.zeros((3, slots), F32)], axis=0
     )
@@ -195,7 +222,7 @@
     if packed:
         got_ref, list_ref, gap_ref, self_ref, pair_ref, out_ref = refs
         width = got_ref.shape[2]
-        slots = list_ref.shape[0]
+        slots = list_ref.shape[1]
         capacity = slots // slab_count
         got = jnp.concatenate(
             [
@@ -221,7 +248,7 @@
     else:
         got_ref, spot_ref, list_ref, gap_ref, self_ref, pair_ref, out_ref = refs
         width = got_ref.shape[2]
-        slots = list_ref.shape[0]
+        slots = list_ref.shape[1]
         got = jnp.concatenate([got_ref[c] for c in range(3)], axis=1)
         spots = jnp.broadcast_to(spot_ref[...].astype(F32), (8, slots)) - 1.0
 
@@ -229,11 +256,15 @@
     spot_col = jnp.transpose(spots)[:, :1]
     land = jnp.where(iota((slots, slots), 0) == spot_row, 1.0, 0.0).astype(BF)
     reply = jnp.where(iota((slots, slots), 1) == spot_col, 1.0, 0.0).astype(BF)
-    partner = list_ref[...].astype(F32)
-    inverse = 1.0 / gap_ref[...]
+    pairs = list_ref.shape[0]
+    filler = jnp.zeros((-2 * pairs % 8, slots), F32)
+    turned = jnp.transpose(
+        jnp.concatenate([list_ref[...].astype(F32), 1.0 / gap_ref[...], filler][: 2 + (2 * pairs % 8 > 0)], axis=0)
+    )
+    partner, inverse = turned[:, :pairs], turned[:, pairs : 2 * pairs]
     column = iota((slots, slots), 1)
     weight = jnp.zeros((slots, slots), F32)
-    for k in range(list_ref.shape[1]):
+    for k in range(pairs):
         weight = weight + jnp.where(column == partner[:, k : k + 1], inverse[:, k : k + 1], 0.0)
     high = weight.astype(BF)
     low = (weight - high.astype(F32)).astype(BF)
@@ -300,7 +331,7 @@
     z_ref[...] = (cells % depth).astype(F32)
     y_ref[...] = (cells // depth).astype(F32)
 
-    group = 16
+    group = math.gcd(slots, spread_unroll)
 
     def spread_group(step, total):
         base = pl.multiple_of(step * group, group)
@@ -355,24 +386,24 @@
             ahead_ref[forward_x.index(number)] = value.astype(BF)
         if number in backward_x:
             behind_ref[backward_x.index(number)] = value.astype(BF)
-        if number in upward_y:
+        if number in upward_y[:3]:
             at = upward_y.index(number)
             up_ref[at : at + 1, :] = value[rows - 1 :]
-        if number in downward_y:
+        if number in downward_y[:3]:
             at = downward_y.index(number)
             down_ref[at : at + 1, :] = value[:1]
-    up_ref[5:, :] = jnp.zeros((3, depth), F32)
-    down_ref[5:, :] = jnp.zeros((3, depth), F32)
+    up_ref[3:, :] = jnp.zeros((5, depth), F32)
+    down_ref[3:, :] = jnp.zeros((5, depth), F32)
 
 
 def stream_kernel(
-    sub_ref, collided_ref, low_ref, high_ref, ahead_ref, behind_ref, corner_f, corner_b, read_ref
+    sub_total, collided_ref, low_ref, high_ref, ahead_ref, behind_ref, read_ref
 ):
     rows, depth = collided_ref.shape[1:]
     row = iota((rows, depth), 0, jnp.int32)
-    at_low, at_high = sub_ref[0] == 0, sub_ref[0] == sub_ref[1] - 1
-    low_wall = jnp.where(at_low, 1, 0)
-    high_wall = jnp.where(at_high, 1, 0)
+    place = lax.axis_index("sub")
+    low_wall = jnp.where(place == 0, 1, 0)
+    high_wall = jnp.where(place == sub_total - 1, 1, 0)
     for number in range(19):
         step_x, step_y, step_z = lattice_dirs[number]
         if step_x == 1:
@@ -384,12 +415,8 @@
         if step_y != 0:
             rolled = pltpu.roll(moved, 1 if step_y == 1 else rows - 1, 0)
             edge_row = 0 if step_y == 1 else rows - 1
-            if step_x == 0:
-                at = (upward_y if step_y == 1 else downward_y).index(number)
-                edge = (low_ref if step_y == 1 else high_ref)[at : at + 1, :]
-            else:
-                at = 0 if step_y == 1 else 1
-                edge = (corner_f if step_x == 1 else corner_b)[at : at + 1, :]
+            at = (upward_y if step_y == 1 else downward_y).index(number)
+            edge = (low_ref if step_y == 1 else high_ref)[at : at + 1, :]
             moved = jnp.where(row == edge_row, edge, rolled)
         if step_z != 0:
             moved = pltpu.roll(moved, 1 if step_z == 1 else depth - 1, 1)
@@ -432,6 +459,7 @@
     pops = populations.reshape(19, rows, depth)
     cells = marker_cell.reshape(slots, width)
     shape = jax.ShapeDtypeStruct
+    limits = pltpu.CompilerParams(vmem_limit_bytes=kernel_memory)
 
     if packed:
         sample_out = [shape((slab_count, 3 * capacity + 16, width), BF)]
@@ -448,6 +476,7 @@
             pltpu.VMEM((slots, width), F32),
             pltpu.VMEM((3, slots, width), F32),
         ],
+        compiler_params=limits,
         name="sample",
     )(
         particle_count.reshape(1),
@@ -456,7 +485,7 @@
         cells,
         marker_count.reshape(1, slots),
         particle_id.reshape(1, slots),
-        particle_velocity.reshape(3, slots),
+        particle_velocity.reshape(3, 1, slots),
     )
     cols = results[-1]
 
@@ -487,11 +516,12 @@
         out_shape=reply_shape,
         in_specs=[whole()] * (len(arrived) + 4),
         out_specs=whole(),
+        compiler_params=limits,
         name="owner",
     )(
         *arrived,
-        pair_list.reshape(slots, -1),
-        pair_gap.reshape(slots, -1),
+        jnp.transpose(pair_list.reshape(slots, -1)),
+        jnp.transpose(pair_gap.reshape(slots, -1)),
         self_coupling,
         pair_coupling,
     )
@@ -514,23 +544,24 @@
             pltpu.VMEM((slots, width), F32),
             pltpu.VMEM((3, slots, width), F32),
         ],
+        compiler_params=limits,
         name="spread",
     )(back, cols, cells, pops)
 
-    low = ring(up, "sub", 1)
-    high = ring(down, "sub", -1)
     ahead = ring(ahead, "slab", 1)
     behind = ring(behind, "slab", -1)
-    corner_f = ring(jnp.concatenate([low[3:4], high[3:4]]), "slab", 1)
-    corner_b = ring(jnp.concatenate([low[4:5], high[4:5]]), "slab", -1)
-    place = jnp.stack([lax.axis_index("sub"), jnp.int32(lax.axis_size("sub"))]).astype(jnp.int32)
+    rise = [ahead[forward_x.index(7), rows - 1 :], behind[backward_x.index(10), rows - 1 :]]
+    sink = [ahead[forward_x.index(9), :1], behind[backward_x.index(8), :1]]
+    low = ring(jnp.concatenate([up[:3]] + [row.astype(F32) for row in rise]), "sub", 1)
+    high = ring(jnp.concatenate([down[:3]] + [row.astype(F32) for row in sink]), "sub", -1)
     read = pl.pallas_call(
-        stream_kernel,
+        functools.partial(stream_kernel, lax.axis_size("sub")),
         out_shape=shape((19, rows, depth), F32),
-        in_specs=[whole(pltpu.SMEM)] + [whole()] * 7,
+        in_specs=[whole()] * 5,
         out_specs=whole(),
+        compiler_params=limits,
         name="stream",
-    )(place, collided, low, high, ahead, behind, corner_f, corner_b)
+    )(collided, low, high, ahead, behind)
     marker_force = jnp.transpose(marker_force, (1, 0, 2))[None, None]
     return (read.reshape(19, 1, rows, depth), marker_force)
 

time: 68.1 us -> 52.9 us (0.78)
  the two profiles are of different devices: /device:TPU:0 before, /device:TPU:1 now
where the time goes in v2:
time: 52.9 us; the launch traced here: 52.5 us
  blocking collectives  24.4 us (46%)
  Pallas kernels  10.7 us (20%)
  starting transfers between devices  8.97 us (17%)
  waiting for transfers between devices  4.4 us (8%)
  local copies, waits for them, and re-layouts  2.6 us (5%)
  between operations  1.44 us (3%)
    all_to_all x2, blocking collectives, exchange(): lax.all_to_all(value, 'slab', split_axis=0, concat_axis=0, tiled=True)  24.4 us
    ppermute x4, starting transfers between devices, ring(): lax.ppermute(value, axis, [(i, (i + steps) % count) for i in range(count)])  8.97 us
    pallas_call x1, Pallas kernels, per_device(): pl.pallas_call(functools.partial(sample_kernel, slab_count, packed), out_...  4.8 us
    ppermute x4, waiting for transfers between devices, ring(): lax.ppermute(value, axis, [(i, (i + steps) % count) for i in range(count)])  4.4 us
    pallas_call x1, Pallas kernels, per_device(): pl.pallas_call(functools.partial(spread_kernel, slab_count, packed), out_...  3.83 us
    unnamed x24, local copies, waits for them, and re-layouts  2.59 us
    pallas_call x1, Pallas kernels, per_device(): pl.pallas_call(functools.partial(owner_kernel, slab_count, packed), out_s...  1.26 us
  transfers between devices with their start and end apart: 4, of which 3 were waited for; matrix products, arithmetic and copies ran while one was open for 0% of the time, Pallas kernels for 0%

profile of v2, /device:TPU:1, one launch (start us, length us, event | category | flops | bytes accessed | tf_op | source)
XLA Modules:
  0.0 52.5 jit_solution(9975913511413852461)
XLA Ops:
  1.3 0.0 copy-start.8
  1.3 0.0 copy-start.10
  1.3 0.0 copy-start.9
  1.3 0.0 copy-start.11
  1.3 0.6 %copy-done.8 = f32[1,1,3,256]{3,1,2,0:T(1,128)S(1)} copy-done((f32[1,1,3,256]{3,1,2,0:T(1,128)S(1)}, f32[1,1,3,256]{3,1,2,0:T(1,128)}, u32[]{:S(2)}) %copy-start.8) | copy-done | bytes 3096
  2.0 0.0 copy-done.10
  2.0 0.0 copy-done.9
  2.0 0.0 copy-done.11
  2.0 1.0 %copy-done = f32[19,1,32,128]{3,2,1,0:T(8,128)S(1)} copy-done((f32[19,1,32,128]{3,2,1,0:T(8,128)S(1)}, f32[19,1,32,128]{3,2,1,0:T(8,128)}, u32[]{:S(2)}) %copy-start) | copy-done | bytes 311320
  3.0 0.9 %copy-done.2 = s32[1,1,256,128]{3,2,1,0:T(8,128)S(1)} copy-done((s32[1,1,256,128]{3,2,1,0:T(8,128)S(1)}, s32[1,1,256,128]{3,2,1,0:T(8,128)}, u32[]{:S(2)}) %copy-start.2) | copy-done | bytes 131096
  3.9 4.8 %sample.1 = (bf16[8,112,128]{2,1,0:T(8,128)(2,1)S(1)}, f32[256,8]{1,0:T(8,128)S(1)}) custom-call(s32[1]{0:T(128)} %bitcast.39.count_ref, s32[8]{0:T(128)S(1)} %bitcast.49, f32[19,32,128]{2,1,0:T(8,128)S(1)} %bitcast.40, s32[256,128]{1,0:T(8,128)S(1)} %bitcast.42, s32[1,256]{1,0:T(1,128)S(1)} %bitcast.47, s32[1,256]{1,0:T(1,128)S(1)} %bitcast.48, ...), custom_call_target="tpu_custom_call" | custom-call | tf_op jit(solution)/shard_map/sample/pallas_call | solution.py:469
  8.7 0.0 copy-start.4
  8.7 0.0 copy-start.5
  8.7 0.0 copy-start.6
  8.7 0.0 copy-start.7
  8.7 13.3 %all_to_all.10.refs_0_ = bf16[8,112,128]{2,1,0:T(8,128)(2,1)S(1)} all-to-all(bf16[8,112,128]{2,1,0:T(8,128)(2,1)S(1)} %get-tuple-element.10), channel_id=1, replica_groups=mesh['slab'=8,'sub'=4] {'slab'}, dimensions={0} | all-to-all | bytes 458752 | tf_op jit(solution)/shard_map/all_to_all | solution.py:493
  22.0 0.0 copy-done.4
  22.0 0.0 copy-done.7
  22.0 0.0 copy-start.3
  22.0 1.3 %owner.1 = bf16[8,96,128]{2,1,0:T(8,128)(2,1)S(1)} custom-call(bf16[8,112,128]{2,1,0:T(8,128)(2,1)S(1)} %all_to_all.10.refs_0_, s32[4,256]{1,0:T(4,128)S(1)} %bitcast.44, f32[4,256]{1,0:T(4,128)S(1)} %bitcast.45, bf16[128,128]{1,0:T(8,128)(2,1)S(1)} %copy-done.4, bf16[128,128]{1,0:T(8,128)(2,1)S(1)} %copy-done.5), custom_call_target="tpu_custom_call" | custom-call | tf_op jit(solution)/shard_map/owner/pallas_call | solution.py:514
  23.3 0.0 copy-start.1
  23.3 11.1 %all_to_all.11.back_ref = bf16[8,96,128]{2,1,0:T(8,128)(2,1)S(1)} all-to-all(bf16[8,96,128]{2,1,0:T(8,128)(2,1)S(1)} %owner.1), channel_id=1, replica_groups=mesh['slab'=8,'sub'=4] {'slab'}, dimensions={0} | all-to-all | bytes 393216 | tf_op jit(solution)/shard_map/all_to_all | solution.py:493
  34.4 3.8 %spread.1 = (bf16[3,256,128]{2,1,0:T(8,128)(2,1)}, f32[19,32,128]{2,1,0:T(8,128)S(1)}, f32[8,128]{1,0:T(8,128)S(1)}, f32[8,128]{1,0:T(8,128)S(1)}, bf16[5,32,128...) custom-call(bf16[8,96,128]{2,1,0:T(8,128)(2,1)S(1)} %all_to_all.11.back_ref, ...), custom_call_target="tpu_custom_call" | custom-call | tf_op jit(solution)/shard_map/spread/pallas_call | solution.py:530
  38.2 0.1 collective-permute-start
  38.3 4.1 %collective-permute-start.1 = (bf16[5,32,128]{2,1,0:T(8,128)(2,1)S(1)}, bf16[5,32,128]{2,1,0:T(8,128)(2,1)S(1)}, u32[]{:S(2)}, u32[]{:S(2)}) collective-permute-start(bf16[5,32,128]{2,1,0:T(8,128)(2,1)S(1)} %get-tuple-element.15), channel_id=1, source_target_pairs={{0,28},{4,0},{8,4},{12,8},{16,12},{20,16},{24,20},{28,24},{1,29},{... | collective-permute-start | bytes 122888 | tf_op jit(solution)/shard_map/ppermute | solution.py:436
  42.5 1.4 %collective-permute-done.ahead_ref = bf16[5,32,128]{2,1,0:T(8,128)(2,1)S(1)} collective-permute-done((bf16[5,32,128]{2,1,0:T(8,128)(2,1)S(1)}, bf16[5,32,128]{2,1,0:T(8,128)(2,1)S(1)}, u32[]{:S(2)}, u32[]{:S(2)}) %collective-permute-start) | collective-permute-done | bytes 40992 | tf_op jit(solution)/shard_map/ppermute | solution.py:436
  43.8 0.0 collective-permute-done.1.behind_ref
  43.9 4.7 %collective-permute-start.2 = (f32[5,128]{1,0:T(8,128)S(1)}, f32[5,128]{1,0:T(8,128)S(1)}, u32[]{:S(2)}, u32[]{:S(2)}) collective-permute-start(f32[5,128]{1,0:T(8,128)S(1)} %pad_maximum_fusion), channel_id=1, source_target_pairs={{0,1},{1,2},{2,3},{3,0},{4,5},{5,6},{6,7},{7,4},{8,9},{9,10},{10,1... | collective-permute-start | bytes 7688 | tf_op jit(solution)/shard_map/ppermute | solution.py:436
  48.6 0.1 collective-permute-start.3
  48.7 0.7 %collective-permute-done.2.low_ref = f32[5,128]{1,0:T(8,128)S(1)} collective-permute-done((f32[5,128]{1,0:T(8,128)S(1)}, f32[5,128]{1,0:T(8,128)S(1)}, u32[]{:S(2)}, u32[]{:S(2)}) %collective-permute-start.2) | collective-permute-done | bytes 2592 | tf_op jit(solution)/shard_map/ppermute | solution.py:436
  49.4 2.3 %collective-permute-done.3.high_ref = f32[5,128]{1,0:T(8,128)S(1)} collective-permute-done((f32[5,128]{1,0:T(8,128)S(1)}, f32[5,128]{1,0:T(8,128)S(1)}, u32[]{:S(2)}, u32[]{:S(2)}) %collective-permute-start.3) | collective-permute-done | bytes 2592 | tf_op jit(solution)/shard_map/ppermute | solution.py:436
  51.7 0.8 %stream.1 = f32[19,32,128]{2,1,0:T(8,128)} custom-call(f32[19,32,128]{2,1,0:T(8,128)S(1)} %get-tuple-element.12.collided_ref, f32[5,128]{1,0:T(8,128)S(1)} %collective-permute-done.2.low_ref, f32[5,128]{1,0:T(8,128)S(1)} %collective-permute-done.3.high_ref, bf16[5,32,128]{2,1,0:T(8,128)(2,1)S(1)} %collective-permute-done.ahead_ref, ...), custom_call_target="tpu_custom_call" | custom-call | tf_op jit(solution)/shard_map/stream/pallas_call | solution.py:557
  (12 shorter events, 0.0 us)
Async XLA Ops:
  1.3 0.7 %copy-start.8 = (f32[1,1,3,256]{3,1,2,0:T(1,128)S(1)}, f32[1,1,3,256]{3,1,2,0:T(1,128)}, u32[]{:S(2)}) copy-start(f32[1,1,3,256]{3,1,2,0:T(1,128)} %param.17) | copy-start | bytes 9220
  1.3 0.7 %copy-start.10 = (s32[1,1,256]{2,1,0:T(1,128)S(1)}, s32[1,1,256]{2,1,0:T(1,128)}, u32[]{:S(2)}) copy-start(s32[1,1,256]{2,1,0:T(1,128)} %param.15) | copy-start | bytes 3076
  1.3 0.7 %copy-start.9 = (s32[1,1,256]{2,1,0:T(1,128)S(1)}, s32[1,1,256]{2,1,0:T(1,128)}, u32[]{:S(2)}) copy-start(s32[1,1,256]{2,1,0:T(1,128)} %param.13) | copy-start | bytes 3076
  1.3 0.7 %copy-start.11 = (s32[1,8]{1,0:T(1,128)S(1)}, s32[1,8]{1,0:T(1,128)}, u32[]{:S(2)}) copy-start(s32[1,8]{1,0:T(1,128)} %param.16) | copy-start | bytes 100
  2.0 1.0 %copy-start = (f32[19,1,32,128]{3,2,1,0:T(8,128)S(1)}, f32[19,1,32,128]{3,2,1,0:T(8,128)}, u32[]{:S(2)}) copy-start(f32[19,1,32,128]{3,2,1,0:T(8,128)} %param.11) | copy-start | bytes 933892
  3.0 0.9 %copy-start.2 = (s32[1,1,256,128]{3,2,1,0:T(8,128)S(1)}, s32[1,1,256,128]{3,2,1,0:T(8,128)}, u32[]{:S(2)}) copy-start(s32[1,1,256,128]{3,2,1,0:T(8,128)} %param.12) | copy-start | bytes 393220
  8.7 13.3 %copy-start.4 = (bf16[128,128]{1,0:T(8,128)(2,1)S(1)}, bf16[128,128]{1,0:T(8,128)(2,1)}, u32[]{:S(2)}) copy-start(bf16[128,128]{1,0:T(8,128)(2,1)} %refs_3_.1) | copy-start | bytes 98308
  8.7 13.3 %copy-start.5 = (bf16[128,128]{1,0:T(8,128)(2,1)S(1)}, bf16[128,128]{1,0:T(8,128)(2,1)}, u32[]{:S(2)}) copy-start(bf16[128,128]{1,0:T(8,128)(2,1)} %refs_4_.1) | copy-start | bytes 98308
  8.7 13.3 %copy-start.6 = (s32[1,1,256,4]{2,3,1,0:T(4,128)S(1)}, s32[1,1,256,4]{2,3,1,0:T(4,128)}, u32[]{:S(2)}) copy-start(s32[1,1,256,4]{2,3,1,0:T(4,128)} %param.18) | copy-start | bytes 12292
  8.7 13.3 %copy-start.7 = (f32[1,1,256,4]{2,3,1,0:T(4,128)S(1)}, f32[1,1,256,4]{2,3,1,0:T(4,128)}, u32[]{:S(2)}) copy-start(f32[1,1,256,4]{2,3,1,0:T(4,128)} %param.19) | copy-start | bytes 12292
  22.0 12.4 %copy-start.3 = (s32[1,1,256,128]{3,2,1,0:T(8,128)S(1)}, s32[1,1,256,128]{3,2,1,0:T(8,128)}, u32[]{:S(2)}) copy-start(s32[1,1,256,128]{3,2,1,0:T(8,128)} %param.12) | copy-start | bytes 393220
  23.3 11.1 %copy-start.1 = (f32[19,1,32,128]{3,2,1,0:T(8,128)S(1)}, f32[19,1,32,128]{3,2,1,0:T(8,128)}, u32[]{:S(2)}) copy-start(f32[19,1,32,128]{3,2,1,0:T(8,128)} %param.11) | copy-start | bytes 933892
  38.2 5.6 %collective-permute-start = (bf16[5,32,128]{2,1,0:T(8,128)(2,1)S(1)}, bf16[5,32,128]{2,1,0:T(8,128)(2,1)S(1)}, u32[]{:S(2)}, u32[]{:S(2)}) collective-permute-start(bf16[5,32,128]{2,1,0:T(8,128)(2,1)S(1)} %get-tuple-element.14), channel_id=1, source_target_pairs={{0,4},{4,8},{8,12},{12,16},{16,20},{20,24},{24,28},{28,0},{1,5},{5... | collective-permute-start | bytes 122888 | tf_op jit(solution)/shard_map/ppermute | solution.py:436
  38.3 5.5 %collective-permute-start.1 = (bf16[5,32,128]{2,1,0:T(8,128)(2,1)S(1)}, bf16[5,32,128]{2,1,0:T(8,128)(2,1)S(1)}, u32[]{:S(2)}, u32[]{:S(2)}) collective-permute-start(bf16[5,32,128]{2,1,0:T(8,128)(2,1)S(1)} %get-tuple-element.15), channel_id=1, source_target_pairs={{0,28},{4,0},{8,4},{12,8},{16,12},{20,16},{24,20},{28,24},{1,29},{... | collective-permute-start | bytes 122888 | tf_op jit(solution)/shard_map/ppermute | solution.py:436
  43.9 5.5 %collective-permute-start.2 = (f32[5,128]{1,0:T(8,128)S(1)}, f32[5,128]{1,0:T(8,128)S(1)}, u32[]{:S(2)}, u32[]{:S(2)}) collective-permute-start(f32[5,128]{1,0:T(8,128)S(1)} %pad_maximum_fusion), channel_id=1, source_target_pairs={{0,1},{1,2},{2,3},{3,0},{4,5},{5,6},{6,7},{7,4},{8,9},{9,10},{10,1... | collective-permute-start | bytes 7688 | tf_op jit(solution)/shard_map/ppermute | solution.py:436
  48.6 3.1 %collective-permute-start.3 = (f32[5,128]{1,0:T(8,128)S(1)}, f32[5,128]{1,0:T(8,128)S(1)}, u32[]{:S(2)}, u32[]{:S(2)}) collective-permute-start(f32[5,128]{1,0:T(8,128)S(1)} %pad_maximum_fusion.1), channel_id=1, source_target_pairs={{0,3},{1,0},{2,1},{3,2},{4,7},{5,4},{6,5},{7,6},{8,11},{9,8},{10,9... | collective-permute-start | bytes 7688 | tf_op jit(solution)/shard_map/ppermute | solution.py:436

commit v3 on v2

--- a/solution.py
+++ b/solution.py
@@ -36,8 +36,8 @@
 backward_x = [2, 8, 10, 12, 14]
 upward_y = [3, 15, 17, 7, 10]
 downward_y = [4, 16, 18, 9, 8]
-sample_unroll = 64
-spread_unroll = 64
+sample_unroll = 256
+spread_unroll = 256
 kernel_memory = 16 << 20
 BF = jnp.bfloat16
 F32 = jnp.float32
@@ -107,23 +107,56 @@
 def sample_kernel(
     slab_count,
     packed,
-    count_ref,
-    table_ref,
-    pops_ref,
-    cell_ref,
-    marker_count_ref,
-    id_ref,
-    velocity_ref,
-    slip_ref,
-    *rest,
+    *refs,
 ):
-    if packed:
-        cols_ref, z_ref, y_ref, sampled_ref = rest
-    else:
-        spot_ref, cols_ref, z_ref, y_ref, sampled_ref = rest
+    sources, refs = refs[:7], refs[7:]
+    slip_ref, refs = refs[0], refs[1:]
+    if not packed:
+        spot_ref, refs = refs[0], refs[1:]
+    cols_ref, refs = refs[0], refs[1:]
+    targets, (z_ref, y_ref, sampled_ref, sems) = refs[:7], refs[7:]
+    copies = [
+        pltpu.make_async_copy(source, target, sems.at[number])
+        for number, (source, target) in enumerate(zip(sources, targets))
+    ]
+    for copy in copies:
+        copy.start()
+    count_ref, table_ref, marker_count_ref, id_ref, velocity_ref, pops_ref, cell_ref = targets
     slots, width = cell_ref.shape
     rows, depth = pops_ref.shape[1:]
     capacity = slots // slab_count
+    for copy in copies[:5]:
+        copy.wait()
+
+    lane = iota((1, slots), 1, jnp.int32)
+    alive = lane < count_ref[0]
+    identity = id_ref[...]
+    block = identity // slots
+    spot = (identity % slots).astype(F32)
+
+    def look_up(b, owner):
+        return jnp.where(block == b, table_ref[b], owner)
+
+    owner = lax.fori_loop(0, slab_count, look_up, jnp.zeros((1, slots), jnp.int32))
+    owner = jnp.where(alive, owner, -1)
+    owner_f = owner.astype(F32)
+    chosen = jnp.where(iota((slab_count, slots), 0) == owner_f, 1.0, 0.0)
+    before = jnp.where(
+        iota((slots, slots), 0) < iota((slots, slots), 1), 1.0, 0.0
+    ).astype(BF)
+    earlier = dot_nn(chosen.astype(BF), before)
+    position = jnp.sum(chosen * earlier, axis=0, keepdims=True)
+    send_row = jnp.where(alive, owner_f * float(capacity) + position, -1.0)
+
+    count = jnp.where(alive, marker_count_ref[...], 0).astype(F32)
+    velocity = jnp.concatenate([velocity_ref[c] for c in range(3)], axis=0)
+    stack = jnp.concatenate(
+        [velocity, count, send_row, jnp.zeros((3, slots), F32)], axis=0
+    )
+    cols = jnp.transpose(stack)
+    cols_ref[...] = cols
+    for copy in copies[5:]:
+        copy.wait()
 
     density, moment = moments_of([pops_ref[number] for number in range(19)])
     flow = jnp.concatenate([part / density for part in moment], axis=0)
@@ -165,33 +198,6 @@
 
     lax.fori_loop(0, slots // group, sample_group, 0)
 
-    lane = iota((1, slots), 1, jnp.int32)
-    alive = lane < count_ref[0]
-    identity = id_ref[...]
-    block = identity // slots
-    spot = (identity % slots).astype(F32)
-
-    def look_up(b, owner):
-        return jnp.where(block == b, table_ref[b], owner)
-
-    owner = lax.fori_loop(0, slab_count, look_up, jnp.zeros((1, slots), jnp.int32))
-    owner = jnp.where(alive, owner, -1)
-    owner_f = owner.astype(F32)
-    chosen = jnp.where(iota((slab_count, slots), 0) == owner_f, 1.0, 0.0)
-    before = jnp.where(
-        iota((slots, slots), 0) < iota((slots, slots), 1), 1.0, 0.0
-    ).astype(BF)
-    earlier = dot_nn(chosen.astype(BF), before)
-    position = jnp.sum(chosen * earlier, axis=0, keepdims=True)
-    send_row = jnp.where(alive, owner_f * float(capacity) + position, -1.0)
-
-    count = jnp.where(alive, marker_count_ref[...], 0).astype(F32)
-    velocity = jnp.concatenate([velocity_ref[c] for c in range(3)], axis=0)
-    stack = jnp.concatenate(
-        [velocity, count, send_row, jnp.zeros((3, slots), F32)], axis=0
-    )
-    cols = jnp.transpose(stack)
-    cols_ref[...] = cols
     live = iota((slots, width), 1) < cols[:, 3:4]
     slips = []
     for c in range(3):
@@ -299,8 +305,8 @@
     collided_ref,
     up_ref,
     down_ref,
-    ahead_ref,
-    behind_ref,
+    first_ref,
+    second_ref,
     z_ref,
     y_ref,
     force_ref,
@@ -362,6 +368,8 @@
     speed_sq = velocity[0] * velocity[0] + velocity[1] * velocity[1] + velocity[2] * velocity[2]
     work_rate = velocity[0] * force[0] + velocity[1] * force[1] + velocity[2] * force[2]
     base_term = 1.0 - 1.5 * speed_sq
+    even = (lax.axis_index("slab") & 1) == 0
+    sent = {}
     for number in range(19):
         step = lattice_dirs[number]
         along, push = None, None
@@ -382,41 +390,50 @@
             )
         value = pops[number] - relax_rate * (pops[number] - equilibrium) + source
         collided_ref[number] = value
-        if number in forward_x:
-            ahead_ref[forward_x.index(number)] = value.astype(BF)
-        if number in backward_x:
-            behind_ref[backward_x.index(number)] = value.astype(BF)
+        if step[0] != 0:
+            sent.setdefault((forward_x if step[0] == 1 else backward_x).index(number), {})[
+                step[0]
+            ] = value
         if number in upward_y[:3]:
             at = upward_y.index(number)
             up_ref[at : at + 1, :] = value[rows - 1 :]
         if number in downward_y[:3]:
             at = downward_y.index(number)
             down_ref[at : at + 1, :] = value[:1]
+    for at, pair in sent.items():
+        first_ref[at] = jnp.where(even, pair[1], pair[-1]).astype(BF)
+        second_ref[at] = jnp.where(even, pair[-1], pair[1]).astype(BF)
     up_ref[3:, :] = jnp.zeros((5, depth), F32)
     down_ref[3:, :] = jnp.zeros((5, depth), F32)
 
 
 def stream_kernel(
-    sub_total, collided_ref, low_ref, high_ref, ahead_ref, behind_ref, read_ref
+    sub_total, collided_ref, one_ref, two_ref, first_ref, second_ref, read_ref
 ):
     rows, depth = collided_ref.shape[1:]
     row = iota((rows, depth), 0, jnp.int32)
     place = lax.axis_index("sub")
+    slab_even = (lax.axis_index("slab") & 1) == 0
+    sub_even = (place & 1) == 0
+    low = jnp.where(sub_even, two_ref[...], one_ref[...])
+    high = jnp.where(sub_even, one_ref[...], two_ref[...])
     low_wall = jnp.where(place == 0, 1, 0)
     high_wall = jnp.where(place == sub_total - 1, 1, 0)
     for number in range(19):
         step_x, step_y, step_z = lattice_dirs[number]
         if step_x == 1:
-            moved = ahead_ref[forward_x.index(number)].astype(F32)
+            at = forward_x.index(number)
+            moved = jnp.where(slab_even, second_ref[at].astype(F32), first_ref[at].astype(F32))
         elif step_x == -1:
-            moved = behind_ref[backward_x.index(number)].astype(F32)
+            at = backward_x.index(number)
+            moved = jnp.where(slab_even, first_ref[at].astype(F32), second_ref[at].astype(F32))
         else:
             moved = collided_ref[number]
         if step_y != 0:
             rolled = pltpu.roll(moved, 1 if step_y == 1 else rows - 1, 0)
             edge_row = 0 if step_y == 1 else rows - 1
             at = (upward_y if step_y == 1 else downward_y).index(number)
-            edge = (low_ref if step_y == 1 else high_ref)[at : at + 1, :]
+            edge = (low if step_y == 1 else high)[at : at + 1]
             moved = jnp.where(row == edge_row, edge, rolled)
         if step_z != 0:
             moved = pltpu.roll(moved, 1 if step_z == 1 else depth - 1, 1)
@@ -431,9 +448,10 @@
     return pl.BlockSpec(memory_space=memory)
 
 
-def ring(value, axis, steps):
+def swap(value, axis, odd):
     count = lax.axis_size(axis)
-    return lax.ppermute(value, axis, [(i, (i + steps) % count) for i in range(count)])
+    pairs = [(i, (i + 1 if i % 2 == odd else i - 1) % count) for i in range(count)]
+    return lax.ppermute(value, axis, pairs)
 
 
 def per_device(
@@ -453,6 +471,7 @@
     slots, width = marker_cell.shape[2:]
     planes, rows, depth = populations.shape[1:]
     assert planes == 1 and slots <= 256 and slots % slab_count == 0
+    assert slab_count % 2 == 0 and lax.axis_size("sub") % 2 == 0
     capacity = slots // slab_count
     assert capacity <= width
     packed = capacity % 16 == 0 and width % capacity == 0
@@ -469,23 +488,36 @@
     results = pl.pallas_call(
         functools.partial(sample_kernel, slab_count, packed),
         out_shape=sample_out,
-        in_specs=[whole(pltpu.SMEM)] * 2 + [whole()] * 5,
+        in_specs=[whole(pltpu.HBM)] * 7,
         out_specs=[whole()] * len(sample_out),
         scratch_shapes=[
+            pltpu.SMEM((1,), jnp.int32),
+            pltpu.SMEM((slab_count,), jnp.int32),
+            pltpu.VMEM((1, slots), jnp.int32),
+            pltpu.VMEM((1, slots), jnp.int32),
+            pltpu.VMEM((3, 1, slots), F32),
+            pltpu.VMEM((19, rows, depth), F32),
+            pltpu.VMEM((slots, width), jnp.int32),
             pltpu.VMEM((slots, width), F32),
             pltpu.VMEM((slots, width), F32),
             pltpu.VMEM((3, slots, width), F32),
+            pltpu.SemaphoreType.DMA((7,)),
         ],
         compiler_params=limits,
         name="sample",
     )(
         particle_count.reshape(1),
-        owner_table.reshape(slab_count),
-        pops,
-        cells,
-        marker_count.reshape(1, slots),
-        particle_id.reshape(1, slots),
-        particle_velocity.reshape(3, 1, slots),
+        *[
+            pltpu.with_memory_space_constraint(value, pltpu.HBM)
+            for value in (
+                owner_table.reshape(slab_count),
+                marker_count.reshape(1, slots),
+                particle_id.reshape(1, slots),
+                particle_velocity.reshape(3, 1, slots),
+                pops,
+                cells,
+            )
+        ],
     )
     cols = results[-1]
 
@@ -527,7 +559,7 @@
     )
     back = exchange(reply) if packed else by_component(exchange(by_owner(reply)))
 
-    marker_force, collided, up, down, ahead, behind = pl.pallas_call(
+    marker_force, collided, up, down, first, second = pl.pallas_call(
         functools.partial(spread_kernel, slab_count, packed),
         out_shape=[
             shape((3, slots, width), BF),
@@ -548,12 +580,20 @@
         name="spread",
     )(back, cols, cells, pops)
 
-    ahead = ring(ahead, "slab", 1)
-    behind = ring(behind, "slab", -1)
-    rise = [ahead[forward_x.index(7), rows - 1 :], behind[backward_x.index(10), rows - 1 :]]
-    sink = [ahead[forward_x.index(9), :1], behind[backward_x.index(8), :1]]
-    low = ring(jnp.concatenate([up[:3]] + [row.astype(F32) for row in rise]), "sub", 1)
-    high = ring(jnp.concatenate([down[:3]] + [row.astype(F32) for row in sink]), "sub", -1)
+    slab_even = (lax.axis_index("slab") & 1) == 0
+    sub_even = (lax.axis_index("sub") & 1) == 0
+    first, second = swap(first, "slab", 0), swap(second, "slab", 1)
+    top, bottom = slice(rows - 1, rows), slice(0, 1)
+    one_up = jnp.where(slab_even, second[1, top], first[1, top])
+    two_up = jnp.where(slab_even, first[2, top], second[2, top])
+    one_down = jnp.where(slab_even, second[2, bottom], first[2, bottom])
+    two_down = jnp.where(slab_even, first[1, bottom], second[1, bottom])
+    up = jnp.concatenate([up[:3], one_up.astype(F32), two_up.astype(F32)])
+    down = jnp.concatenate([down[:3], one_down.astype(F32), two_down.astype(F32)])
+    low_high = (
+        swap(jnp.where(sub_even, up, down), "sub", 0),
+        swap(jnp.where(sub_even, down, up), "sub", 1),
+    )
     read = pl.pallas_call(
         functools.partial(stream_kernel, lax.axis_size("sub")),
         out_shape=shape((19, rows, depth), F32),
@@ -561,7 +601,7 @@
         out_specs=whole(),
         compiler_params=limits,
         name="stream",
-    )(collided, low, high, ahead, behind)
+    )(collided, *low_high, first, second)
     marker_force = jnp.transpose(marker_force, (1, 0, 2))[None, None]
     return (read.reshape(19, 1, rows, depth), marker_force)
 

time: 52.9 us -> 48.1 us (0.909)
  local copies, waits for them, and re-layouts: 2.6 us -> 0.04 us
  starting transfers between devices: 8.97 us -> 7.17 us
  Pallas kernels: 10.7 us -> 9.72 us
  waiting for transfers between devices: 4.4 us -> 5.04 us
    unnamed x24 -> x12, local copies, waits for them, and re-layouts: 2.59 us -> 0.04 us
    ppermute x4, starting transfers between devices: 8.97 us -> 7.17 us  [swap(): return lax.ppermute(value, axis, pairs)]
    ppermute x4, waiting for transfers between devices: 4.4 us -> 5.04 us  [swap(): return lax.ppermute(value, axis, pairs)]
    pallas_call x1, Pallas kernels: 4.8 us -> 4.27 us  [per_device(): pl.pallas_call(functools.partial(sample_kernel, slab_count, packed), out_...]
where the time goes in v3:
time: 48.1 us; the launch traced here: 47.7 us
  blocking collectives  24.4 us (51%)
  Pallas kernels  9.72 us (20%)
  starting transfers between devices  7.17 us (15%)
  waiting for transfers between devices  5.04 us (10%)
  between operations  1.36 us (3%)
    all_to_all x2, blocking collectives, exchange(): lax.all_to_all(value, 'slab', split_axis=0, concat_axis=0, tiled=True)  24.4 us
    ppermute x4, starting transfers between devices, swap(): return lax.ppermute(value, axis, pairs)  7.17 us
    ppermute x4, waiting for transfers between devices, swap(): return lax.ppermute(value, axis, pairs)  5.04 us
    pallas_call x1, Pallas kernels, per_device(): pl.pallas_call(functools.partial(sample_kernel, slab_count, packed), out_...  4.27 us
    pallas_call x1, Pallas kernels, per_device(): pl.pallas_call(functools.partial(spread_kernel, slab_count, packed), out_...  3.36 us
    pallas_call x1, Pallas kernels, per_device(): pl.pallas_call(functools.partial(owner_kernel, slab_count, packed), out_s...  1.26 us
  transfers between devices with their start and end apart: 4, of which 3 were waited for; matrix products, arithmetic and copies ran while one was open for 0% of the time, Pallas kernels for 0%

profile of v3, /device:TPU:1, one launch (start us, length us, event | category | flops | bytes accessed | tf_op | source)
XLA Modules:
  0.0 47.7 jit_solution(7261595067447993638)
XLA Ops:
  1.3 4.3 %sample.1 = (bf16[8,112,128]{2,1,0:T(8,128)(2,1)S(1)}, f32[256,8]{1,0:T(8,128)S(1)}) custom-call(s32[1]{0:T(128)} %bitcast.39.refs_0_, s32[8]{0:T(128)} %bitcast.50, s32[1,256]{1,0:T(1,128)} %bitcast.48, s32[1,256]{1,0:T(1,128)} %bitcast.49, f32[3,1,256]{2,1,0:T(1,128)} %bitcast.47, f32[19,32,128]{2,1,0:T(8,128)} %bitcast.40, s32[256,128]{1,0:T(8,128)} %bitcast.42), custom_call_target="tpu_custom_call" | custom-call | tf_op jit(solution)/shard_map/sample/pallas_call | solution.py:488
  5.6 0.0 copy-start.2
  5.6 0.0 copy-start.3
  5.6 0.0 copy-start.4
  5.6 0.0 copy-start.5
  5.6 13.3 %all_to_all.10.refs_0_ = bf16[8,112,128]{2,1,0:T(8,128)(2,1)S(1)} all-to-all(bf16[8,112,128]{2,1,0:T(8,128)(2,1)S(1)} %get-tuple-element.10), channel_id=1, replica_groups=mesh['slab'=8,'sub'=4] {'slab'}, dimensions={0} | all-to-all | bytes 458752 | tf_op jit(solution)/shard_map/all_to_all | solution.py:525
  18.9 0.0 copy-done.2
  18.9 0.0 copy-done.3
  18.9 0.0 copy-done.4
  18.9 0.0 copy-done.5
  18.9 0.0 copy-start.1
  18.9 1.3 %owner.1 = bf16[8,96,128]{2,1,0:T(8,128)(2,1)S(1)} custom-call(bf16[8,112,128]{2,1,0:T(8,128)(2,1)S(1)} %all_to_all.10.refs_0_, s32[4,256]{1,0:T(4,128)S(1)} %bitcast.44, f32[4,256]{1,0:T(4,128)S(1)} %bitcast.45, bf16[128,128]{1,0:T(8,128)(2,1)S(1)} %copy-done.2, bf16[128,128]{1,0:T(8,128)(2,1)S(1)} %copy-done.3), custom_call_target="tpu_custom_call" | custom-call | tf_op jit(solution)/shard_map/owner/pallas_call | solution.py:546
  20.2 0.0 copy-start
  20.2 11.1 %all_to_all.11.back_ref = bf16[8,96,128]{2,1,0:T(8,128)(2,1)S(1)} all-to-all(bf16[8,96,128]{2,1,0:T(8,128)(2,1)S(1)} %owner.1), channel_id=1, replica_groups=mesh['slab'=8,'sub'=4] {'slab'}, dimensions={0} | all-to-all | bytes 393216 | tf_op jit(solution)/shard_map/all_to_all | solution.py:525
  31.3 0.0 copy-done.1
  31.3 0.0 copy-done
  31.3 3.4 %spread.1 = (bf16[3,256,128]{2,1,0:T(8,128)(2,1)}, f32[19,32,128]{2,1,0:T(8,128)S(1)}, f32[8,128]{1,0:T(8,128)S(1)}, f32[8,128]{1,0:T(8,128)S(1)}, bf16[5,32,128...) custom-call(bf16[8,96,128]{2,1,0:T(8,128)(2,1)S(1)} %all_to_all.11.back_ref, ...), custom_call_target="tpu_custom_call" | custom-call | tf_op jit(solution)/shard_map/spread/pallas_call | solution.py:562
  34.6 2.8 %collective-permute-start = (bf16[5,32,128]{2,1,0:T(8,128)(2,1)S(1)}, bf16[5,32,128]{2,1,0:T(8,128)(2,1)S(1)}, u32[]{:S(2)}, u32[]{:S(2)}) collective-permute-start(bf16[5,32,128]{2,1,0:T(8,128)(2,1)S(1)} %get-tuple-element.14), channel_id=1, source_target_pairs={{0,28},{4,8},{8,4},{12,16},{16,12},{20,24},{24,20},{28,0},{1,29},{... | collective-permute-start | bytes 122888 | tf_op jit(solution)/shard_map/ppermute | solution.py:454
  37.4 0.0 collective-permute-start.1
  37.5 2.8 %collective-permute-done.second_ref = bf16[5,32,128]{2,1,0:T(8,128)(2,1)S(1)} collective-permute-done((bf16[5,32,128]{2,1,0:T(8,128)(2,1)S(1)}, bf16[5,32,128]{2,1,0:T(8,128)(2,1)S(1)}, u32[]{:S(2)}, u32[]{:S(2)}) %collective-permute-start) | collective-permute-done | bytes 40992 | tf_op jit(solution)/shard_map/ppermute | solution.py:454
  40.2 0.4 collective-permute-done.1.first_ref
  40.7 3.2 %collective-permute-start.2 = (f32[5,128]{1,0:T(8,128)S(1)}, f32[5,128]{1,0:T(8,128)S(1)}, u32[]{:S(2)}, u32[]{:S(2)}) collective-permute-start(f32[5,128]{1,0:T(8,128)S(1)} %get-tuple-element.25), channel_id=1, source_target_pairs={{0,1},{1,0},{2,3},{3,2},{4,5},{5,4},{6,7},{7,6},{8,9},{9,8},{10,11... | collective-permute-start | bytes 7688 | tf_op jit(solution)/shard_map/ppermute | solution.py:454
  43.9 1.2 %collective-permute-start.3 = (f32[5,128]{1,0:T(8,128)S(1)}, f32[5,128]{1,0:T(8,128)S(1)}, u32[]{:S(2)}, u32[]{:S(2)}) collective-permute-start(f32[5,128]{1,0:T(8,128)S(1)} %get-tuple-element.24), channel_id=1, source_target_pairs={{0,3},{1,2},{2,1},{3,0},{4,7},{5,6},{6,5},{7,4},{8,11},{9,10},{10,... | collective-permute-start | bytes 7688 | tf_op jit(solution)/shard_map/ppermute | solution.py:454
  45.0 0.0 collective-permute-done.2.one_ref
  45.0 1.9 %collective-permute-done.3.two_ref = f32[5,128]{1,0:T(8,128)S(1)} collective-permute-done((f32[5,128]{1,0:T(8,128)S(1)}, f32[5,128]{1,0:T(8,128)S(1)}, u32[]{:S(2)}, u32[]{:S(2)}) %collective-permute-start.3) | collective-permute-done | bytes 2592 | tf_op jit(solution)/shard_map/ppermute | solution.py:454
  46.9 0.8 %stream.1 = f32[19,32,128]{2,1,0:T(8,128)} custom-call(f32[19,32,128]{2,1,0:T(8,128)S(1)} %get-tuple-element.12.collided_ref, f32[5,128]{1,0:T(8,128)S(1)} %collective-permute-done.2.one_ref, f32[5,128]{1,0:T(8,128)S(1)} %collective-permute-done.3.two_ref, bf16[5,32,128]{2,1,0:T(8,128)(2,1)S(1)} %collective-permute-done.1.first_ref, ...), custom_call_target="tpu_custom_call" | custom-call | tf_op jit(solution)/shard_map/stream/pallas_call | solution.py:597
  (4 shorter events, 0.0 us)
Async XLA Ops:
  5.6 13.3 %copy-start.2 = (bf16[128,128]{1,0:T(8,128)(2,1)S(1)}, bf16[128,128]{1,0:T(8,128)(2,1)}, u32[]{:S(2)}) copy-start(bf16[128,128]{1,0:T(8,128)(2,1)} %refs_3_.1) | copy-start | bytes 98308
  5.6 13.3 %copy-start.3 = (bf16[128,128]{1,0:T(8,128)(2,1)S(1)}, bf16[128,128]{1,0:T(8,128)(2,1)}, u32[]{:S(2)}) copy-start(bf16[128,128]{1,0:T(8,128)(2,1)} %refs_4_.1) | copy-start | bytes 98308
  5.6 13.3 %copy-start.4 = (s32[1,1,256,4]{2,3,1,0:T(4,128)S(1)}, s32[1,1,256,4]{2,3,1,0:T(4,128)}, u32[]{:S(2)}) copy-start(s32[1,1,256,4]{2,3,1,0:T(4,128)} %param.18) | copy-start | bytes 12292
  5.6 13.3 %copy-start.5 = (f32[1,1,256,4]{2,3,1,0:T(4,128)S(1)}, f32[1,1,256,4]{2,3,1,0:T(4,128)}, u32[]{:S(2)}) copy-start(f32[1,1,256,4]{2,3,1,0:T(4,128)} %param.19) | copy-start | bytes 12292
  18.9 12.4 %copy-start.1 = (s32[1,1,256,128]{3,2,1,0:T(8,128)S(1)}, s32[1,1,256,128]{3,2,1,0:T(8,128)}, u32[]{:S(2)}) copy-start(s32[1,1,256,128]{3,2,1,0:T(8,128)} %param.12) | copy-start | bytes 393220
  20.2 11.1 %copy-start = (f32[19,1,32,128]{3,2,1,0:T(8,128)S(1)}, f32[19,1,32,128]{3,2,1,0:T(8,128)}, u32[]{:S(2)}) copy-start(f32[19,1,32,128]{3,2,1,0:T(8,128)} %param.11) | copy-start | bytes 933892
  34.6 5.6 %collective-permute-start = (bf16[5,32,128]{2,1,0:T(8,128)(2,1)S(1)}, bf16[5,32,128]{2,1,0:T(8,128)(2,1)S(1)}, u32[]{:S(2)}, u32[]{:S(2)}) collective-permute-start(bf16[5,32,128]{2,1,0:T(8,128)(2,1)S(1)} %get-tuple-element.14), channel_id=1, source_target_pairs={{0,28},{4,8},{8,4},{12,16},{16,12},{20,24},{24,20},{28,0},{1,29},{... | collective-permute-start | bytes 122888 | tf_op jit(solution)/shard_map/ppermute | solution.py:454
  37.4 3.2 %collective-permute-start.1 = (bf16[5,32,128]{2,1,0:T(8,128)(2,1)S(1)}, bf16[5,32,128]{2,1,0:T(8,128)(2,1)S(1)}, u32[]{:S(2)}, u32[]{:S(2)}) collective-permute-start(bf16[5,32,128]{2,1,0:T(8,128)(2,1)S(1)} %get-tuple-element.15), channel_id=1, source_target_pairs={{0,4},{4,0},{8,12},{12,8},{16,20},{20,16},{24,28},{28,24},{1,5},{5... | collective-permute-start | bytes 122888 | tf_op jit(solution)/shard_map/ppermute | solution.py:454
  40.7 4.4 %collective-permute-start.2 = (f32[5,128]{1,0:T(8,128)S(1)}, f32[5,128]{1,0:T(8,128)S(1)}, u32[]{:S(2)}, u32[]{:S(2)}) collective-permute-start(f32[5,128]{1,0:T(8,128)S(1)} %get-tuple-element.25), channel_id=1, source_target_pairs={{0,1},{1,0},{2,3},{3,2},{4,5},{5,4},{6,7},{7,6},{8,9},{9,8},{10,11... | collective-permute-start | bytes 7688 | tf_op jit(solution)/shard_map/ppermute | solution.py:454
  43.9 3.0 %collective-permute-start.3 = (f32[5,128]{1,0:T(8,128)S(1)}, f32[5,128]{1,0:T(8,128)S(1)}, u32[]{:S(2)}, u32[]{:S(2)}) collective-permute-start(f32[5,128]{1,0:T(8,128)S(1)} %get-tuple-element.24), channel_id=1, source_target_pairs={{0,3},{1,2},{2,1},{3,0},{4,7},{5,6},{6,5},{7,4},{8,11},{9,10},{10,... | collective-permute-start | bytes 7688 | tf_op jit(solution)/shard_map/ppermute | solution.py:454

commit v4 on v3

--- a/solution.py
+++ b/solution.py
@@ -36,8 +36,7 @@
 backward_x = [2, 8, 10, 12, 14]
 upward_y = [3, 15, 17, 7, 10]
 downward_y = [4, 16, 18, 9, 8]
-sample_unroll = 256
-spread_unroll = 256
+mark_rows = 8
 kernel_memory = 16 << 20
 BF = jnp.bfloat16
 F32 = jnp.float32
@@ -104,17 +103,23 @@
     return blocks[0]
 
 
-def sample_kernel(
-    slab_count,
-    packed,
-    *refs,
-):
+def pieces_of(value):
+    parts = []
+    for step in range(3):
+        part = value.astype(BF)
+        parts.append(part)
+        if step < 2:
+            value = value - part.astype(F32)
+    return parts
+
+
+def sample_kernel(slab_count, packed, *refs):
     sources, refs = refs[:7], refs[7:]
     slip_ref, refs = refs[0], refs[1:]
     if not packed:
         spot_ref, refs = refs[0], refs[1:]
-    cols_ref, refs = refs[0], refs[1:]
-    targets, (z_ref, y_ref, sampled_ref, sems) = refs[:7], refs[7:]
+    send_ref, sorted_ref, z_ref, y_ref = refs[:4]
+    targets, (sems,) = refs[4:11], refs[11:]
     copies = [
         pltpu.make_async_copy(source, target, sems.at[number])
         for number, (source, target) in enumerate(zip(sources, targets))
@@ -147,16 +152,37 @@
     earlier = dot_nn(chosen.astype(BF), before)
     position = jnp.sum(chosen * earlier, axis=0, keepdims=True)
     send_row = jnp.where(alive, owner_f * float(capacity) + position, -1.0)
-
-    count = jnp.where(alive, marker_count_ref[...], 0).astype(F32)
-    velocity = jnp.concatenate([velocity_ref[c] for c in range(3)], axis=0)
+    place = jnp.where(iota((slots, slots), 0) == send_row, 1.0, 0.0).astype(BF)
+
+    where_to = jnp.where(iota((width, slots), 0) == position, 1.0, 0.0).astype(BF)
+    if packed:
+        taken = (iota((slab_count * mark_rows, slots), 0, jnp.int32) // mark_rows).astype(
+            F32
+        ) == owner_f
+        marks = dot_nt(jnp.where(taken, spot + 1.0, 0.0).astype(BF), where_to)
+        slip_ref[:, 3 * capacity :, :] = marks.reshape(slab_count, mark_rows, width).astype(BF)
+    else:
+        spot_ref[...] = dot_nt((chosen * (spot + 1.0)).astype(BF), where_to).astype(BF)
+
+    count = marker_count_ref[...].astype(F32)
+    pieces = pieces_of(jnp.concatenate([velocity_ref[c] for c in range(3)], axis=0))
     stack = jnp.concatenate(
-        [velocity, count, send_row, jnp.zeros((3, slots), F32)], axis=0
-    )
-    cols = jnp.transpose(stack)
-    cols_ref[...] = cols
+        [piece.astype(F32) for piece in pieces] + [count, send_row, jnp.zeros((5, slots), F32)],
+        axis=0,
+    )
+    turned = jnp.transpose(stack)
+    send_ref[...] = turned[:, 8:16]
+    arranged = dot_nn(place, turned.astype(BF))
+    velocity = (arranged[:, 0:3] + arranged[:, 3:6]) + arranged[:, 6:9]
+    sorted_ref[...] = arranged[:, 8:16]
+
     for copy in copies[5:]:
         copy.wait()
+    cells = cell_ref[...]
+    parted = jnp.concatenate([(cells % depth).astype(BF), (cells // depth).astype(BF)], axis=1)
+    moved = dot_nn(place, parted)
+    z_ref[...] = moved[:, :width]
+    y_ref[...] = moved[:, width:]
 
     density, moment = moments_of([pops_ref[number] for number in range(19)])
     flow = jnp.concatenate([part / density for part in moment], axis=0)
@@ -164,17 +190,11 @@
     low = (flow - high.astype(F32)).astype(BF)
     flow_pair = jnp.concatenate([high, low], axis=1)
 
-    cells = cell_ref[...]
-    z_ref[...] = (cells % depth).astype(F32)
-    y_ref[...] = (cells // depth).astype(F32)
-
-    group = math.gcd(slots, sample_unroll)
-
-    def sample_group(step, carry):
-        base = pl.multiple_of(step * group, group)
-        for eight in range(0, group, 8):
-            z_rows = z_ref[pl.ds(base + eight, 8), :]
-            y_rows = y_ref[pl.ds(base + eight, 8), :]
+    for base in range(0, slots, 16):
+        found_rows = []
+        for eight in range(base, base + 16, 8):
+            z_rows = z_ref[eight : eight + 8, :]
+            y_rows = y_ref[eight : eight + 8, :]
             parts = [[], [], []]
             for first in range(0, 8, 2):
                 picks = jnp.concatenate(
@@ -192,32 +212,35 @@
                             found[c] = jnp.where(mask, picked[at : at + 8, cut], found[c])
                     for c in range(3):
                         parts[c].append(found[c])
-            for c in range(3):
-                sampled_ref[c, pl.ds(base + eight, 8), :] = fold_rows(parts[c])
-        return carry
-
-    lax.fori_loop(0, slots // group, sample_group, 0)
-
-    live = iota((slots, width), 1) < cols[:, 3:4]
-    slips = []
-    for c in range(3):
-        slips.append(jnp.where(live, cols[:, c : c + 1] - sampled_ref[c], 0.0).astype(BF))
-    place = jnp.where(iota((slots, slots), 0) == send_row, 1.0, 0.0).astype(BF)
-    sent = dot_nn(place, jnp.concatenate(slips, axis=1)).astype(BF)
-    where_to = jnp.where(iota((width, slots), 0) == position, 1.0, 0.0).astype(BF)
-    if packed:
+            found_rows.append([fold_rows(parts[c]) for c in range(3)])
+        live = iota((16, width), 1) < arranged[base : base + 16, 9:10]
         for c in range(3):
-            slip_ref[:, c * capacity : (c + 1) * capacity, :] = sent[
-                :, c * width : (c + 1) * width
-            ].reshape(slab_count, capacity, width)
-        taken = (iota((slab_count * 16, slots), 0, jnp.int32) // 16).astype(F32) == owner_f
-        marks = dot_nt(jnp.where(taken, spot + 1.0, 0.0).astype(BF), where_to)
-        slip_ref[:, 3 * capacity :, :] = marks.astype(BF).reshape(slab_count, 16, width)
-    else:
-        for c in range(3):
-            slip_ref[c] = sent[:, c * width : (c + 1) * width]
-        marks = dot_nt((chosen * (spot + 1.0)).astype(BF), where_to)
-        spot_ref[...] = marks.astype(BF)
+            sampled = jnp.concatenate([found_rows[0][c], found_rows[1][c]], axis=0)
+            slip = jnp.where(live, velocity[base : base + 16, c : c + 1] - sampled, 0.0)
+            if packed:
+                at = c * capacity + base % capacity
+                slip_ref[base // capacity, at : at + 16, :] = slip.astype(BF)
+            else:
+                slip_ref[c, base : base + 16, :] = slip.astype(BF)
+
+
+def weight_kernel(list_ref, gap_ref, weight_ref):
+    pairs, slots = list_ref.shape
+    filler = jnp.zeros((-2 * pairs % 8, slots), F32)
+    turned = jnp.transpose(
+        jnp.concatenate(
+            [list_ref[...].astype(F32), 1.0 / gap_ref[...], filler][: 2 + (2 * pairs % 8 > 0)],
+            axis=0,
+        )
+    )
+    column = iota((slots, slots), 1)
+    weight = jnp.zeros((slots, slots), F32)
+    for k in range(pairs):
+        inverse = turned[:, pairs + k : pairs + k + 1]
+        weight = weight + jnp.where(column == turned[:, k : k + 1], inverse, 0.0)
+    high = weight.astype(BF)
+    weight_ref[0] = high
+    weight_ref[1] = (weight - high.astype(F32)).astype(BF)
 
 
 def owner_kernel(
@@ -226,9 +249,9 @@
     *refs,
 ):
     if packed:
-        got_ref, list_ref, gap_ref, self_ref, pair_ref, out_ref = refs
+        got_ref, weight_ref, self_ref, pair_ref, out_ref = refs
         width = got_ref.shape[2]
-        slots = list_ref.shape[1]
+        slots = weight_ref.shape[1]
         capacity = slots // slab_count
         got = jnp.concatenate(
             [
@@ -243,7 +266,7 @@
         for start in range(0, slab_count, per_tile):
             total = jnp.zeros((8, width), F32)
             for source in range(start, min(start + per_tile, slab_count)):
-                mark = got_ref[source, 3 * capacity : 3 * capacity + 16, :].astype(F32)[:8]
+                mark = got_ref[source, 3 * capacity : 3 * capacity + mark_rows, :].astype(F32)
                 off = (source - start) * capacity
                 if off:
                     mark = pltpu.roll(mark, off, 1)
@@ -252,9 +275,9 @@
             tiles.append(total)
         spots = jnp.concatenate(tiles, axis=1) - 1.0
     else:
-        got_ref, spot_ref, list_ref, gap_ref, self_ref, pair_ref, out_ref = refs
+        got_ref, spot_ref, weight_ref, self_ref, pair_ref, out_ref = refs
         width = got_ref.shape[2]
-        slots = list_ref.shape[1]
+        slots = weight_ref.shape[1]
         got = jnp.concatenate([got_ref[c] for c in range(3)], axis=1)
         spots = jnp.broadcast_to(spot_ref[...].astype(F32), (8, slots)) - 1.0
 
@@ -262,21 +285,8 @@
     spot_col = jnp.transpose(spots)[:, :1]
     land = jnp.where(iota((slots, slots), 0) == spot_row, 1.0, 0.0).astype(BF)
     reply = jnp.where(iota((slots, slots), 1) == spot_col, 1.0, 0.0).astype(BF)
-    pairs = list_ref.shape[0]
-    filler = jnp.zeros((-2 * pairs % 8, slots), F32)
-    turned = jnp.transpose(
-        jnp.concatenate([list_ref[...].astype(F32), 1.0 / gap_ref[...], filler][: 2 + (2 * pairs % 8 > 0)], axis=0)
-    )
-    partner, inverse = turned[:, :pairs], turned[:, pairs : 2 * pairs]
-    column = iota((slots, slots), 1)
-    weight = jnp.zeros((slots, slots), F32)
-    for k in range(pairs):
-        weight = weight + jnp.where(column == partner[:, k : k + 1], inverse[:, k : k + 1], 0.0)
-    high = weight.astype(BF)
-    low = (weight - high.astype(F32)).astype(BF)
-
     owned = dot_nn(land, got).astype(BF)
-    near = (dot_nn(high, owned) + dot_nn(low, owned)).astype(BF)
+    near = (dot_nn(weight_ref[0], owned) + dot_nn(weight_ref[1], owned)).astype(BF)
     coupling = jnp.concatenate([self_ref[...], pair_ref[...]], axis=0)
     fixed = []
     for c in range(3):
@@ -294,58 +304,51 @@
             out_ref[c] = cut
 
 
+def returned_rows(slab_count, packed, back_ref, sorted_ref, base, count):
+    if packed:
+        capacity = sorted_ref.shape[0] // slab_count
+        at, block = base % capacity, slice(base // capacity, (base + count - 1) // capacity + 1)
+        take = min(count, capacity)
+        parts = [
+            back_ref[block, c * capacity + at : c * capacity + at + take, :].reshape(count, -1)
+            for c in range(3)
+        ]
+    else:
+        parts = [back_ref[c, base : base + count, :] for c in range(3)]
+    live = iota(parts[0].shape, 1) < sorted_ref[base : base + count, 1:2]
+    return [jnp.where(live, part.astype(F32), 0.0) for part in parts]
+
+
+def finish_kernel(slab_count, packed, back_ref, sorted_ref, send_ref, out_ref):
+    slots = sorted_ref.shape[0]
+    masked = returned_rows(slab_count, packed, back_ref, sorted_ref, 0, slots)
+    fetch = jnp.where(iota((slots, slots), 1) == send_ref[:, 2:3], 1.0, 0.0).astype(BF)
+    for c in range(3):
+        out_ref[c] = dot_nn(fetch, masked[c].astype(BF)).astype(BF)
+
+
 def spread_kernel(
     slab_count,
     packed,
     back_ref,
-    cols_ref,
-    cell_ref,
+    sorted_ref,
+    z_ref,
+    y_ref,
     pops_ref,
-    force_out_ref,
     collided_ref,
     up_ref,
     down_ref,
     first_ref,
     second_ref,
-    z_ref,
-    y_ref,
-    force_ref,
 ):
-    slots, width = cell_ref.shape
+    slots, width = z_ref.shape
     rows, depth = pops_ref.shape[1:]
-    capacity = slots // slab_count
-    if packed:
-        back = jnp.concatenate(
-            [
-                back_ref[:, c * capacity : (c + 1) * capacity, :].reshape(slots, width)
-                for c in range(3)
-            ],
-            axis=1,
-        )
-    else:
-        back = jnp.concatenate([back_ref[c] for c in range(3)], axis=1)
-    cols = cols_ref[...]
-    fetch = jnp.where(iota((slots, slots), 1) == cols[:, 4:5], 1.0, 0.0).astype(BF)
-    own = dot_nn(fetch, back)
-    live = iota((slots, width), 1) < cols[:, 3:4]
-    for c in range(3):
-        masked = jnp.where(live, own[:, c * width : (c + 1) * width], 0.0)
-        force_ref[c] = masked
-        force_out_ref[c] = masked.astype(BF)
-
-    cells = cell_ref[...]
-    z_ref[...] = (cells % depth).astype(F32)
-    y_ref[...] = (cells // depth).astype(F32)
-
-    group = math.gcd(slots, spread_unroll)
-
-    def spread_group(step, total):
-        base = pl.multiple_of(step * group, group)
-        z_rows = z_ref[pl.ds(base, group), :]
-        y_rows = y_ref[pl.ds(base, group), :]
-        f_rows = [force_ref[c, pl.ds(base, group), :] for c in range(3)]
-        picks, terms = [], []
-        for s in range(group):
+    picks, terms = [], []
+    for base in range(0, slots, 16):
+        f_rows = returned_rows(slab_count, packed, back_ref, sorted_ref, base, 16)
+        z_rows = z_ref[base : base + 16, :]
+        y_rows = y_ref[base : base + 16, :]
+        for s in range(16):
             picks.append(one_hot_rows(z_rows[s : s + 1], depth))
             tall = jnp.broadcast_to(y_rows[s : s + 1], (16, width)).astype(BF)
             parts = []
@@ -355,11 +358,7 @@
                     number = (iota((16, width), 0) + float(start)).astype(BF)
                     parts.append(jnp.where(number == tall, value, jnp.zeros((), BF)))
             terms.append(jnp.concatenate(parts, axis=0))
-        return total + dot_nt(jnp.concatenate(terms, axis=1), jnp.concatenate(picks, axis=1))
-
-    total = lax.fori_loop(
-        0, slots // group, spread_group, jnp.zeros((3 * rows, depth), F32)
-    )
+    total = dot_nt(jnp.concatenate(terms, axis=1), jnp.concatenate(picks, axis=1))
 
     force = [total[c * rows : (c + 1) * rows] for c in range(3)]
     pops = [pops_ref[number] for number in range(19)]
@@ -481,10 +480,10 @@
     limits = pltpu.CompilerParams(vmem_limit_bytes=kernel_memory)
 
     if packed:
-        sample_out = [shape((slab_count, 3 * capacity + 16, width), BF)]
+        sample_out = [shape((slab_count, 3 * capacity + mark_rows, width), BF)]
     else:
         sample_out = [shape((3, slots, width), BF), shape((slab_count, width), BF)]
-    sample_out.append(shape((slots, 8), F32))
+    sample_out += [shape((slots, 8), F32)] * 2 + [shape((slots, width), F32)] * 2
     results = pl.pallas_call(
         functools.partial(sample_kernel, slab_count, packed),
         out_shape=sample_out,
@@ -498,9 +497,6 @@
             pltpu.VMEM((3, 1, slots), F32),
             pltpu.VMEM((19, rows, depth), F32),
             pltpu.VMEM((slots, width), jnp.int32),
-            pltpu.VMEM((slots, width), F32),
-            pltpu.VMEM((slots, width), F32),
-            pltpu.VMEM((3, slots, width), F32),
             pltpu.SemaphoreType.DMA((7,)),
         ],
         compiler_params=limits,
@@ -519,7 +515,19 @@
             )
         ],
     )
-    cols = results[-1]
+    send, ordered, z_cells, y_cells = results[-4:]
+    weights = pl.pallas_call(
+        weight_kernel,
+        out_shape=shape((2, slots, slots), BF),
+        in_specs=[whole()] * 2,
+        out_specs=whole(),
+        compiler_params=limits,
+        cost_estimate=pl.CostEstimate(flops=10_000_000, bytes_accessed=300_000, transcendentals=0),
+        name="weights",
+    )(
+        jnp.transpose(pair_list.reshape(slots, -1)),
+        jnp.transpose(pair_gap.reshape(slots, -1)),
+    )
 
     def exchange(value):
         return lax.all_to_all(value, "slab", split_axis=0, concat_axis=0, tiled=True)
@@ -546,39 +554,41 @@
     reply = pl.pallas_call(
         functools.partial(owner_kernel, slab_count, packed),
         out_shape=reply_shape,
-        in_specs=[whole()] * (len(arrived) + 4),
+        in_specs=[whole()] * (len(arrived) + 3),
         out_specs=whole(),
         compiler_params=limits,
         name="owner",
     )(
         *arrived,
-        jnp.transpose(pair_list.reshape(slots, -1)),
-        jnp.transpose(pair_gap.reshape(slots, -1)),
+        weights,
         self_coupling,
         pair_coupling,
     )
     back = exchange(reply) if packed else by_component(exchange(by_owner(reply)))
 
-    marker_force, collided, up, down, first, second = pl.pallas_call(
+    collided, up, down, first, second = pl.pallas_call(
         functools.partial(spread_kernel, slab_count, packed),
         out_shape=[
-            shape((3, slots, width), BF),
             shape((19, rows, depth), F32),
             shape((8, depth), F32),
             shape((8, depth), F32),
             shape((5, rows, depth), BF),
             shape((5, rows, depth), BF),
         ],
-        in_specs=[whole()] * 4,
-        out_specs=[whole()] * 6,
-        scratch_shapes=[
-            pltpu.VMEM((slots, width), F32),
-            pltpu.VMEM((slots, width), F32),
-            pltpu.VMEM((3, slots, width), F32),
-        ],
+        in_specs=[whole()] * 5,
+        out_specs=[whole()] * 5,
         compiler_params=limits,
         name="spread",
-    )(back, cols, cells, pops)
+    )(back, ordered, z_cells, y_cells, pops)
+    marker_force = pl.pallas_call(
+        functools.partial(finish_kernel, slab_count, packed),
+        out_shape=shape((3, slots, width), BF),
+        in_specs=[whole()] * 3,
+        out_specs=whole(),
+        compiler_params=limits,
+        cost_estimate=pl.CostEstimate(flops=50_000_000, bytes_accessed=400_000, transcendentals=0),
+        name="finish",
+    )(back, ordered, send)
 
     slab_even = (lax.axis_index("slab") & 1) == 0
     sub_even = (lax.axis_index("sub") & 1) == 0

time: 48.1 us -> 48.1 us (level)
  blocking collectives: 24.4 us -> 11 us
  starting transfers between devices: 7.17 us -> 13.6 us
  waiting for transfers between devices: 5.04 us -> 10.2 us
  Pallas kernels: 9.72 us -> 11.5 us
    all_to_all x2 -> x1, blocking collectives: 24.4 us -> 11 us  [exchange(): lax.all_to_all(value, 'slab', split_axis=0, concat_axis=0, tiled=True)]
    all_to_all x0 -> x1, starting transfers between devices: none -> 6.38 us  [exchange(): lax.all_to_all(value, 'slab', split_axis=0, concat_axis=0, tiled=True)]
    all_to_all x0 -> x1, waiting for transfers between devices: none -> 6.17 us  [exchange(): lax.all_to_all(value, 'slab', split_axis=0, concat_axis=0, tiled=True)]
    pallas_call x0 -> x2, Pallas kernels: none -> 1.56 us  [the longest x1 1.02 us: per_device(): pl.pallas_call(functools.partial(finish_kernel, slab_count, packed), out_...]
    ppermute x4, waiting for transfers between devices: 5.04 us -> 4 us  [swap(): return lax.ppermute(value, axis, pairs)]
    pallas_call x1, Pallas kernels: 4.27 us -> 5.18 us  [per_device(): pl.pallas_call(functools.partial(sample_kernel, slab_count, packed), out_...]
  transfers between devices with their start and end apart: 4 -> 5, of which waited for: 3 -> 4; matrix products, arithmetic and copies ran while one was open for 0% -> 0% of each run, Pallas kernels for 0% -> 3%
where the time goes in v4:
time: 48.1 us; the launch traced here: 47.7 us
  starting transfers between devices  13.6 us (28%)
  Pallas kernels  11.5 us (24%)
  blocking collectives  11 us (23%)
  waiting for transfers between devices  10.2 us (21%)
  between operations  1.37 us (3%)
    all_to_all x1, blocking collectives, exchange(): lax.all_to_all(value, 'slab', split_axis=0, concat_axis=0, tiled=True)  11 us
    ppermute x4, starting transfers between devices, swap(): return lax.ppermute(value, axis, pairs)  7.25 us
    all_to_all x1, starting transfers between devices, exchange(): lax.all_to_all(value, 'slab', split_axis=0, concat_axis=0, tiled=True)  6.38 us
    all_to_all x1, waiting for transfers between devices, exchange(): lax.all_to_all(value, 'slab', split_axis=0, concat_axis=0, tiled=True)  6.17 us
    pallas_call x1, Pallas kernels, per_device(): pl.pallas_call(functools.partial(sample_kernel, slab_count, packed), out_...  5.18 us
    ppermute x4, waiting for transfers between devices, swap(): return lax.ppermute(value, axis, pairs)  4 us
    pallas_call x1, Pallas kernels, per_device(): pl.pallas_call(functools.partial(spread_kernel, slab_count, packed), out_...  3 us
    pallas_call x1, Pallas kernels, per_device(): pl.pallas_call(functools.partial(finish_kernel, slab_count, packed), out_...  1.02 us
  transfers between devices with their start and end apart: 5, of which 4 were waited for; matrix products, arithmetic and copies ran while one was open for 0% of the time, Pallas kernels for 3%

profile of v4, /device:TPU:1, one launch (start us, length us, event | category | flops | bytes accessed | tf_op | source)
XLA Modules:
  0.0 47.7 jit_solution(15192370397215925581)
XLA Ops:
  1.3 5.2 %sample.1 = (bf16[8,104,128]{2,1,0:T(8,128)(2,1)}, f32[256,8]{1,0:T(8,128)S(1)}, f32[256,8]{1,0:T(8,128)S(1)}, f32[256,128]{1,0:T(8,128)S(1)}, f32[256,128]{1,0:T(8,128)S(1)}) custom-call(s32[1]{0:T(128)} %bitcast.39.refs_0_, s32[8]{0:T(128)} %bitcast.50, s32[1,256]{1,0:T(1,128)} %bitcast.48, s32[1,256]{1,0:T(1,128)} %bitcast.49, f32[3,1,256]{2,1,0:T(1,128)} %bitcast.47, ...), custom_call_target="tpu_custom_call" | custom-call | tf_op jit(solution)/shard_map/sample/pallas_call | solution.py:487
  6.5 0.0 copy-start.3
  6.5 0.0 copy-start.4
  6.5 6.4 %all-to-all-start = ((bf16[8,104,128]{2,1,0:T(8,128)(2,1)}), bf16[8,104,128]{2,1,0:T(8,128)(2,1)S(1)}, u32[]{:S(2)}, u32[]{:S(2)}) async-start(bf16[8,104,128]{2,1,0:T(8,128)(2,1)} %get-tuple-element.12), calls=%async_computation | async-start | bytes 425984 | tf_op jit(solution)/shard_map/all_to_all | solution.py:533
  12.9 0.0 copy-done.3
  12.9 0.0 copy-done.4
  12.9 0.0 copy-start.1
  12.9 0.0 copy-start.2
  12.9 0.5 %weights.1.refs_1_ = bf16[2,256,256]{2,1,0:T(8,128)(2,1)S(1)} custom-call(s32[4,256]{1,0:T(4,128)S(1)} %bitcast.42, f32[4,256]{1,0:T(4,128)S(1)} %bitcast.43), custom_call_target="tpu_custom_call" | custom-call | flops 10000000 | bytes 300000 | tf_op jit(solution)/shard_map/weights/pallas_call | solution.py:519
  13.5 6.2 %all-to-all-done.refs_0_ = bf16[8,104,128]{2,1,0:T(8,128)(2,1)S(1)} async-done(((bf16[8,104,128]{2,1,0:T(8,128)(2,1)}), bf16[8,104,128]{2,1,0:T(8,128)(2,1)S(1)}, u32[]{:S(2)}, u32[]{:S(2)}) %all-to-all-start) | async-done | bytes 213024 | tf_op jit(solution)/shard_map/all_to_all | solution.py:533
  19.6 0.0 copy-done.1
  19.6 0.0 copy-done.2
  19.6 1.0 %owner.1 = bf16[8,96,128]{2,1,0:T(8,128)(2,1)S(1)} custom-call(bf16[8,104,128]{2,1,0:T(8,128)(2,1)S(1)} %all-to-all-done.refs_0_, bf16[2,256,256]{2,1,0:T(8,128)(2,1)S(1)} %weights.1.refs_1_, bf16[128,128]{1,0:T(8,128)(2,1)S(1)} %copy-done.1, bf16[128,128]{1,0:T(8,128)(2,1)S(1)} %copy-done.2), custom_call_target="tpu_custom_call" | custom-call | tf_op jit(solution)/shard_map/owner/pallas_call | solution.py:554
  20.6 0.0 copy-start
  20.6 11.0 %all_to_all.10.back_ref = bf16[8,96,128]{2,1,0:T(8,128)(2,1)S(1)} all-to-all(bf16[8,96,128]{2,1,0:T(8,128)(2,1)S(1)} %owner.1), channel_id=1, replica_groups=mesh['slab'=8,'sub'=4] {'slab'}, dimensions={0} | all-to-all | bytes 393216 | tf_op jit(solution)/shard_map/all_to_all | solution.py:533
  31.6 0.0 copy-done
  31.6 3.0 %spread.1 = (f32[19,32,128]{2,1,0:T(8,128)S(1)}, f32[8,128]{1,0:T(8,128)S(1)}, f32[8,128]{1,0:T(8,128)S(1)}, bf16[5,32,128]{2,1,0:T(8,128)(2,1)S(1)}, bf16[5,32,128]{2,1,0:T(8,128)(2,1)S(1)}) custom-call(bf16[8,96,128]{2,1,0:T(8,128)(2,1)S(1)} %all_to_all.10.back_ref, f32[256,8]{1,0:T(8,128)S(1)} %get-tuple-element.13.sorted_ref, ...), custom_call_target="tpu_custom_call" | custom-call | tf_op jit(solution)/shard_map/spread/pallas_call | solution.py:569
  34.6 2.9 %collective-permute-start = (bf16[5,32,128]{2,1,0:T(8,128)(2,1)S(1)}, bf16[5,32,128]{2,1,0:T(8,128)(2,1)S(1)}, u32[]{:S(2)}, u32[]{:S(2)}) collective-permute-start(bf16[5,32,128]{2,1,0:T(8,128)(2,1)S(1)} %get-tuple-element.18), channel_id=1, source_target_pairs={{0,28},{4,8},{8,4},{12,16},{16,12},{20,24},{24,20},{28,0},{1,29},{... | collective-permute-start | bytes 122888 | tf_op jit(solution)/shard_map/ppermute | solution.py:453
  37.5 0.0 collective-permute-start.1
  37.5 2.8 %collective-permute-done.second_ref = bf16[5,32,128]{2,1,0:T(8,128)(2,1)S(1)} collective-permute-done((bf16[5,32,128]{2,1,0:T(8,128)(2,1)S(1)}, bf16[5,32,128]{2,1,0:T(8,128)(2,1)S(1)}, u32[]{:S(2)}, u32[]{:S(2)}) %collective-permute-start) | collective-permute-done | bytes 40992 | tf_op jit(solution)/shard_map/ppermute | solution.py:453
  40.2 0.4 collective-permute-done.1.first_ref
  40.7 3.2 %collective-permute-start.2 = (f32[5,128]{1,0:T(8,128)S(1)}, f32[5,128]{1,0:T(8,128)S(1)}, u32[]{:S(2)}, u32[]{:S(2)}) collective-permute-start(f32[5,128]{1,0:T(8,128)S(1)} %get-tuple-element.29), channel_id=1, source_target_pairs={{0,1},{1,0},{2,3},{3,2},{4,5},{5,4},{6,7},{7,6},{8,9},{9,8},{10,11... | collective-permute-start | bytes 7688 | tf_op jit(solution)/shard_map/ppermute | solution.py:453
  43.9 1.2 %collective-permute-start.3 = (f32[5,128]{1,0:T(8,128)S(1)}, f32[5,128]{1,0:T(8,128)S(1)}, u32[]{:S(2)}, u32[]{:S(2)}) collective-permute-start(f32[5,128]{1,0:T(8,128)S(1)} %get-tuple-element.28), channel_id=1, source_target_pairs={{0,3},{1,2},{2,1},{3,0},{4,7},{5,6},{6,5},{7,4},{8,11},{9,10},{10,... | collective-permute-start | bytes 7688 | tf_op jit(solution)/shard_map/ppermute | solution.py:453
  45.0 1.0 %finish.1 = bf16[3,256,128]{2,1,0:T(8,128)(2,1)} custom-call(bf16[8,96,128]{2,1,0:T(8,128)(2,1)S(1)} %all_to_all.10.back_ref, f32[256,8]{1,0:T(8,128)S(1)} %get-tuple-element.13.sorted_ref, f32[256,8]{1,0:T(8,128)S(1)} %get-tuple-element.21.send_ref), custom_call_target="tpu_custom_call" | custom-call | flops 50000000 | bytes 400000 | tf_op jit(solution)/shard_map/finish/pallas_call | solution.py:583
  46.0 0.0 collective-permute-done.2.one_ref
  46.0 0.8 %collective-permute-done.3.two_ref = f32[5,128]{1,0:T(8,128)S(1)} collective-permute-done((f32[5,128]{1,0:T(8,128)S(1)}, f32[5,128]{1,0:T(8,128)S(1)}, u32[]{:S(2)}, u32[]{:S(2)}) %collective-permute-start.3) | collective-permute-done | bytes 2592 | tf_op jit(solution)/shard_map/ppermute | solution.py:453
  46.9 0.8 %stream.1 = f32[19,32,128]{2,1,0:T(8,128)} custom-call(f32[19,32,128]{2,1,0:T(8,128)S(1)} %get-tuple-element.16.collided_ref, f32[5,128]{1,0:T(8,128)S(1)} %collective-permute-done.2.one_ref, f32[5,128]{1,0:T(8,128)S(1)} %collective-permute-done.3.two_ref, bf16[5,32,128]{2,1,0:T(8,128)(2,1)S(1)} %collective-permute-done.1.first_ref, ...), custom_call_target="tpu_custom_call" | custom-call | tf_op jit(solution)/shard_map/stream/pallas_call | solution.py:607
  (4 shorter events, 0.0 us)
Async XLA Ops:
  6.5 6.4 %copy-start.3 = (s32[1,1,256,4]{2,3,1,0:T(4,128)S(1)}, s32[1,1,256,4]{2,3,1,0:T(4,128)}, u32[]{:S(2)}) copy-start(s32[1,1,256,4]{2,3,1,0:T(4,128)} %param.18) | copy-start | bytes 12292
  6.5 6.4 %copy-start.4 = (f32[1,1,256,4]{2,3,1,0:T(4,128)S(1)}, f32[1,1,256,4]{2,3,1,0:T(4,128)}, u32[]{:S(2)}) copy-start(f32[1,1,256,4]{2,3,1,0:T(4,128)} %param.19) | copy-start | bytes 12292
  6.5 13.1 %all-to-all-start = ((bf16[8,104,128]{2,1,0:T(8,128)(2,1)}), bf16[8,104,128]{2,1,0:T(8,128)(2,1)S(1)}, u32[]{:S(2)}, u32[]{:S(2)}) async-start(bf16[8,104,128]{2,1,0:T(8,128)(2,1)} %get-tuple-element.12), calls=%async_computation | async-start | bytes 425984 | tf_op jit(solution)/shard_map/all_to_all | solution.py:533
  12.9 6.7 %copy-start.1 = (bf16[128,128]{1,0:T(8,128)(2,1)S(1)}, bf16[128,128]{1,0:T(8,128)(2,1)}, u32[]{:S(2)}) copy-start(bf16[128,128]{1,0:T(8,128)(2,1)} %refs_2_.1) | copy-start | bytes 98308
  12.9 6.7 %copy-start.2 = (bf16[128,128]{1,0:T(8,128)(2,1)S(1)}, bf16[128,128]{1,0:T(8,128)(2,1)}, u32[]{:S(2)}) copy-start(bf16[128,128]{1,0:T(8,128)(2,1)} %refs_3_.1) | copy-start | bytes 98308
  20.6 11.0 %copy-start = (f32[19,1,32,128]{3,2,1,0:T(8,128)S(1)}, f32[19,1,32,128]{3,2,1,0:T(8,128)}, u32[]{:S(2)}) copy-start(f32[19,1,32,128]{3,2,1,0:T(8,128)} %param.11) | copy-start | bytes 933892
  34.6 5.6 %collective-permute-start = (bf16[5,32,128]{2,1,0:T(8,128)(2,1)S(1)}, bf16[5,32,128]{2,1,0:T(8,128)(2,1)S(1)}, u32[]{:S(2)}, u32[]{:S(2)}) collective-permute-start(bf16[5,32,128]{2,1,0:T(8,128)(2,1)S(1)} %get-tuple-element.18), channel_id=1, source_target_pairs={{0,28},{4,8},{8,4},{12,16},{16,12},{20,24},{24,20},{28,0},{1,29},{... | collective-permute-start | bytes 122888 | tf_op jit(solution)/shard_map/ppermute | solution.py:453
  37.5 3.2 %collective-permute-start.1 = (bf16[5,32,128]{2,1,0:T(8,128)(2,1)S(1)}, bf16[5,32,128]{2,1,0:T(8,128)(2,1)S(1)}, u32[]{:S(2)}, u32[]{:S(2)}) collective-permute-start(bf16[5,32,128]{2,1,0:T(8,128)(2,1)S(1)} %get-tuple-element.19), channel_id=1, source_target_pairs={{0,4},{4,0},{8,12},{12,8},{16,20},{20,16},{24,28},{28,24},{1,5},{5... | collective-permute-start | bytes 122888 | tf_op jit(solution)/shard_map/ppermute | solution.py:453
  40.7 5.4 %collective-permute-start.2 = (f32[5,128]{1,0:T(8,128)S(1)}, f32[5,128]{1,0:T(8,128)S(1)}, u32[]{:S(2)}, u32[]{:S(2)}) collective-permute-start(f32[5,128]{1,0:T(8,128)S(1)} %get-tuple-element.29), channel_id=1, source_target_pairs={{0,1},{1,0},{2,3},{3,2},{4,5},{5,4},{6,7},{7,6},{8,9},{9,8},{10,11... | collective-permute-start | bytes 7688 | tf_op jit(solution)/shard_map/ppermute | solution.py:453
  43.9 3.0 %collective-permute-start.3 = (f32[5,128]{1,0:T(8,128)S(1)}, f32[5,128]{1,0:T(8,128)S(1)}, u32[]{:S(2)}, u32[]{:S(2)}) collective-permute-start(f32[5,128]{1,0:T(8,128)S(1)} %get-tuple-element.28), channel_id=1, source_target_pairs={{0,3},{1,2},{2,1},{3,0},{4,7},{5,6},{6,5},{7,4},{8,11},{9,10},{10,... | collective-permute-start | bytes 7688 | tf_op jit(solution)/shard_map/ppermute | solution.py:453

commit v5 on v4

--- a/solution.py
+++ b/solution.py
@@ -113,20 +113,40 @@
     return parts
 
 
+def pair_weights(list_ref, gap_ref, weight_ref):
+    pairs, slots = list_ref.shape
+    filler = jnp.zeros((-2 * pairs % 8, slots), F32)
+    turned = jnp.transpose(
+        jnp.concatenate(
+            [list_ref[...].astype(F32), 1.0 / gap_ref[...], filler][: 2 + (2 * pairs % 8 > 0)],
+            axis=0,
+        )
+    )
+    column = iota((slots, slots), 1)
+    weight = jnp.zeros((slots, slots), F32)
+    for k in range(pairs):
+        inverse = turned[:, pairs + k : pairs + k + 1]
+        weight = weight + jnp.where(column == turned[:, k : k + 1], inverse, 0.0)
+    high = weight.astype(BF)
+    weight_ref[0] = high
+    weight_ref[1] = (weight - high.astype(F32)).astype(BF)
+
+
 def sample_kernel(slab_count, packed, *refs):
-    sources, refs = refs[:7], refs[7:]
+    sources, refs = refs[:9], refs[9:]
     slip_ref, refs = refs[0], refs[1:]
     if not packed:
         spot_ref, refs = refs[0], refs[1:]
-    send_ref, sorted_ref, z_ref, y_ref = refs[:4]
-    targets, (sems,) = refs[4:11], refs[11:]
+    send_ref, sorted_ref, z_ref, y_ref, weight_ref = refs[:5]
+    targets, (sems,) = refs[5:14], refs[14:]
     copies = [
         pltpu.make_async_copy(source, target, sems.at[number])
         for number, (source, target) in enumerate(zip(sources, targets))
     ]
     for copy in copies:
         copy.start()
-    count_ref, table_ref, marker_count_ref, id_ref, velocity_ref, pops_ref, cell_ref = targets
+    count_ref, table_ref, marker_count_ref, id_ref, velocity_ref, *targets = targets
+    list_ref, gap_ref, cell_ref, pops_ref = targets
     slots, width = cell_ref.shape
     rows, depth = pops_ref.shape[1:]
     capacity = slots // slab_count
@@ -176,7 +196,10 @@
     velocity = (arranged[:, 0:3] + arranged[:, 3:6]) + arranged[:, 6:9]
     sorted_ref[...] = arranged[:, 8:16]
 
-    for copy in copies[5:]:
+    for copy in copies[5:7]:
+        copy.wait()
+    pair_weights(list_ref, gap_ref, weight_ref)
+    for copy in copies[7:]:
         copy.wait()
     cells = cell_ref[...]
     parted = jnp.concatenate([(cells % depth).astype(BF), (cells // depth).astype(BF)], axis=1)
@@ -222,25 +245,6 @@
                 slip_ref[base // capacity, at : at + 16, :] = slip.astype(BF)
             else:
                 slip_ref[c, base : base + 16, :] = slip.astype(BF)
-
-
-def weight_kernel(list_ref, gap_ref, weight_ref):
-    pairs, slots = list_ref.shape
-    filler = jnp.zeros((-2 * pairs % 8, slots), F32)
-    turned = jnp.transpose(
-        jnp.concatenate(
-            [list_ref[...].astype(F32), 1.0 / gap_ref[...], filler][: 2 + (2 * pairs % 8 > 0)],
-            axis=0,
-        )
-    )
-    column = iota((slots, slots), 1)
-    weight = jnp.zeros((slots, slots), F32)
-    for k in range(pairs):
-        inverse = turned[:, pairs + k : pairs + k + 1]
-        weight = weight + jnp.where(column == turned[:, k : k + 1], inverse, 0.0)
-    high = weight.astype(BF)
-    weight_ref[0] = high
-    weight_ref[1] = (weight - high.astype(F32)).astype(BF)
 
 
 def owner_kernel(
@@ -484,10 +488,11 @@
     else:
         sample_out = [shape((3, slots, width), BF), shape((slab_count, width), BF)]
     sample_out += [shape((slots, 8), F32)] * 2 + [shape((slots, width), F32)] * 2
+    sample_out.append(shape((2, slots, slots), BF))
     results = pl.pallas_call(
         functools.partial(sample_kernel, slab_count, packed),
         out_shape=sample_out,
-        in_specs=[whole(pltpu.HBM)] * 7,
+        in_specs=[whole(pltpu.HBM)] * 9,
         out_specs=[whole()] * len(sample_out),
         scratch_shapes=[
             pltpu.SMEM((1,), jnp.int32),
@@ -495,9 +500,11 @@
             pltpu.VMEM((1, slots), jnp.int32),
             pltpu.VMEM((1, slots), jnp.int32),
             pltpu.VMEM((3, 1, slots), F32),
+            pltpu.VMEM((pair_list.shape[3], slots), jnp.int32),
+            pltpu.VMEM((pair_list.shape[3], slots), F32),
+            pltpu.VMEM((slots, width), jnp.int32),
             pltpu.VMEM((19, rows, depth), F32),
-            pltpu.VMEM((slots, width), jnp.int32),
-            pltpu.SemaphoreType.DMA((7,)),
+            pltpu.SemaphoreType.DMA((9,)),
         ],
         compiler_params=limits,
         name="sample",
@@ -510,24 +517,14 @@
                 marker_count.reshape(1, slots),
                 particle_id.reshape(1, slots),
                 particle_velocity.reshape(3, 1, slots),
+                jnp.transpose(pair_list.reshape(slots, -1)),
+                jnp.transpose(pair_gap.reshape(slots, -1)),
+                cells,
                 pops,
-                cells,
             )
         ],
     )
-    send, ordered, z_cells, y_cells = results[-4:]
-    weights = pl.pallas_call(
-        weight_kernel,
-        out_shape=shape((2, slots, slots), BF),
-        in_specs=[whole()] * 2,
-        out_specs=whole(),
-        compiler_params=limits,
-        cost_estimate=pl.CostEstimate(flops=10_000_000, bytes_accessed=300_000, transcendentals=0),
-        name="weights",
-    )(
-        jnp.transpose(pair_list.reshape(slots, -1)),
-        jnp.transpose(pair_gap.reshape(slots, -1)),
-    )
+    send, ordered, z_cells, y_cells, weights = results[-5:]
 
     def exchange(value):
         return lax.all_to_all(value, "slab", split_axis=0, concat_axis=0, tiled=True)

time: 48.1 us -> 47.8 us (level)
  blocking collectives: 11 us -> 23.9 us
  starting transfers between devices: 13.6 us -> 7.24 us
  waiting for transfers between devices: 10.2 us -> 4 us
  Pallas kernels: 11.5 us -> 10.9 us
    all_to_all x1 -> x2, blocking collectives: 11 us -> 23.9 us  [exchange(): lax.all_to_all(value, 'slab', split_axis=0, concat_axis=0, tiled=True)]
    all_to_all x1 -> x0, starting transfers between devices: 6.38 us -> none  [exchange(): lax.all_to_all(value, 'slab', split_axis=0, concat_axis=0, tiled=True)]
    all_to_all x1 -> x0, waiting for transfers between devices: 6.17 us -> none  [exchange(): lax.all_to_all(value, 'slab', split_axis=0, concat_axis=0, tiled=True)]
    pallas_call x1 -> x0, Pallas kernels: 0.55 us -> none  [per_device(): pl.pallas_call(weight_kernel, out_shape=shape((2, slots, slots), BF), in_...]
  transfers between devices with their start and end apart: 5 -> 4, of which waited for: 4 -> 3; matrix products, arithmetic and copies ran while one was open for 0% -> 0% of each run, Pallas kernels for 3% -> 2%
where the time goes in v5:
time: 47.8 us; the launch traced here: 47.4 us
  blocking collectives  23.9 us (50%)
  Pallas kernels  10.9 us (23%)
  starting transfers between devices  7.24 us (15%)
  waiting for transfers between devices  4 us (8%)
  between operations  1.33 us (3%)
    all_to_all x2, blocking collectives, exchange(): lax.all_to_all(value, 'slab', split_axis=0, concat_axis=0, tiled=True)  23.9 us
    ppermute x4, starting transfers between devices, swap(): return lax.ppermute(value, axis, pairs)  7.24 us
    pallas_call x1, Pallas kernels, per_device(): pl.pallas_call(functools.partial(sample_kernel, slab_count, packed), out_...  5.1 us
    ppermute x4, waiting for transfers between devices, swap(): return lax.ppermute(value, axis, pairs)  4 us
    pallas_call x1, Pallas kernels, per_device(): pl.pallas_call(functools.partial(spread_kernel, slab_count, packed), out_...  3 us
    pallas_call x1, Pallas kernels, per_device(): pl.pallas_call(functools.partial(finish_kernel, slab_count, packed), out_...  1.02 us
    pallas_call x1, Pallas kernels, per_device(): pl.pallas_call(functools.partial(owner_kernel, slab_count, packed), out_s...  0.96 us
  transfers between devices with their start and end apart: 4, of which 3 were waited for; matrix products, arithmetic and copies ran while one was open for 0% of the time, Pallas kernels for 2%

profile of v5, /device:TPU:1, one launch (start us, length us, event | category | flops | bytes accessed | tf_op | source)
XLA Modules:
  0.0 47.4 jit_solution(14312626256689301886)
XLA Ops:
  1.3 5.1 %sample.1 = (bf16[8,104,128]{2,1,0:T(8,128)(2,1)S(1)}, f32[256,8]{1,0:T(8,128)S(1)}, f32[256,8]{1,0:T(8,128)S(1)}, f32[256,128]{1,0:T(8,128)S(1)}, f32[256,128]{...) custom-call(s32[1]{0:T(128)} %bitcast.39.refs_0_, s32[8]{0:T(128)} %bitcast.50, s32[1,256]{1,0:T(1,128)} %bitcast.48, ...), custom_call_target="tpu_custom_call" | custom-call | tf_op jit(solution)/shard_map/sample/pallas_call | solution.py:492
  6.4 0.0 copy-start.1
  6.4 0.0 copy-start.2
  6.4 12.9 %all_to_all.10.refs_0_ = bf16[8,104,128]{2,1,0:T(8,128)(2,1)S(1)} all-to-all(bf16[8,104,128]{2,1,0:T(8,128)(2,1)S(1)} %get-tuple-element.13), channel_id=1, replica_groups=mesh['slab'=8,'sub'=4] {'slab'}, dimensions={0} | all-to-all | bytes 425984 | tf_op jit(solution)/shard_map/all_to_all | solution.py:530
  19.3 0.0 copy-done.1
  19.3 0.0 copy-done.2
  19.3 1.0 %owner.1 = bf16[8,96,128]{2,1,0:T(8,128)(2,1)S(1)} custom-call(bf16[8,104,128]{2,1,0:T(8,128)(2,1)S(1)} %all_to_all.10.refs_0_, bf16[2,256,256]{2,1,0:T(8,128)(2,1)S(1)} %get-tuple-element.14.refs_1_, bf16[128,128]{1,0:T(8,128)(2,1)S(1)} %copy-done.1, bf16[128,128]{1,0:T(8,128)(2,1)S(1)} %copy-done.2), custom_call_target="tpu_custom_call" | custom-call | tf_op jit(solution)/shard_map/owner/pallas_call | solution.py:551
  20.3 0.0 copy-start
  20.3 11.0 %all_to_all.11.back_ref = bf16[8,96,128]{2,1,0:T(8,128)(2,1)S(1)} all-to-all(bf16[8,96,128]{2,1,0:T(8,128)(2,1)S(1)} %owner.1), channel_id=1, replica_groups=mesh['slab'=8,'sub'=4] {'slab'}, dimensions={0} | all-to-all | bytes 393216 | tf_op jit(solution)/shard_map/all_to_all | solution.py:530
  31.3 0.0 copy-done
  31.3 3.0 %spread.1 = (f32[19,32,128]{2,1,0:T(8,128)S(1)}, f32[8,128]{1,0:T(8,128)S(1)}, f32[8,128]{1,0:T(8,128)S(1)}, bf16[5,32,128]{2,1,0:T(8,128)(2,1)S(1)}, bf16[5,32,128]{2,1,0:T(8,128)(2,1)S(1)}) custom-call(bf16[8,96,128]{2,1,0:T(8,128)(2,1)S(1)} %all_to_all.11.back_ref, f32[256,8]{1,0:T(8,128)S(1)} %get-tuple-element.15.sorted_ref, ...), custom_call_target="tpu_custom_call" | custom-call | tf_op jit(solution)/shard_map/spread/pallas_call | solution.py:566
  34.3 2.9 %collective-permute-start = (bf16[5,32,128]{2,1,0:T(8,128)(2,1)S(1)}, bf16[5,32,128]{2,1,0:T(8,128)(2,1)S(1)}, u32[]{:S(2)}, u32[]{:S(2)}) collective-permute-start(bf16[5,32,128]{2,1,0:T(8,128)(2,1)S(1)} %get-tuple-element.20), channel_id=1, source_target_pairs={{0,28},{4,8},{8,4},{12,16},{16,12},{20,24},{24,20},{28,0},{1,29},{... | collective-permute-start | bytes 122888 | tf_op jit(solution)/shard_map/ppermute | solution.py:457
  37.2 0.0 collective-permute-start.1
  37.2 2.8 %collective-permute-done.second_ref = bf16[5,32,128]{2,1,0:T(8,128)(2,1)S(1)} collective-permute-done((bf16[5,32,128]{2,1,0:T(8,128)(2,1)S(1)}, bf16[5,32,128]{2,1,0:T(8,128)(2,1)S(1)}, u32[]{:S(2)}, u32[]{:S(2)}) %collective-permute-start) | collective-permute-done | bytes 40992 | tf_op jit(solution)/shard_map/ppermute | solution.py:457
  40.0 0.4 collective-permute-done.1.first_ref
  40.4 3.2 %collective-permute-start.2 = (f32[5,128]{1,0:T(8,128)S(1)}, f32[5,128]{1,0:T(8,128)S(1)}, u32[]{:S(2)}, u32[]{:S(2)}) collective-permute-start(f32[5,128]{1,0:T(8,128)S(1)} %get-tuple-element.31), channel_id=1, source_target_pairs={{0,1},{1,0},{2,3},{3,2},{4,5},{5,4},{6,7},{7,6},{8,9},{9,8},{10,11... | collective-permute-start | bytes 7688 | tf_op jit(solution)/shard_map/ppermute | solution.py:457
  43.6 1.2 %collective-permute-start.3 = (f32[5,128]{1,0:T(8,128)S(1)}, f32[5,128]{1,0:T(8,128)S(1)}, u32[]{:S(2)}, u32[]{:S(2)}) collective-permute-start(f32[5,128]{1,0:T(8,128)S(1)} %get-tuple-element.30), channel_id=1, source_target_pairs={{0,3},{1,2},{2,1},{3,0},{4,7},{5,6},{6,5},{7,4},{8,11},{9,10},{10,... | collective-permute-start | bytes 7688 | tf_op jit(solution)/shard_map/ppermute | solution.py:457
  44.7 1.0 %finish.1 = bf16[3,256,128]{2,1,0:T(8,128)(2,1)} custom-call(bf16[8,96,128]{2,1,0:T(8,128)(2,1)S(1)} %all_to_all.11.back_ref, f32[256,8]{1,0:T(8,128)S(1)} %get-tuple-element.15.sorted_ref, f32[256,8]{1,0:T(8,128)S(1)} %get-tuple-element.23.send_ref), custom_call_target="tpu_custom_call" | custom-call | flops 50000000 | bytes 400000 | tf_op jit(solution)/shard_map/finish/pallas_call | solution.py:580
  45.8 0.0 collective-permute-done.2.one_ref
  45.8 0.8 %collective-permute-done.3.two_ref = f32[5,128]{1,0:T(8,128)S(1)} collective-permute-done((f32[5,128]{1,0:T(8,128)S(1)}, f32[5,128]{1,0:T(8,128)S(1)}, u32[]{:S(2)}, u32[]{:S(2)}) %collective-permute-start.3) | collective-permute-done | bytes 2592 | tf_op jit(solution)/shard_map/ppermute | solution.py:457
  46.6 0.8 %stream.1 = f32[19,32,128]{2,1,0:T(8,128)} custom-call(f32[19,32,128]{2,1,0:T(8,128)S(1)} %get-tuple-element.18.collided_ref, f32[5,128]{1,0:T(8,128)S(1)} %collective-permute-done.2.one_ref, f32[5,128]{1,0:T(8,128)S(1)} %collective-permute-done.3.two_ref, bf16[5,32,128]{2,1,0:T(8,128)(2,1)S(1)} %collective-permute-done.1.first_ref, ...), custom_call_target="tpu_custom_call" | custom-call | tf_op jit(solution)/shard_map/stream/pallas_call | solution.py:604
  (4 shorter events, 0.0 us)
Async XLA Ops:
  6.4 13.0 %copy-start.1 = (bf16[128,128]{1,0:T(8,128)(2,1)S(1)}, bf16[128,128]{1,0:T(8,128)(2,1)}, u32[]{:S(2)}) copy-start(bf16[128,128]{1,0:T(8,128)(2,1)} %refs_2_.1) | copy-start | bytes 98308
  6.4 12.9 %copy-start.2 = (bf16[128,128]{1,0:T(8,128)(2,1)S(1)}, bf16[128,128]{1,0:T(8,128)(2,1)}, u32[]{:S(2)}) copy-start(bf16[128,128]{1,0:T(8,128)(2,1)} %refs_3_.1) | copy-start | bytes 98308
  20.3 11.0 %copy-start = (f32[19,1,32,128]{3,2,1,0:T(8,128)S(1)}, f32[19,1,32,128]{3,2,1,0:T(8,128)}, u32[]{:S(2)}) copy-start(f32[19,1,32,128]{3,2,1,0:T(8,128)} %param.11) | copy-start | bytes 933892
  34.3 5.6 %collective-permute-start = (bf16[5,32,128]{2,1,0:T(8,128)(2,1)S(1)}, bf16[5,32,128]{2,1,0:T(8,128)(2,1)S(1)}, u32[]{:S(2)}, u32[]{:S(2)}) collective-permute-start(bf16[5,32,128]{2,1,0:T(8,128)(2,1)S(1)} %get-tuple-element.20), channel_id=1, source_target_pairs={{0,28},{4,8},{8,4},{12,16},{16,12},{20,24},{24,20},{28,0},{1,29},{... | collective-permute-start | bytes 122888 | tf_op jit(solution)/shard_map/ppermute | solution.py:457
  37.2 3.2 %collective-permute-start.1 = (bf16[5,32,128]{2,1,0:T(8,128)(2,1)S(1)}, bf16[5,32,128]{2,1,0:T(8,128)(2,1)S(1)}, u32[]{:S(2)}, u32[]{:S(2)}) collective-permute-start(bf16[5,32,128]{2,1,0:T(8,128)(2,1)S(1)} %get-tuple-element.21), channel_id=1, source_target_pairs={{0,4},{4,0},{8,12},{12,8},{16,20},{20,16},{24,28},{28,24},{1,5},{5... | collective-permute-start | bytes 122888 | tf_op jit(solution)/shard_map/ppermute | solution.py:457
  40.4 5.4 %collective-permute-start.2 = (f32[5,128]{1,0:T(8,128)S(1)}, f32[5,128]{1,0:T(8,128)S(1)}, u32[]{:S(2)}, u32[]{:S(2)}) collective-permute-start(f32[5,128]{1,0:T(8,128)S(1)} %get-tuple-element.31), channel_id=1, source_target_pairs={{0,1},{1,0},{2,3},{3,2},{4,5},{5,4},{6,7},{7,6},{8,9},{9,8},{10,11... | collective-permute-start | bytes 7688 | tf_op jit(solution)/shard_map/ppermute | solution.py:457
  43.6 3.0 %collective-permute-start.3 = (f32[5,128]{1,0:T(8,128)S(1)}, f32[5,128]{1,0:T(8,128)S(1)}, u32[]{:S(2)}, u32[]{:S(2)}) collective-permute-start(f32[5,128]{1,0:T(8,128)S(1)} %get-tuple-element.30), channel_id=1, source_target_pairs={{0,3},{1,2},{2,1},{3,0},{4,7},{5,6},{6,5},{7,4},{8,11},{9,10},{10,... | collective-permute-start | bytes 7688 | tf_op jit(solution)/shard_map/ppermute | solution.py:457

commit v6 on v5

--- a/solution.py
+++ b/solution.py
@@ -40,6 +40,7 @@
 kernel_memory = 16 << 20
 BF = jnp.bfloat16
 F32 = jnp.float32
+PICK = jnp.float8_e4m3fn
 
 
 def iota(shape, dim, dtype=F32):
@@ -74,13 +75,14 @@
     return density, moment
 
 
-def one_hot_rows(row, count, kind=BF):
-    tall = jnp.broadcast_to(row, (16, row.shape[1])).astype(kind)
-    one, zero = jnp.ones((), kind), jnp.zeros((), kind)
+def one_hot_rows(row, count):
+    tile = (32, row.shape[1])
+    tall = jnp.broadcast_to(row, tile).astype(BF)
+    one, zero = jnp.ones(tile, F32).astype(PICK), jnp.zeros(tile, F32).astype(PICK)
     parts = []
-    for start in range(0, count, 16):
-        number = iota((16, row.shape[1]), 0, F32) + float(start)
-        parts.append(jnp.where(number.astype(kind) == tall, one, zero))
+    for start in range(0, count, 32):
+        number = (iota(tile, 0) + float(start)).astype(BF)
+        parts.append(jnp.where(number == tall, one, zero))
     return jnp.concatenate(parts, axis=0)
 
 
@@ -113,7 +115,7 @@
     return parts
 
 
-def pair_weights(list_ref, gap_ref, weight_ref):
+def pair_weights(list_ref, gap_ref):
     pairs, slots = list_ref.shape
     filler = jnp.zeros((-2 * pairs % 8, slots), F32)
     turned = jnp.transpose(
@@ -128,25 +130,23 @@
         inverse = turned[:, pairs + k : pairs + k + 1]
         weight = weight + jnp.where(column == turned[:, k : k + 1], inverse, 0.0)
     high = weight.astype(BF)
-    weight_ref[0] = high
-    weight_ref[1] = (weight - high.astype(F32)).astype(BF)
+    return jnp.concatenate([high, (weight - high.astype(F32)).astype(BF)], axis=1)
 
 
 def sample_kernel(slab_count, packed, *refs):
-    sources, refs = refs[:9], refs[9:]
+    sources, refs = refs[:7], refs[7:]
     slip_ref, refs = refs[0], refs[1:]
     if not packed:
         spot_ref, refs = refs[0], refs[1:]
-    send_ref, sorted_ref, z_ref, y_ref, weight_ref = refs[:5]
-    targets, (sems,) = refs[5:14], refs[14:]
+    send_ref, sorted_ref, z_ref, y_ref = refs[:4]
+    targets, (sems,) = refs[4:11], refs[11:]
     copies = [
         pltpu.make_async_copy(source, target, sems.at[number])
         for number, (source, target) in enumerate(zip(sources, targets))
     ]
     for copy in copies:
         copy.start()
-    count_ref, table_ref, marker_count_ref, id_ref, velocity_ref, *targets = targets
-    list_ref, gap_ref, cell_ref, pops_ref = targets
+    count_ref, table_ref, marker_count_ref, id_ref, velocity_ref, cell_ref, pops_ref = targets
     slots, width = cell_ref.shape
     rows, depth = pops_ref.shape[1:]
     capacity = slots // slab_count
@@ -196,10 +196,7 @@
     velocity = (arranged[:, 0:3] + arranged[:, 3:6]) + arranged[:, 6:9]
     sorted_ref[...] = arranged[:, 8:16]
 
-    for copy in copies[5:7]:
-        copy.wait()
-    pair_weights(list_ref, gap_ref, weight_ref)
-    for copy in copies[7:]:
+    for copy in copies[5:]:
         copy.wait()
     cells = cell_ref[...]
     parted = jnp.concatenate([(cells % depth).astype(BF), (cells // depth).astype(BF)], axis=1)
@@ -253,9 +250,9 @@
     *refs,
 ):
     if packed:
-        got_ref, weight_ref, self_ref, pair_ref, out_ref = refs
+        got_ref, list_ref, gap_ref, self_ref, pair_ref, out_ref = refs
         width = got_ref.shape[2]
-        slots = weight_ref.shape[1]
+        slots = list_ref.shape[1]
         capacity = slots // slab_count
         got = jnp.concatenate(
             [
@@ -279,9 +276,9 @@
             tiles.append(total)
         spots = jnp.concatenate(tiles, axis=1) - 1.0
     else:
-        got_ref, spot_ref, weight_ref, self_ref, pair_ref, out_ref = refs
+        got_ref, spot_ref, list_ref, gap_ref, self_ref, pair_ref, out_ref = refs
         width = got_ref.shape[2]
-        slots = weight_ref.shape[1]
+        slots = list_ref.shape[1]
         got = jnp.concatenate([got_ref[c] for c in range(3)], axis=1)
         spots = jnp.broadcast_to(spot_ref[...].astype(F32), (8, slots)) - 1.0
 
@@ -289,17 +286,14 @@
     spot_col = jnp.transpose(spots)[:, :1]
     land = jnp.where(iota((slots, slots), 0) == spot_row, 1.0, 0.0).astype(BF)
     reply = jnp.where(iota((slots, slots), 1) == spot_col, 1.0, 0.0).astype(BF)
+    chosen = dot_nn(reply, pair_weights(list_ref, gap_ref)).astype(BF)
     owned = dot_nn(land, got).astype(BF)
-    near = (dot_nn(weight_ref[0], owned) + dot_nn(weight_ref[1], owned)).astype(BF)
+    near = (dot_nn(chosen[:, :slots], owned) + dot_nn(chosen[:, slots:], owned)).astype(BF)
     coupling = jnp.concatenate([self_ref[...], pair_ref[...]], axis=0)
-    fixed = []
     for c in range(3):
-        cut = slice(c * width, (c + 1) * width)
-        both = jnp.concatenate([owned[:, cut], near[:, cut]], axis=1)
-        fixed.append(dot_nn(both, coupling).astype(BF))
-    replies = dot_nn(reply, jnp.concatenate(fixed, axis=1)).astype(BF)
-    for c in range(3):
-        cut = replies[:, c * width : (c + 1) * width]
+        span = slice(c * width, (c + 1) * width)
+        both = jnp.concatenate([got[:, span], near[:, span]], axis=1)
+        cut = dot_nn(both, coupling).astype(BF)
         if packed:
             out_ref[:, c * capacity : (c + 1) * capacity, :] = cut.reshape(
                 slab_count, capacity, width
@@ -488,11 +482,10 @@
     else:
         sample_out = [shape((3, slots, width), BF), shape((slab_count, width), BF)]
     sample_out += [shape((slots, 8), F32)] * 2 + [shape((slots, width), F32)] * 2
-    sample_out.append(shape((2, slots, slots), BF))
     results = pl.pallas_call(
         functools.partial(sample_kernel, slab_count, packed),
         out_shape=sample_out,
-        in_specs=[whole(pltpu.HBM)] * 9,
+        in_specs=[whole(pltpu.HBM)] * 7,
         out_specs=[whole()] * len(sample_out),
         scratch_shapes=[
             pltpu.SMEM((1,), jnp.int32),
@@ -500,11 +493,9 @@
             pltpu.VMEM((1, slots), jnp.int32),
             pltpu.VMEM((1, slots), jnp.int32),
             pltpu.VMEM((3, 1, slots), F32),
-            pltpu.VMEM((pair_list.shape[3], slots), jnp.int32),
-            pltpu.VMEM((pair_list.shape[3], slots), F32),
             pltpu.VMEM((slots, width), jnp.int32),
             pltpu.VMEM((19, rows, depth), F32),
-            pltpu.SemaphoreType.DMA((9,)),
+            pltpu.SemaphoreType.DMA((7,)),
         ],
         compiler_params=limits,
         name="sample",
@@ -517,14 +508,12 @@
                 marker_count.reshape(1, slots),
                 particle_id.reshape(1, slots),
                 particle_velocity.reshape(3, 1, slots),
-                jnp.transpose(pair_list.reshape(slots, -1)),
-                jnp.transpose(pair_gap.reshape(slots, -1)),
                 cells,
                 pops,
             )
         ],
     )
-    send, ordered, z_cells, y_cells, weights = results[-5:]
+    send, ordered, z_cells, y_cells = results[-4:]
 
     def exchange(value):
         return lax.all_to_all(value, "slab", split_axis=0, concat_axis=0, tiled=True)
@@ -551,13 +540,14 @@
     reply = pl.pallas_call(
         functools.partial(owner_kernel, slab_count, packed),
         out_shape=reply_shape,
-        in_specs=[whole()] * (len(arrived) + 3),
+        in_specs=[whole()] * (len(arrived) + 4),
         out_specs=whole(),
         compiler_params=limits,
         name="owner",
     )(
         *arrived,
-        weights,
+        jnp.transpose(pair_list.reshape(slots, -1)),
+        jnp.transpose(pair_gap.reshape(slots, -1)),
         self_coupling,
         pair_coupling,
     )

time: 47.8 us -> 46.1 us (0.964)
  Pallas kernels: 10.9 us -> 9.07 us
    pallas_call x1, Pallas kernels: 5.1 us -> 3.88 us  [per_device(): pl.pallas_call(functools.partial(sample_kernel, slab_count, packed), out_...]
    pallas_call x1, Pallas kernels: 3 us -> 2.03 us  [per_device(): pl.pallas_call(functools.partial(spread_kernel, slab_count, packed), out_...]
where the time goes in v6:
time: 46.1 us; the launch traced here: 45.8 us
  blocking collectives  24 us (52%)
  Pallas kernels  9.07 us (20%)
  starting transfers between devices  7.24 us (16%)
  waiting for transfers between devices  4 us (9%)
  between operations  1.36 us (3%)
    all_to_all x2, blocking collectives, exchange(): lax.all_to_all(value, 'slab', split_axis=0, concat_axis=0, tiled=True)  24 us
    ppermute x4, starting transfers between devices, swap(): return lax.ppermute(value, axis, pairs)  7.24 us
    ppermute x4, waiting for transfers between devices, swap(): return lax.ppermute(value, axis, pairs)  4 us
    pallas_call x1, Pallas kernels, per_device(): pl.pallas_call(functools.partial(sample_kernel, slab_count, packed), out_...  3.88 us
    pallas_call x1, Pallas kernels, per_device(): pl.pallas_call(functools.partial(spread_kernel, slab_count, packed), out_...  2.03 us
    pallas_call x1, Pallas kernels, per_device(): pl.pallas_call(functools.partial(owner_kernel, slab_count, packed), out_s...  1.31 us
    pallas_call x1, Pallas kernels, per_device(): pl.pallas_call(functools.partial(finish_kernel, slab_count, packed), out_...  1.02 us
  transfers between devices with their start and end apart: 4, of which 3 were waited for; matrix products, arithmetic and copies ran while one was open for 0% of the time, Pallas kernels for 2%

profile of v6, /device:TPU:1, one launch (start us, length us, event | category | flops | bytes accessed | tf_op | source)
XLA Modules:
  0.0 45.8 jit_solution(15278598313253970593)
XLA Ops:
  1.3 3.9 %sample.1 = (bf16[8,104,128]{2,1,0:T(8,128)(2,1)S(1)}, f32[256,8]{1,0:T(8,128)S(1)}, f32[256,8]{1,0:T(8,128)S(1)}, f32[256,128]{1,0:T(8,128)S(1)}, f32[256,128]{1,0:T(8,128)S(1)}) custom-call(s32[1]{0:T(128)} %bitcast.39.refs_0_, s32[8]{0:T(128)} %bitcast.50, s32[1,256]{1,0:T(1,128)} %bitcast.48, s32[1,256]{1,0:T(1,128)} %bitcast.49, f32[3,1,256]{2,1,0:T(1,128)} %bitcast.47, ...), custom_call_target="tpu_custom_call" | custom-call | tf_op jit(solution)/shard_map/sample/pallas_call | solution.py:485
  5.2 0.0 copy-start.1
  5.2 0.0 copy-start.2
  5.2 0.0 copy-start.3
  5.2 0.0 copy-start.4
  5.2 13.1 %all_to_all.10.refs_0_ = bf16[8,104,128]{2,1,0:T(8,128)(2,1)S(1)} all-to-all(bf16[8,104,128]{2,1,0:T(8,128)(2,1)S(1)} %get-tuple-element.12), channel_id=1, replica_groups=mesh['slab'=8,'sub'=4] {'slab'}, dimensions={0} | all-to-all | bytes 425984 | tf_op jit(solution)/shard_map/all_to_all | solution.py:519
  18.3 0.0 copy-done.1
  18.3 0.0 copy-done.2
  18.3 0.0 copy-done.3
  18.3 0.0 copy-done.4
  18.3 1.3 %owner.1 = bf16[8,96,128]{2,1,0:T(8,128)(2,1)S(1)} custom-call(bf16[8,104,128]{2,1,0:T(8,128)(2,1)S(1)} %all_to_all.10.refs_0_, s32[4,256]{1,0:T(4,128)S(1)} %bitcast.42, f32[4,256]{1,0:T(4,128)S(1)} %bitcast.43, bf16[128,128]{1,0:T(8,128)(2,1)S(1)} %copy-done.1, bf16[128,128]{1,0:T(8,128)(2,1)S(1)} %copy-done.2), custom_call_target="tpu_custom_call" | custom-call | tf_op jit(solution)/shard_map/owner/pallas_call | solution.py:540
  19.6 0.0 copy-start
  19.6 11.0 %all_to_all.11.back_ref = bf16[8,96,128]{2,1,0:T(8,128)(2,1)S(1)} all-to-all(bf16[8,96,128]{2,1,0:T(8,128)(2,1)S(1)} %owner.1), channel_id=1, replica_groups=mesh['slab'=8,'sub'=4] {'slab'}, dimensions={0} | all-to-all | bytes 393216 | tf_op jit(solution)/shard_map/all_to_all | solution.py:519
  30.6 0.0 copy-done
  30.6 2.0 %spread.1 = (f32[19,32,128]{2,1,0:T(8,128)S(1)}, f32[8,128]{1,0:T(8,128)S(1)}, f32[8,128]{1,0:T(8,128)S(1)}, bf16[5,32,128]{2,1,0:T(8,128)(2,1)S(1)}, bf16[5,32,128]{2,1,0:T(8,128)(2,1)S(1)}) custom-call(bf16[8,96,128]{2,1,0:T(8,128)(2,1)S(1)} %all_to_all.11.back_ref, f32[256,8]{1,0:T(8,128)S(1)} %get-tuple-element.13.sorted_ref, ...), custom_call_target="tpu_custom_call" | custom-call | tf_op jit(solution)/shard_map/spread/pallas_call | solution.py:556
  32.6 2.9 %collective-permute-start = (bf16[5,32,128]{2,1,0:T(8,128)(2,1)S(1)}, bf16[5,32,128]{2,1,0:T(8,128)(2,1)S(1)}, u32[]{:S(2)}, u32[]{:S(2)}) collective-permute-start(bf16[5,32,128]{2,1,0:T(8,128)(2,1)S(1)} %get-tuple-element.18), channel_id=1, source_target_pairs={{0,28},{4,8},{8,4},{12,16},{16,12},{20,24},{24,20},{28,0},{1,29},{... | collective-permute-start | bytes 122888 | tf_op jit(solution)/shard_map/ppermute | solution.py:451
  35.5 0.0 collective-permute-start.1
  35.5 2.8 %collective-permute-done.second_ref = bf16[5,32,128]{2,1,0:T(8,128)(2,1)S(1)} collective-permute-done((bf16[5,32,128]{2,1,0:T(8,128)(2,1)S(1)}, bf16[5,32,128]{2,1,0:T(8,128)(2,1)S(1)}, u32[]{:S(2)}, u32[]{:S(2)}) %collective-permute-start) | collective-permute-done | bytes 40992 | tf_op jit(solution)/shard_map/ppermute | solution.py:451
  38.3 0.4 collective-permute-done.1.first_ref
  38.7 3.2 %collective-permute-start.2 = (f32[5,128]{1,0:T(8,128)S(1)}, f32[5,128]{1,0:T(8,128)S(1)}, u32[]{:S(2)}, u32[]{:S(2)}) collective-permute-start(f32[5,128]{1,0:T(8,128)S(1)} %get-tuple-element.29), channel_id=1, source_target_pairs={{0,1},{1,0},{2,3},{3,2},{4,5},{5,4},{6,7},{7,6},{8,9},{9,8},{10,11... | collective-permute-start | bytes 7688 | tf_op jit(solution)/shard_map/ppermute | solution.py:451
  41.9 1.2 %collective-permute-start.3 = (f32[5,128]{1,0:T(8,128)S(1)}, f32[5,128]{1,0:T(8,128)S(1)}, u32[]{:S(2)}, u32[]{:S(2)}) collective-permute-start(f32[5,128]{1,0:T(8,128)S(1)} %get-tuple-element.28), channel_id=1, source_target_pairs={{0,3},{1,2},{2,1},{3,0},{4,7},{5,6},{6,5},{7,4},{8,11},{9,10},{10,... | collective-permute-start | bytes 7688 | tf_op jit(solution)/shard_map/ppermute | solution.py:451
  43.1 1.0 %finish.1 = bf16[3,256,128]{2,1,0:T(8,128)(2,1)} custom-call(bf16[8,96,128]{2,1,0:T(8,128)(2,1)S(1)} %all_to_all.11.back_ref, f32[256,8]{1,0:T(8,128)S(1)} %get-tuple-element.13.sorted_ref, f32[256,8]{1,0:T(8,128)S(1)} %get-tuple-element.21.send_ref), custom_call_target="tpu_custom_call" | custom-call | flops 50000000 | bytes 400000 | tf_op jit(solution)/shard_map/finish/pallas_call | solution.py:570
  44.1 0.0 collective-permute-done.2.one_ref
  44.1 0.8 %collective-permute-done.3.two_ref = f32[5,128]{1,0:T(8,128)S(1)} collective-permute-done((f32[5,128]{1,0:T(8,128)S(1)}, f32[5,128]{1,0:T(8,128)S(1)}, u32[]{:S(2)}, u32[]{:S(2)}) %collective-permute-start.3) | collective-permute-done | bytes 2592 | tf_op jit(solution)/shard_map/ppermute | solution.py:451
  44.9 0.8 %stream.1 = f32[19,32,128]{2,1,0:T(8,128)} custom-call(f32[19,32,128]{2,1,0:T(8,128)S(1)} %get-tuple-element.16.collided_ref, f32[5,128]{1,0:T(8,128)S(1)} %collective-permute-done.2.one_ref, f32[5,128]{1,0:T(8,128)S(1)} %collective-permute-done.3.two_ref, bf16[5,32,128]{2,1,0:T(8,128)(2,1)S(1)} %collective-permute-done.1.first_ref, ...), custom_call_target="tpu_custom_call" | custom-call | tf_op jit(solution)/shard_map/stream/pallas_call | solution.py:594
  (4 shorter events, 0.0 us)
Async XLA Ops:
  5.2 13.1 %copy-start.1 = (bf16[128,128]{1,0:T(8,128)(2,1)S(1)}, bf16[128,128]{1,0:T(8,128)(2,1)}, u32[]{:S(2)}) copy-start(bf16[128,128]{1,0:T(8,128)(2,1)} %refs_3_.1) | copy-start | bytes 98308
  5.2 13.1 %copy-start.2 = (bf16[128,128]{1,0:T(8,128)(2,1)S(1)}, bf16[128,128]{1,0:T(8,128)(2,1)}, u32[]{:S(2)}) copy-start(bf16[128,128]{1,0:T(8,128)(2,1)} %refs_4_.1) | copy-start | bytes 98308
  5.2 13.1 %copy-start.3 = (s32[1,1,256,4]{2,3,1,0:T(4,128)S(1)}, s32[1,1,256,4]{2,3,1,0:T(4,128)}, u32[]{:S(2)}) copy-start(s32[1,1,256,4]{2,3,1,0:T(4,128)} %param.18) | copy-start | bytes 12292
  5.2 13.1 %copy-start.4 = (f32[1,1,256,4]{2,3,1,0:T(4,128)S(1)}, f32[1,1,256,4]{2,3,1,0:T(4,128)}, u32[]{:S(2)}) copy-start(f32[1,1,256,4]{2,3,1,0:T(4,128)} %param.19) | copy-start | bytes 12292
  19.6 11.0 %copy-start = (f32[19,1,32,128]{3,2,1,0:T(8,128)S(1)}, f32[19,1,32,128]{3,2,1,0:T(8,128)}, u32[]{:S(2)}) copy-start(f32[19,1,32,128]{3,2,1,0:T(8,128)} %param.11) | copy-start | bytes 933892
  32.6 5.6 %collective-permute-start = (bf16[5,32,128]{2,1,0:T(8,128)(2,1)S(1)}, bf16[5,32,128]{2,1,0:T(8,128)(2,1)S(1)}, u32[]{:S(2)}, u32[]{:S(2)}) collective-permute-start(bf16[5,32,128]{2,1,0:T(8,128)(2,1)S(1)} %get-tuple-element.18), channel_id=1, source_target_pairs={{0,28},{4,8},{8,4},{12,16},{16,12},{20,24},{24,20},{28,0},{1,29},{... | collective-permute-start | bytes 122888 | tf_op jit(solution)/shard_map/ppermute | solution.py:451
  35.5 3.2 %collective-permute-start.1 = (bf16[5,32,128]{2,1,0:T(8,128)(2,1)S(1)}, bf16[5,32,128]{2,1,0:T(8,128)(2,1)S(1)}, u32[]{:S(2)}, u32[]{:S(2)}) collective-permute-start(bf16[5,32,128]{2,1,0:T(8,128)(2,1)S(1)} %get-tuple-element.19), channel_id=1, source_target_pairs={{0,4},{4,0},{8,12},{12,8},{16,20},{20,16},{24,28},{28,24},{1,5},{5... | collective-permute-start | bytes 122888 | tf_op jit(solution)/shard_map/ppermute | solution.py:451
  38.7 5.4 %collective-permute-start.2 = (f32[5,128]{1,0:T(8,128)S(1)}, f32[5,128]{1,0:T(8,128)S(1)}, u32[]{:S(2)}, u32[]{:S(2)}) collective-permute-start(f32[5,128]{1,0:T(8,128)S(1)} %get-tuple-element.29), channel_id=1, source_target_pairs={{0,1},{1,0},{2,3},{3,2},{4,5},{5,4},{6,7},{7,6},{8,9},{9,8},{10,11... | collective-permute-start | bytes 7688 | tf_op jit(solution)/shard_map/ppermute | solution.py:451
  41.9 3.0 %collective-permute-start.3 = (f32[5,128]{1,0:T(8,128)S(1)}, f32[5,128]{1,0:T(8,128)S(1)}, u32[]{:S(2)}, u32[]{:S(2)}) collective-permute-start(f32[5,128]{1,0:T(8,128)S(1)} %get-tuple-element.28), channel_id=1, source_target_pairs={{0,3},{1,2},{2,1},{3,0},{4,7},{5,6},{6,5},{7,4},{8,11},{9,10},{10,... | collective-permute-start | bytes 7688 | tf_op jit(solution)/shard_map/ppermute | solution.py:451

commit v7 on v6

--- a/solution.py
+++ b/solution.py
@@ -117,20 +117,13 @@
 
 def pair_weights(list_ref, gap_ref):
     pairs, slots = list_ref.shape
-    filler = jnp.zeros((-2 * pairs % 8, slots), F32)
-    turned = jnp.transpose(
-        jnp.concatenate(
-            [list_ref[...].astype(F32), 1.0 / gap_ref[...], filler][: 2 + (2 * pairs % 8 > 0)],
-            axis=0,
-        )
-    )
-    column = iota((slots, slots), 1)
+    row = iota((slots, slots), 0, jnp.int32)
+    inverse = 1.0 / gap_ref[...]
     weight = jnp.zeros((slots, slots), F32)
     for k in range(pairs):
-        inverse = turned[:, pairs + k : pairs + k + 1]
-        weight = weight + jnp.where(column == turned[:, k : k + 1], inverse, 0.0)
+        weight = weight + jnp.where(row == list_ref[k : k + 1, :], inverse[k : k + 1], 0.0)
     high = weight.astype(BF)
-    return jnp.concatenate([high, (weight - high.astype(F32)).astype(BF)], axis=1)
+    return high, (weight - high.astype(F32)).astype(BF)
 
 
 def sample_kernel(slab_count, packed, *refs):
@@ -162,7 +155,9 @@
     def look_up(b, owner):
         return jnp.where(block == b, table_ref[b], owner)
 
-    owner = lax.fori_loop(0, slab_count, look_up, jnp.zeros((1, slots), jnp.int32))
+    owner = lax.fori_loop(
+        0, slab_count, look_up, jnp.zeros((1, slots), jnp.int32), unroll=slab_count <= 16
+    )
     owner = jnp.where(alive, owner, -1)
     owner_f = owner.astype(F32)
     chosen = jnp.where(iota((slab_count, slots), 0) == owner_f, 1.0, 0.0)
@@ -286,9 +281,9 @@
     spot_col = jnp.transpose(spots)[:, :1]
     land = jnp.where(iota((slots, slots), 0) == spot_row, 1.0, 0.0).astype(BF)
     reply = jnp.where(iota((slots, slots), 1) == spot_col, 1.0, 0.0).astype(BF)
-    chosen = dot_nn(reply, pair_weights(list_ref, gap_ref)).astype(BF)
+    chosen = [dot_nt(reply, part).astype(BF) for part in pair_weights(list_ref, gap_ref)]
     owned = dot_nn(land, got).astype(BF)
-    near = (dot_nn(chosen[:, :slots], owned) + dot_nn(chosen[:, slots:], owned)).astype(BF)
+    near = (dot_nn(chosen[0], owned) + dot_nn(chosen[1], owned)).astype(BF)
     coupling = jnp.concatenate([self_ref[...], pair_ref[...]], axis=0)
     for c in range(3):
         span = slice(c * width, (c + 1) * width)
@@ -405,7 +400,7 @@
 
 
 def stream_kernel(
-    sub_total, collided_ref, one_ref, two_ref, first_ref, second_ref, read_ref
+    sub_total, collided_ref, one_ref, two_ref, first_ref, second_ref, read_ref, out_ref, sems
 ):
     rows, depth = collided_ref.shape[1:]
     row = iota((rows, depth), 0, jnp.int32)
@@ -416,6 +411,7 @@
     high = jnp.where(sub_even, one_ref[...], two_ref[...])
     low_wall = jnp.where(place == 0, 1, 0)
     high_wall = jnp.where(place == sub_total - 1, 1, 0)
+    copies = []
     for number in range(19):
         step_x, step_y, step_z = lattice_dirs[number]
         if step_x == 1:
@@ -438,7 +434,13 @@
             wall = low_wall if step_y == 1 else high_wall
             at_wall = (row == edge_row) & (wall == 1)
             moved = jnp.where(at_wall, collided_ref[opposite_of[number]], moved)
-        read_ref[number] = moved
+        out_ref[number] = moved
+        copies.append(
+            pltpu.make_async_copy(out_ref.at[number], read_ref.at[number], sems.at[number])
+        )
+        copies[-1].start()
+    for copy in copies:
+        copy.wait()
 
 
 def whole(memory=pltpu.VMEM):
@@ -595,7 +597,8 @@
         functools.partial(stream_kernel, lax.axis_size("sub")),
         out_shape=shape((19, rows, depth), F32),
         in_specs=[whole()] * 5,
-        out_specs=whole(),
+        out_specs=whole(pltpu.HBM),
+        scratch_shapes=[pltpu.VMEM((19, rows, depth), F32), pltpu.SemaphoreType.DMA((19,))],
         compiler_params=limits,
         name="stream",
     )(collided, *low_high, first, second)

time: 46.1 us -> 45.8 us (level)
  no operation moved by 1% of the time
where the time goes in v7:
time: 45.8 us; the launch traced here: 45.5 us
  blocking collectives  24 us (52%)
  Pallas kernels  8.82 us (19%)
  starting transfers between devices  7.24 us (16%)
  waiting for transfers between devices  4 us (9%)
  between operations  1.36 us (3%)
    all_to_all x2, blocking collectives, exchange(): lax.all_to_all(value, 'slab', split_axis=0, concat_axis=0, tiled=True)  24 us
    ppermute x4, starting transfers between devices, swap(): return lax.ppermute(value, axis, pairs)  7.24 us
    ppermute x4, waiting for transfers between devices, swap(): return lax.ppermute(value, axis, pairs)  4 us
    pallas_call x1, Pallas kernels, per_device(): pl.pallas_call(functools.partial(sample_kernel, slab_count, packed), out_...  3.83 us
    pallas_call x1, Pallas kernels, per_device(): pl.pallas_call(functools.partial(spread_kernel, slab_count, packed), out_...  2.03 us
    pallas_call x1, Pallas kernels, per_device(): pl.pallas_call(functools.partial(owner_kernel, slab_count, packed), out_s...  1.03 us
    pallas_call x1, Pallas kernels, per_device(): pl.pallas_call(functools.partial(finish_kernel, slab_count, packed), out_...  1.02 us
  transfers between devices with their start and end apart: 4, of which 3 were waited for; matrix products, arithmetic and copies ran while one was open for 0% of the time, Pallas kernels for 2%

profile of v7, /device:TPU:1, one launch (start us, length us, event | category | flops | bytes accessed | tf_op | source)
XLA Modules:
  0.0 45.5 jit_solution(843023254325884729)
XLA Ops:
  1.3 3.8 %sample.1 = (bf16[8,104,128]{2,1,0:T(8,128)(2,1)S(1)}, f32[256,8]{1,0:T(8,128)S(1)}, f32[256,8]{1,0:T(8,128)S(1)}, f32[256,128]{1,0:T(8,128)S(1)}, f32[256,128]{1,0:T(8,128)S(1)}) custom-call(s32[1]{0:T(128)} %bitcast.39.refs_0_, s32[8]{0:T(128)} %bitcast.50, s32[1,256]{1,0:T(1,128)} %bitcast.48, s32[1,256]{1,0:T(1,128)} %bitcast.49, f32[3,1,256]{2,1,0:T(1,128)} %bitcast.47, ...), custom_call_target="tpu_custom_call" | custom-call | tf_op jit(solution)/shard_map/sample/pallas_call | solution.py:487
  5.1 0.0 copy-start.1
  5.1 0.0 copy-start.2
  5.1 0.0 copy-start.3
  5.2 0.0 copy-start.4
  5.2 13.1 %all_to_all.10.refs_0_ = bf16[8,104,128]{2,1,0:T(8,128)(2,1)S(1)} all-to-all(bf16[8,104,128]{2,1,0:T(8,128)(2,1)S(1)} %get-tuple-element.12), channel_id=1, replica_groups=mesh['slab'=8,'sub'=4] {'slab'}, dimensions={0} | all-to-all | bytes 425984 | tf_op jit(solution)/shard_map/all_to_all | solution.py:521
  18.2 0.0 copy-done.1
  18.2 0.0 copy-done.2
  18.2 0.0 copy-done.3
  18.2 0.0 copy-done.4
  18.2 1.0 %owner.1 = bf16[8,96,128]{2,1,0:T(8,128)(2,1)S(1)} custom-call(bf16[8,104,128]{2,1,0:T(8,128)(2,1)S(1)} %all_to_all.10.refs_0_, s32[4,256]{1,0:T(4,128)S(1)} %bitcast.42, f32[4,256]{1,0:T(4,128)S(1)} %bitcast.43, bf16[128,128]{1,0:T(8,128)(2,1)S(1)} %copy-done.1, bf16[128,128]{1,0:T(8,128)(2,1)S(1)} %copy-done.2), custom_call_target="tpu_custom_call" | custom-call | tf_op jit(solution)/shard_map/owner/pallas_call | solution.py:542
  19.3 0.0 copy-start
  19.3 11.0 %all_to_all.11.back_ref = bf16[8,96,128]{2,1,0:T(8,128)(2,1)S(1)} all-to-all(bf16[8,96,128]{2,1,0:T(8,128)(2,1)S(1)} %owner.1), channel_id=1, replica_groups=mesh['slab'=8,'sub'=4] {'slab'}, dimensions={0} | all-to-all | bytes 393216 | tf_op jit(solution)/shard_map/all_to_all | solution.py:521
  30.3 0.0 copy-done
  30.3 2.0 %spread.1 = (f32[19,32,128]{2,1,0:T(8,128)S(1)}, f32[8,128]{1,0:T(8,128)S(1)}, f32[8,128]{1,0:T(8,128)S(1)}, bf16[5,32,128]{2,1,0:T(8,128)(2,1)S(1)}, bf16[5,32,128]{2,1,0:T(8,128)(2,1)S(1)}) custom-call(bf16[8,96,128]{2,1,0:T(8,128)(2,1)S(1)} %all_to_all.11.back_ref, f32[256,8]{1,0:T(8,128)S(1)} %get-tuple-element.13.sorted_ref, ...), custom_call_target="tpu_custom_call" | custom-call | tf_op jit(solution)/shard_map/spread/pallas_call | solution.py:558
  32.3 2.9 %collective-permute-start = (bf16[5,32,128]{2,1,0:T(8,128)(2,1)S(1)}, bf16[5,32,128]{2,1,0:T(8,128)(2,1)S(1)}, u32[]{:S(2)}, u32[]{:S(2)}) collective-permute-start(bf16[5,32,128]{2,1,0:T(8,128)(2,1)S(1)} %get-tuple-element.18), channel_id=1, source_target_pairs={{0,28},{4,8},{8,4},{12,16},{16,12},{20,24},{24,20},{28,0},{1,29},{... | collective-permute-start | bytes 122888 | tf_op jit(solution)/shard_map/ppermute | solution.py:453
  35.2 0.0 collective-permute-start.1
  35.2 2.8 %collective-permute-done.second_ref = bf16[5,32,128]{2,1,0:T(8,128)(2,1)S(1)} collective-permute-done((bf16[5,32,128]{2,1,0:T(8,128)(2,1)S(1)}, bf16[5,32,128]{2,1,0:T(8,128)(2,1)S(1)}, u32[]{:S(2)}, u32[]{:S(2)}) %collective-permute-start) | collective-permute-done | bytes 40992 | tf_op jit(solution)/shard_map/ppermute | solution.py:453
  38.0 0.4 collective-permute-done.1.first_ref
  38.4 3.2 %collective-permute-start.2 = (f32[5,128]{1,0:T(8,128)S(1)}, f32[5,128]{1,0:T(8,128)S(1)}, u32[]{:S(2)}, u32[]{:S(2)}) collective-permute-start(f32[5,128]{1,0:T(8,128)S(1)} %get-tuple-element.29), channel_id=1, source_target_pairs={{0,1},{1,0},{2,3},{3,2},{4,5},{5,4},{6,7},{7,6},{8,9},{9,8},{10,11... | collective-permute-start | bytes 7688 | tf_op jit(solution)/shard_map/ppermute | solution.py:453
  41.6 1.2 %collective-permute-start.3 = (f32[5,128]{1,0:T(8,128)S(1)}, f32[5,128]{1,0:T(8,128)S(1)}, u32[]{:S(2)}, u32[]{:S(2)}) collective-permute-start(f32[5,128]{1,0:T(8,128)S(1)} %get-tuple-element.28), channel_id=1, source_target_pairs={{0,3},{1,2},{2,1},{3,0},{4,7},{5,6},{6,5},{7,4},{8,11},{9,10},{10,... | collective-permute-start | bytes 7688 | tf_op jit(solution)/shard_map/ppermute | solution.py:453
  42.7 1.0 %finish.1 = bf16[3,256,128]{2,1,0:T(8,128)(2,1)} custom-call(bf16[8,96,128]{2,1,0:T(8,128)(2,1)S(1)} %all_to_all.11.back_ref, f32[256,8]{1,0:T(8,128)S(1)} %get-tuple-element.13.sorted_ref, f32[256,8]{1,0:T(8,128)S(1)} %get-tuple-element.21.send_ref), custom_call_target="tpu_custom_call" | custom-call | flops 50000000 | bytes 400000 | tf_op jit(solution)/shard_map/finish/pallas_call | solution.py:572
  43.8 0.0 collective-permute-done.2.one_ref
  43.8 0.8 %collective-permute-done.3.two_ref = f32[5,128]{1,0:T(8,128)S(1)} collective-permute-done((f32[5,128]{1,0:T(8,128)S(1)}, f32[5,128]{1,0:T(8,128)S(1)}, u32[]{:S(2)}, u32[]{:S(2)}) %collective-permute-start.3) | collective-permute-done | bytes 2592 | tf_op jit(solution)/shard_map/ppermute | solution.py:453
  44.6 0.9 %stream.1 = f32[19,32,128]{2,1,0:T(8,128)} custom-call(f32[19,32,128]{2,1,0:T(8,128)S(1)} %get-tuple-element.16.collided_ref, f32[5,128]{1,0:T(8,128)S(1)} %collective-permute-done.2.one_ref, f32[5,128]{1,0:T(8,128)S(1)} %collective-permute-done.3.two_ref, bf16[5,32,128]{2,1,0:T(8,128)(2,1)S(1)} %collective-permute-done.1.first_ref, ...), custom_call_target="tpu_custom_call" | custom-call | tf_op jit(solution)/shard_map/stream/pallas_call | solution.py:596
  (4 shorter events, 0.0 us)
Async XLA Ops:
  5.1 13.1 %copy-start.1 = (bf16[128,128]{1,0:T(8,128)(2,1)S(1)}, bf16[128,128]{1,0:T(8,128)(2,1)}, u32[]{:S(2)}) copy-start(bf16[128,128]{1,0:T(8,128)(2,1)} %refs_3_.1) | copy-start | bytes 98308
  5.1 13.1 %copy-start.2 = (bf16[128,128]{1,0:T(8,128)(2,1)S(1)}, bf16[128,128]{1,0:T(8,128)(2,1)}, u32[]{:S(2)}) copy-start(bf16[128,128]{1,0:T(8,128)(2,1)} %refs_4_.1) | copy-start | bytes 98308
  5.1 13.1 %copy-start.3 = (s32[1,1,256,4]{2,3,1,0:T(4,128)S(1)}, s32[1,1,256,4]{2,3,1,0:T(4,128)}, u32[]{:S(2)}) copy-start(s32[1,1,256,4]{2,3,1,0:T(4,128)} %param.18) | copy-start | bytes 12292
  5.2 13.1 %copy-start.4 = (f32[1,1,256,4]{2,3,1,0:T(4,128)S(1)}, f32[1,1,256,4]{2,3,1,0:T(4,128)}, u32[]{:S(2)}) copy-start(f32[1,1,256,4]{2,3,1,0:T(4,128)} %param.19) | copy-start | bytes 12292
  19.3 11.0 %copy-start = (f32[19,1,32,128]{3,2,1,0:T(8,128)S(1)}, f32[19,1,32,128]{3,2,1,0:T(8,128)}, u32[]{:S(2)}) copy-start(f32[19,1,32,128]{3,2,1,0:T(8,128)} %param.11) | copy-start | bytes 933892
  32.3 5.6 %collective-permute-start = (bf16[5,32,128]{2,1,0:T(8,128)(2,1)S(1)}, bf16[5,32,128]{2,1,0:T(8,128)(2,1)S(1)}, u32[]{:S(2)}, u32[]{:S(2)}) collective-permute-start(bf16[5,32,128]{2,1,0:T(8,128)(2,1)S(1)} %get-tuple-element.18), channel_id=1, source_target_pairs={{0,28},{4,8},{8,4},{12,16},{16,12},{20,24},{24,20},{28,0},{1,29},{... | collective-permute-start | bytes 122888 | tf_op jit(solution)/shard_map/ppermute | solution.py:453
  35.2 3.2 %collective-permute-start.1 = (bf16[5,32,128]{2,1,0:T(8,128)(2,1)S(1)}, bf16[5,32,128]{2,1,0:T(8,128)(2,1)S(1)}, u32[]{:S(2)}, u32[]{:S(2)}) collective-permute-start(bf16[5,32,128]{2,1,0:T(8,128)(2,1)S(1)} %get-tuple-element.19), channel_id=1, source_target_pairs={{0,4},{4,0},{8,12},{12,8},{16,20},{20,16},{24,28},{28,24},{1,5},{5... | collective-permute-start | bytes 122888 | tf_op jit(solution)/shard_map/ppermute | solution.py:453
  38.4 5.4 %collective-permute-start.2 = (f32[5,128]{1,0:T(8,128)S(1)}, f32[5,128]{1,0:T(8,128)S(1)}, u32[]{:S(2)}, u32[]{:S(2)}) collective-permute-start(f32[5,128]{1,0:T(8,128)S(1)} %get-tuple-element.29), channel_id=1, source_target_pairs={{0,1},{1,0},{2,3},{3,2},{4,5},{5,4},{6,7},{7,6},{8,9},{9,8},{10,11... | collective-permute-start | bytes 7688 | tf_op jit(solution)/shard_map/ppermute | solution.py:453
  41.6 3.0 %collective-permute-start.3 = (f32[5,128]{1,0:T(8,128)S(1)}, f32[5,128]{1,0:T(8,128)S(1)}, u32[]{:S(2)}, u32[]{:S(2)}) collective-permute-start(f32[5,128]{1,0:T(8,128)S(1)} %get-tuple-element.28), channel_id=1, source_target_pairs={{0,3},{1,2},{2,1},{3,0},{4,7},{5,6},{6,5},{7,4},{8,11},{9,10},{10,... | collective-permute-start | bytes 7688 | tf_op jit(solution)/shard_map/ppermute | solution.py:453

commit v8 on v7

--- a/solution.py
+++ b/solution.py
@@ -105,16 +105,6 @@
     return blocks[0]
 
 
-def pieces_of(value):
-    parts = []
-    for step in range(3):
-        part = value.astype(BF)
-        parts.append(part)
-        if step < 2:
-            value = value - part.astype(F32)
-    return parts
-
-
 def pair_weights(list_ref, gap_ref):
     pairs, slots = list_ref.shape
     row = iota((slots, slots), 0, jnp.int32)
@@ -179,23 +169,19 @@
     else:
         spot_ref[...] = dot_nt((chosen * (spot + 1.0)).astype(BF), where_to).astype(BF)
 
-    count = marker_count_ref[...].astype(F32)
-    pieces = pieces_of(jnp.concatenate([velocity_ref[c] for c in range(3)], axis=0))
+    count = jnp.where(alive, marker_count_ref[...], 0).astype(F32)
     stack = jnp.concatenate(
-        [piece.astype(F32) for piece in pieces] + [count, send_row, jnp.zeros((5, slots), F32)],
-        axis=0,
+        [velocity_ref[c] for c in range(3)] + [count, send_row, jnp.zeros((3, slots), F32)], axis=0
     )
-    turned = jnp.transpose(stack)
-    send_ref[...] = turned[:, 8:16]
-    arranged = dot_nn(place, turned.astype(BF))
-    velocity = (arranged[:, 0:3] + arranged[:, 3:6]) + arranged[:, 6:9]
-    sorted_ref[...] = arranged[:, 8:16]
+    own = jnp.transpose(stack)
+    send_ref[...] = own
+    sorted_ref[...] = dot_nn(place, own.astype(BF))
 
     for copy in copies[5:]:
         copy.wait()
     cells = cell_ref[...]
-    parted = jnp.concatenate([(cells % depth).astype(BF), (cells // depth).astype(BF)], axis=1)
-    moved = dot_nn(place, parted)
+    z_all, y_all = (cells % depth).astype(F32), (cells // depth).astype(F32)
+    moved = dot_nn(place, jnp.concatenate([z_all, y_all], axis=1).astype(BF))
     z_ref[...] = moved[:, :width]
     y_ref[...] = moved[:, width:]
 
@@ -205,11 +191,12 @@
     low = (flow - high.astype(F32)).astype(BF)
     flow_pair = jnp.concatenate([high, low], axis=1)
 
+    slips = []
     for base in range(0, slots, 16):
         found_rows = []
         for eight in range(base, base + 16, 8):
-            z_rows = z_ref[eight : eight + 8, :]
-            y_rows = y_ref[eight : eight + 8, :]
+            z_rows = z_all[eight : eight + 8]
+            y_rows = y_all[eight : eight + 8]
             parts = [[], [], []]
             for first in range(0, 8, 2):
                 picks = jnp.concatenate(
@@ -228,15 +215,22 @@
                     for c in range(3):
                         parts[c].append(found[c])
             found_rows.append([fold_rows(parts[c]) for c in range(3)])
-        live = iota((16, width), 1) < arranged[base : base + 16, 9:10]
+        live = iota((16, width), 1) < own[base : base + 16, 3:4]
+        row = []
         for c in range(3):
             sampled = jnp.concatenate([found_rows[0][c], found_rows[1][c]], axis=0)
-            slip = jnp.where(live, velocity[base : base + 16, c : c + 1] - sampled, 0.0)
-            if packed:
-                at = c * capacity + base % capacity
-                slip_ref[base // capacity, at : at + 16, :] = slip.astype(BF)
-            else:
-                slip_ref[c, base : base + 16, :] = slip.astype(BF)
+            slip = jnp.where(live, own[base : base + 16, c : c + 1] - sampled, 0.0)
+            row.append(slip.astype(BF))
+        slips.append(jnp.concatenate(row, axis=1))
+    sent = dot_nn(place, jnp.concatenate(slips, axis=0)).astype(BF)
+    for c in range(3):
+        cut = sent[:, c * width : (c + 1) * width]
+        if packed:
+            slip_ref[:, c * capacity : (c + 1) * capacity, :] = cut.reshape(
+                slab_count, capacity, width
+            )
+        else:
+            slip_ref[c] = cut
 
 
 def owner_kernel(
@@ -308,14 +302,14 @@
         ]
     else:
         parts = [back_ref[c, base : base + count, :] for c in range(3)]
-    live = iota(parts[0].shape, 1) < sorted_ref[base : base + count, 1:2]
+    live = iota(parts[0].shape, 1) < sorted_ref[base : base + count, 3:4]
     return [jnp.where(live, part.astype(F32), 0.0) for part in parts]
 
 
 def finish_kernel(slab_count, packed, back_ref, sorted_ref, send_ref, out_ref):
     slots = sorted_ref.shape[0]
     masked = returned_rows(slab_count, packed, back_ref, sorted_ref, 0, slots)
-    fetch = jnp.where(iota((slots, slots), 1) == send_ref[:, 2:3], 1.0, 0.0).astype(BF)
+    fetch = jnp.where(iota((slots, slots), 1) == send_ref[:, 4:5], 1.0, 0.0).astype(BF)
     for c in range(3):
         out_ref[c] = dot_nn(fetch, masked[c].astype(BF)).astype(BF)
 
@@ -400,7 +394,7 @@
 
 
 def stream_kernel(
-    sub_total, collided_ref, one_ref, two_ref, first_ref, second_ref, read_ref, out_ref, sems
+    sub_total, collided_ref, one_ref, two_ref, first_ref, second_ref, read_ref
 ):
     rows, depth = collided_ref.shape[1:]
     row = iota((rows, depth), 0, jnp.int32)
@@ -411,7 +405,6 @@
     high = jnp.where(sub_even, one_ref[...], two_ref[...])
     low_wall = jnp.where(place == 0, 1, 0)
     high_wall = jnp.where(place == sub_total - 1, 1, 0)
-    copies = []
     for number in range(19):
         step_x, step_y, step_z = lattice_dirs[number]
         if step_x == 1:
@@ -434,13 +427,7 @@
             wall = low_wall if step_y == 1 else high_wall
             at_wall = (row == edge_row) & (wall == 1)
             moved = jnp.where(at_wall, collided_ref[opposite_of[number]], moved)
-        out_ref[number] = moved
-        copies.append(
-            pltpu.make_async_copy(out_ref.at[number], read_ref.at[number], sems.at[number])
-        )
-        copies[-1].start()
-    for copy in copies:
-        copy.wait()
+        read_ref[number] = moved
 
 
 def whole(memory=pltpu.VMEM):
@@ -597,8 +584,7 @@
         functools.partial(stream_kernel, lax.axis_size("sub")),
         out_shape=shape((19, rows, depth), F32),
         in_specs=[whole()] * 5,
-        out_specs=whole(pltpu.HBM),
-        scratch_shapes=[pltpu.VMEM((19, rows, depth), F32), pltpu.SemaphoreType.DMA((19,))],
+        out_specs=whole(),
         compiler_params=limits,
         name="stream",
     )(collided, *low_high, first, second)

time: 45.8 us -> 45.6 us (level)
  no operation moved by 1% of the time
where the time goes in v8:
time: 45.6 us; the launch traced here: 45.3 us
  blocking collectives  24 us (53%)
  Pallas kernels  8.58 us (19%)
  starting transfers between devices  7.24 us (16%)
  waiting for transfers between devices  4 us (9%)
  between operations  1.36 us (3%)
    all_to_all x2, blocking collectives, exchange(): lax.all_to_all(value, 'slab', split_axis=0, concat_axis=0, tiled=True)  24 us
    ppermute x4, starting transfers between devices, swap(): return lax.ppermute(value, axis, pairs)  7.24 us
    ppermute x4, waiting for transfers between devices, swap(): return lax.ppermute(value, axis, pairs)  4 us
    pallas_call x1, Pallas kernels, per_device(): pl.pallas_call(functools.partial(sample_kernel, slab_count, packed), out_...  3.68 us
    pallas_call x1, Pallas kernels, per_device(): pl.pallas_call(functools.partial(spread_kernel, slab_count, packed), out_...  2.03 us
    pallas_call x1, Pallas kernels, per_device(): pl.pallas_call(functools.partial(finish_kernel, slab_count, packed), out_...  1.02 us
    pallas_call x1, Pallas kernels, per_device(): pl.pallas_call(functools.partial(owner_kernel, slab_count, packed), out_s...  1.02 us
  transfers between devices with their start and end apart: 4, of which 3 were waited for; matrix products, arithmetic and copies ran while one was open for 0% of the time, Pallas kernels for 2%

profile of v8, /device:TPU:1, one launch (start us, length us, event | category | flops | bytes accessed | tf_op | source)
XLA Modules:
  0.0 45.3 jit_solution(14190959632128929489)
XLA Ops:
  1.3 3.7 %sample.1 = (bf16[8,104,128]{2,1,0:T(8,128)(2,1)S(1)}, f32[256,8]{1,0:T(8,128)S(1)}, f32[256,8]{1,0:T(8,128)S(1)}, f32[256,128]{1,0:T(8,128)S(1)}, f32[256,128]{1,0:T(8,128)S(1)}) custom-call(s32[1]{0:T(128)} %bitcast.39.refs_0_, s32[8]{0:T(128)} %bitcast.50, s32[1,256]{1,0:T(1,128)} %bitcast.48, s32[1,256]{1,0:T(1,128)} %bitcast.49, f32[3,1,256]{2,1,0:T(1,128)} %bitcast.47, ...), custom_call_target="tpu_custom_call" | custom-call | tf_op jit(solution)/shard_map/sample/pallas_call | solution.py:474
  5.0 0.0 copy-start.1
  5.0 0.0 copy-start.2
  5.0 0.0 copy-start.3
  5.0 0.0 copy-start.4
  5.0 13.1 %all_to_all.10.refs_0_ = bf16[8,104,128]{2,1,0:T(8,128)(2,1)S(1)} all-to-all(bf16[8,104,128]{2,1,0:T(8,128)(2,1)S(1)} %get-tuple-element.12), channel_id=1, replica_groups=mesh['slab'=8,'sub'=4] {'slab'}, dimensions={0} | all-to-all | bytes 425984 | tf_op jit(solution)/shard_map/all_to_all | solution.py:508
  18.1 0.0 copy-done.1
  18.1 0.0 copy-done.2
  18.1 0.0 copy-done.3
  18.1 0.0 copy-done.4
  18.1 1.0 %owner.1 = bf16[8,96,128]{2,1,0:T(8,128)(2,1)S(1)} custom-call(bf16[8,104,128]{2,1,0:T(8,128)(2,1)S(1)} %all_to_all.10.refs_0_, s32[4,256]{1,0:T(4,128)S(1)} %bitcast.42, f32[4,256]{1,0:T(4,128)S(1)} %bitcast.43, bf16[128,128]{1,0:T(8,128)(2,1)S(1)} %copy-done.1, bf16[128,128]{1,0:T(8,128)(2,1)S(1)} %copy-done.2), custom_call_target="tpu_custom_call" | custom-call | tf_op jit(solution)/shard_map/owner/pallas_call | solution.py:529
  19.1 0.0 copy-start
  19.1 11.0 %all_to_all.11.back_ref = bf16[8,96,128]{2,1,0:T(8,128)(2,1)S(1)} all-to-all(bf16[8,96,128]{2,1,0:T(8,128)(2,1)S(1)} %owner.1), channel_id=1, replica_groups=mesh['slab'=8,'sub'=4] {'slab'}, dimensions={0} | all-to-all | bytes 393216 | tf_op jit(solution)/shard_map/all_to_all | solution.py:508
  30.1 0.0 copy-done
  30.1 2.0 %spread.1 = (f32[19,32,128]{2,1,0:T(8,128)S(1)}, f32[8,128]{1,0:T(8,128)S(1)}, f32[8,128]{1,0:T(8,128)S(1)}, bf16[5,32,128]{2,1,0:T(8,128)(2,1)S(1)}, bf16[5,32,128]{2,1,0:T(8,128)(2,1)S(1)}) custom-call(bf16[8,96,128]{2,1,0:T(8,128)(2,1)S(1)} %all_to_all.11.back_ref, f32[256,8]{1,0:T(8,128)S(1)} %get-tuple-element.13.sorted_ref, ...), custom_call_target="tpu_custom_call" | custom-call | tf_op jit(solution)/shard_map/spread/pallas_call | solution.py:545
  32.2 2.9 %collective-permute-start = (bf16[5,32,128]{2,1,0:T(8,128)(2,1)S(1)}, bf16[5,32,128]{2,1,0:T(8,128)(2,1)S(1)}, u32[]{:S(2)}, u32[]{:S(2)}) collective-permute-start(bf16[5,32,128]{2,1,0:T(8,128)(2,1)S(1)} %get-tuple-element.18), channel_id=1, source_target_pairs={{0,28},{4,8},{8,4},{12,16},{16,12},{20,24},{24,20},{28,0},{1,29},{... | collective-permute-start | bytes 122888 | tf_op jit(solution)/shard_map/ppermute | solution.py:440
  35.0 0.0 collective-permute-start.1
  35.0 2.8 %collective-permute-done.second_ref = bf16[5,32,128]{2,1,0:T(8,128)(2,1)S(1)} collective-permute-done((bf16[5,32,128]{2,1,0:T(8,128)(2,1)S(1)}, bf16[5,32,128]{2,1,0:T(8,128)(2,1)S(1)}, u32[]{:S(2)}, u32[]{:S(2)}) %collective-permute-start) | collective-permute-done | bytes 40992 | tf_op jit(solution)/shard_map/ppermute | solution.py:440
  37.8 0.4 collective-permute-done.1.first_ref
  38.2 3.2 %collective-permute-start.2 = (f32[5,128]{1,0:T(8,128)S(1)}, f32[5,128]{1,0:T(8,128)S(1)}, u32[]{:S(2)}, u32[]{:S(2)}) collective-permute-start(f32[5,128]{1,0:T(8,128)S(1)} %get-tuple-element.29), channel_id=1, source_target_pairs={{0,1},{1,0},{2,3},{3,2},{4,5},{5,4},{6,7},{7,6},{8,9},{9,8},{10,11... | collective-permute-start | bytes 7688 | tf_op jit(solution)/shard_map/ppermute | solution.py:440
  41.4 1.2 %collective-permute-start.3 = (f32[5,128]{1,0:T(8,128)S(1)}, f32[5,128]{1,0:T(8,128)S(1)}, u32[]{:S(2)}, u32[]{:S(2)}) collective-permute-start(f32[5,128]{1,0:T(8,128)S(1)} %get-tuple-element.28), channel_id=1, source_target_pairs={{0,3},{1,2},{2,1},{3,0},{4,7},{5,6},{6,5},{7,4},{8,11},{9,10},{10,... | collective-permute-start | bytes 7688 | tf_op jit(solution)/shard_map/ppermute | solution.py:440
  42.6 1.0 %finish.1 = bf16[3,256,128]{2,1,0:T(8,128)(2,1)} custom-call(bf16[8,96,128]{2,1,0:T(8,128)(2,1)S(1)} %all_to_all.11.back_ref, f32[256,8]{1,0:T(8,128)S(1)} %get-tuple-element.13.sorted_ref, f32[256,8]{1,0:T(8,128)S(1)} %get-tuple-element.21.send_ref), custom_call_target="tpu_custom_call" | custom-call | flops 50000000 | bytes 400000 | tf_op jit(solution)/shard_map/finish/pallas_call | solution.py:559
  43.6 0.0 collective-permute-done.2.one_ref
  43.6 0.8 %collective-permute-done.3.two_ref = f32[5,128]{1,0:T(8,128)S(1)} collective-permute-done((f32[5,128]{1,0:T(8,128)S(1)}, f32[5,128]{1,0:T(8,128)S(1)}, u32[]{:S(2)}, u32[]{:S(2)}) %collective-permute-start.3) | collective-permute-done | bytes 2592 | tf_op jit(solution)/shard_map/ppermute | solution.py:440
  44.4 0.8 %stream.1 = f32[19,32,128]{2,1,0:T(8,128)} custom-call(f32[19,32,128]{2,1,0:T(8,128)S(1)} %get-tuple-element.16.collided_ref, f32[5,128]{1,0:T(8,128)S(1)} %collective-permute-done.2.one_ref, f32[5,128]{1,0:T(8,128)S(1)} %collective-permute-done.3.two_ref, bf16[5,32,128]{2,1,0:T(8,128)(2,1)S(1)} %collective-permute-done.1.first_ref, ...), custom_call_target="tpu_custom_call" | custom-call | tf_op jit(solution)/shard_map/stream/pallas_call | solution.py:583
  (4 shorter events, 0.0 us)
Async XLA Ops:
  5.0 13.1 %copy-start.1 = (bf16[128,128]{1,0:T(8,128)(2,1)S(1)}, bf16[128,128]{1,0:T(8,128)(2,1)}, u32[]{:S(2)}) copy-start(bf16[128,128]{1,0:T(8,128)(2,1)} %refs_3_.1) | copy-start | bytes 98308
  5.0 13.1 %copy-start.2 = (bf16[128,128]{1,0:T(8,128)(2,1)S(1)}, bf16[128,128]{1,0:T(8,128)(2,1)}, u32[]{:S(2)}) copy-start(bf16[128,128]{1,0:T(8,128)(2,1)} %refs_4_.1) | copy-start | bytes 98308
  5.0 13.1 %copy-start.3 = (s32[1,1,256,4]{2,3,1,0:T(4,128)S(1)}, s32[1,1,256,4]{2,3,1,0:T(4,128)}, u32[]{:S(2)}) copy-start(s32[1,1,256,4]{2,3,1,0:T(4,128)} %param.18) | copy-start | bytes 12292
  5.0 13.1 %copy-start.4 = (f32[1,1,256,4]{2,3,1,0:T(4,128)S(1)}, f32[1,1,256,4]{2,3,1,0:T(4,128)}, u32[]{:S(2)}) copy-start(f32[1,1,256,4]{2,3,1,0:T(4,128)} %param.19) | copy-start | bytes 12292
  19.1 11.0 %copy-start = (f32[19,1,32,128]{3,2,1,0:T(8,128)S(1)}, f32[19,1,32,128]{3,2,1,0:T(8,128)}, u32[]{:S(2)}) copy-start(f32[19,1,32,128]{3,2,1,0:T(8,128)} %param.11) | copy-start | bytes 933892
  32.2 5.6 %collective-permute-start = (bf16[5,32,128]{2,1,0:T(8,128)(2,1)S(1)}, bf16[5,32,128]{2,1,0:T(8,128)(2,1)S(1)}, u32[]{:S(2)}, u32[]{:S(2)}) collective-permute-start(bf16[5,32,128]{2,1,0:T(8,128)(2,1)S(1)} %get-tuple-element.18), channel_id=1, source_target_pairs={{0,28},{4,8},{8,4},{12,16},{16,12},{20,24},{24,20},{28,0},{1,29},{... | collective-permute-start | bytes 122888 | tf_op jit(solution)/shard_map/ppermute | solution.py:440
  35.0 3.2 %collective-permute-start.1 = (bf16[5,32,128]{2,1,0:T(8,128)(2,1)S(1)}, bf16[5,32,128]{2,1,0:T(8,128)(2,1)S(1)}, u32[]{:S(2)}, u32[]{:S(2)}) collective-permute-start(bf16[5,32,128]{2,1,0:T(8,128)(2,1)S(1)} %get-tuple-element.19), channel_id=1, source_target_pairs={{0,4},{4,0},{8,12},{12,8},{16,20},{20,16},{24,28},{28,24},{1,5},{5... | collective-permute-start | bytes 122888 | tf_op jit(solution)/shard_map/ppermute | solution.py:440
  38.2 5.4 %collective-permute-start.2 = (f32[5,128]{1,0:T(8,128)S(1)}, f32[5,128]{1,0:T(8,128)S(1)}, u32[]{:S(2)}, u32[]{:S(2)}) collective-permute-start(f32[5,128]{1,0:T(8,128)S(1)} %get-tuple-element.29), channel_id=1, source_target_pairs={{0,1},{1,0},{2,3},{3,2},{4,5},{5,4},{6,7},{7,6},{8,9},{9,8},{10,11... | collective-permute-start | bytes 7688 | tf_op jit(solution)/shard_map/ppermute | solution.py:440
  41.4 3.0 %collective-permute-start.3 = (f32[5,128]{1,0:T(8,128)S(1)}, f32[5,128]{1,0:T(8,128)S(1)}, u32[]{:S(2)}, u32[]{:S(2)}) collective-permute-start(f32[5,128]{1,0:T(8,128)S(1)} %get-tuple-element.28), channel_id=1, source_target_pairs={{0,3},{1,2},{2,1},{3,0},{4,7},{5,6},{6,5},{7,4},{8,11},{9,10},{10,... | collective-permute-start | bytes 7688 | tf_op jit(solution)/shard_map/ppermute | solution.py:440

commit v9 on v8

--- a/solution.py
+++ b/solution.py
@@ -117,27 +117,26 @@
 
 
 def sample_kernel(slab_count, packed, *refs):
-    sources, refs = refs[:7], refs[7:]
+    left_ref, sources, refs = refs[0], refs[1:7], refs[7:]
     slip_ref, refs = refs[0], refs[1:]
     if not packed:
         spot_ref, refs = refs[0], refs[1:]
     send_ref, sorted_ref, z_ref, y_ref = refs[:4]
-    targets, (sems,) = refs[4:11], refs[11:]
+    targets, (sems,) = refs[4:10], refs[10:]
     copies = [
         pltpu.make_async_copy(source, target, sems.at[number])
         for number, (source, target) in enumerate(zip(sources, targets))
     ]
     for copy in copies:
         copy.start()
-    count_ref, table_ref, marker_count_ref, id_ref, velocity_ref, cell_ref, pops_ref = targets
+    table_ref, marker_count_ref, id_ref, velocity_ref, cell_ref, pops_ref = targets
     slots, width = cell_ref.shape
     rows, depth = pops_ref.shape[1:]
     capacity = slots // slab_count
-    for copy in copies[:5]:
+    for copy in copies[:4]:
         copy.wait()
 
-    lane = iota((1, slots), 1, jnp.int32)
-    alive = lane < count_ref[0]
+    alive = left_ref[...] > 0
     identity = id_ref[...]
     block = identity // slots
     spot = (identity % slots).astype(F32)
@@ -177,7 +176,7 @@
     send_ref[...] = own
     sorted_ref[...] = dot_nn(place, own.astype(BF))
 
-    for copy in copies[5:]:
+    for copy in copies[4:]:
         copy.wait()
     cells = cell_ref[...]
     z_all, y_all = (cells % depth).astype(F32), (cells // depth).astype(F32)
@@ -474,22 +473,21 @@
     results = pl.pallas_call(
         functools.partial(sample_kernel, slab_count, packed),
         out_shape=sample_out,
-        in_specs=[whole(pltpu.HBM)] * 7,
+        in_specs=[whole()] + [whole(pltpu.HBM)] * 6,
         out_specs=[whole()] * len(sample_out),
         scratch_shapes=[
-            pltpu.SMEM((1,), jnp.int32),
             pltpu.SMEM((slab_count,), jnp.int32),
             pltpu.VMEM((1, slots), jnp.int32),
             pltpu.VMEM((1, slots), jnp.int32),
             pltpu.VMEM((3, 1, slots), F32),
             pltpu.VMEM((slots, width), jnp.int32),
             pltpu.VMEM((19, rows, depth), F32),
-            pltpu.SemaphoreType.DMA((7,)),
+            pltpu.SemaphoreType.DMA((6,)),
         ],
         compiler_params=limits,
         name="sample",
     )(
-        particle_count.reshape(1),
+        particle_count - lax.broadcasted_iota(jnp.int32, (1, slots), 1),
         *[
             pltpu.with_memory_space_constraint(value, pltpu.HBM)
             for value in (

time: 45.6 us -> 45.6 us (level)
  no operation moved by 1% of the time
where the time goes in v9:
time: 45.6 us; the launch traced here: 45.3 us
  blocking collectives  24 us (53%)
  Pallas kernels  8.59 us (19%)
  starting transfers between devices  7.24 us (16%)
  waiting for transfers between devices  4 us (9%)
  between operations  1.36 us (3%)
    all_to_all x2, blocking collectives, exchange(): lax.all_to_all(value, 'slab', split_axis=0, concat_axis=0, tiled=True)  24 us
    ppermute x4, starting transfers between devices, swap(): return lax.ppermute(value, axis, pairs)  7.24 us
    ppermute x4, waiting for transfers between devices, swap(): return lax.ppermute(value, axis, pairs)  4 us
    pallas_call x1, Pallas kernels, per_device(): pl.pallas_call(functools.partial(sample_kernel, slab_count, packed), out_...  3.68 us
    pallas_call x1, Pallas kernels, per_device(): pl.pallas_call(functools.partial(spread_kernel, slab_count, packed), out_...  2.03 us
    pallas_call x1, Pallas kernels, per_device(): pl.pallas_call(functools.partial(owner_kernel, slab_count, packed), out_s...  1.03 us
    pallas_call x1, Pallas kernels, per_device(): pl.pallas_call(functools.partial(finish_kernel, slab_count, packed), out_...  1.02 us
  transfers between devices with their start and end apart: 4, of which 3 were waited for; matrix products, arithmetic and copies ran while one was open for 0% of the time, Pallas kernels for 2%

profile of v9, /device:TPU:1, one launch (start us, length us, event | category | flops | bytes accessed | tf_op | source)
XLA Modules:
  0.0 45.3 jit_solution(11852739221713845323)
XLA Ops:
  1.3 3.7 %sample.1 = (bf16[8,104,128]{2,1,0:T(8,128)(2,1)S(1)}, f32[256,8]{1,0:T(8,128)S(1)}, f32[256,8]{1,0:T(8,128)S(1)}, f32[256,128]{1,0:T(8,128)S(1)}, f32[256,128]{1,0:T(8,128)S(1)}) custom-call(s32[1,256]{1,0:T(1,128)S(1)} %iota_subtract_fusion.refs_0_, s32[8]{0:T(128)} %bitcast.50, s32[1,256]{1,0:T(1,128)} %bitcast.48, s32[1,256]{1,0:T(1,128)} %bitcast.49, ...), custom_call_target="tpu_custom_call" | custom-call | tf_op jit(solution)/shard_map/sample/pallas_call | solution.py:473
  5.0 0.0 copy-start.1
  5.0 0.0 copy-start.2
  5.0 0.0 copy-start.3
  5.0 0.0 copy-start.4
  5.0 13.1 %all_to_all.10.refs_0_ = bf16[8,104,128]{2,1,0:T(8,128)(2,1)S(1)} all-to-all(bf16[8,104,128]{2,1,0:T(8,128)(2,1)S(1)} %get-tuple-element.12), channel_id=1, replica_groups=mesh['slab'=8,'sub'=4] {'slab'}, dimensions={0} | all-to-all | bytes 425984 | tf_op jit(solution)/shard_map/all_to_all | solution.py:506
  18.1 0.0 copy-done.1
  18.1 0.0 copy-done.2
  18.1 0.0 copy-done.3
  18.1 0.0 copy-done.4
  18.1 1.0 %owner.1 = bf16[8,96,128]{2,1,0:T(8,128)(2,1)S(1)} custom-call(bf16[8,104,128]{2,1,0:T(8,128)(2,1)S(1)} %all_to_all.10.refs_0_, s32[4,256]{1,0:T(4,128)S(1)} %bitcast.42, f32[4,256]{1,0:T(4,128)S(1)} %bitcast.43, bf16[128,128]{1,0:T(8,128)(2,1)S(1)} %copy-done.1, bf16[128,128]{1,0:T(8,128)(2,1)S(1)} %copy-done.2), custom_call_target="tpu_custom_call" | custom-call | tf_op jit(solution)/shard_map/owner/pallas_call | solution.py:527
  19.1 0.0 copy-start
  19.1 11.0 %all_to_all.11.back_ref = bf16[8,96,128]{2,1,0:T(8,128)(2,1)S(1)} all-to-all(bf16[8,96,128]{2,1,0:T(8,128)(2,1)S(1)} %owner.1), channel_id=1, replica_groups=mesh['slab'=8,'sub'=4] {'slab'}, dimensions={0} | all-to-all | bytes 393216 | tf_op jit(solution)/shard_map/all_to_all | solution.py:506
  30.1 0.0 copy-done
  30.1 2.0 %spread.1 = (f32[19,32,128]{2,1,0:T(8,128)S(1)}, f32[8,128]{1,0:T(8,128)S(1)}, f32[8,128]{1,0:T(8,128)S(1)}, bf16[5,32,128]{2,1,0:T(8,128)(2,1)S(1)}, bf16[5,32,128]{2,1,0:T(8,128)(2,1)S(1)}) custom-call(bf16[8,96,128]{2,1,0:T(8,128)(2,1)S(1)} %all_to_all.11.back_ref, f32[256,8]{1,0:T(8,128)S(1)} %get-tuple-element.13.sorted_ref, ...), custom_call_target="tpu_custom_call" | custom-call | tf_op jit(solution)/shard_map/spread/pallas_call | solution.py:543
  32.2 2.9 %collective-permute-start = (bf16[5,32,128]{2,1,0:T(8,128)(2,1)S(1)}, bf16[5,32,128]{2,1,0:T(8,128)(2,1)S(1)}, u32[]{:S(2)}, u32[]{:S(2)}) collective-permute-start(bf16[5,32,128]{2,1,0:T(8,128)(2,1)S(1)} %get-tuple-element.18), channel_id=1, source_target_pairs={{0,28},{4,8},{8,4},{12,16},{16,12},{20,24},{24,20},{28,0},{1,29},{... | collective-permute-start | bytes 122888 | tf_op jit(solution)/shard_map/ppermute | solution.py:439
  35.1 0.0 collective-permute-start.1
  35.1 2.8 %collective-permute-done.second_ref = bf16[5,32,128]{2,1,0:T(8,128)(2,1)S(1)} collective-permute-done((bf16[5,32,128]{2,1,0:T(8,128)(2,1)S(1)}, bf16[5,32,128]{2,1,0:T(8,128)(2,1)S(1)}, u32[]{:S(2)}, u32[]{:S(2)}) %collective-permute-start) | collective-permute-done | bytes 40992 | tf_op jit(solution)/shard_map/ppermute | solution.py:439
  37.8 0.4 collective-permute-done.1.first_ref
  38.2 3.2 %collective-permute-start.2 = (f32[5,128]{1,0:T(8,128)S(1)}, f32[5,128]{1,0:T(8,128)S(1)}, u32[]{:S(2)}, u32[]{:S(2)}) collective-permute-start(f32[5,128]{1,0:T(8,128)S(1)} %get-tuple-element.29), channel_id=1, source_target_pairs={{0,1},{1,0},{2,3},{3,2},{4,5},{5,4},{6,7},{7,6},{8,9},{9,8},{10,11... | collective-permute-start | bytes 7688 | tf_op jit(solution)/shard_map/ppermute | solution.py:439
  41.4 1.2 %collective-permute-start.3 = (f32[5,128]{1,0:T(8,128)S(1)}, f32[5,128]{1,0:T(8,128)S(1)}, u32[]{:S(2)}, u32[]{:S(2)}) collective-permute-start(f32[5,128]{1,0:T(8,128)S(1)} %get-tuple-element.28), channel_id=1, source_target_pairs={{0,3},{1,2},{2,1},{3,0},{4,7},{5,6},{6,5},{7,4},{8,11},{9,10},{10,... | collective-permute-start | bytes 7688 | tf_op jit(solution)/shard_map/ppermute | solution.py:439
  42.6 1.0 %finish.1 = bf16[3,256,128]{2,1,0:T(8,128)(2,1)} custom-call(bf16[8,96,128]{2,1,0:T(8,128)(2,1)S(1)} %all_to_all.11.back_ref, f32[256,8]{1,0:T(8,128)S(1)} %get-tuple-element.13.sorted_ref, f32[256,8]{1,0:T(8,128)S(1)} %get-tuple-element.21.send_ref), custom_call_target="tpu_custom_call" | custom-call | flops 50000000 | bytes 400000 | tf_op jit(solution)/shard_map/finish/pallas_call | solution.py:557
  43.6 0.0 collective-permute-done.2.one_ref
  43.6 0.8 %collective-permute-done.3.two_ref = f32[5,128]{1,0:T(8,128)S(1)} collective-permute-done((f32[5,128]{1,0:T(8,128)S(1)}, f32[5,128]{1,0:T(8,128)S(1)}, u32[]{:S(2)}, u32[]{:S(2)}) %collective-permute-start.3) | collective-permute-done | bytes 2592 | tf_op jit(solution)/shard_map/ppermute | solution.py:439
  44.5 0.8 %stream.1 = f32[19,32,128]{2,1,0:T(8,128)} custom-call(f32[19,32,128]{2,1,0:T(8,128)S(1)} %get-tuple-element.16.collided_ref, f32[5,128]{1,0:T(8,128)S(1)} %collective-permute-done.2.one_ref, f32[5,128]{1,0:T(8,128)S(1)} %collective-permute-done.3.two_ref, bf16[5,32,128]{2,1,0:T(8,128)(2,1)S(1)} %collective-permute-done.1.first_ref, ...), custom_call_target="tpu_custom_call" | custom-call | tf_op jit(solution)/shard_map/stream/pallas_call | solution.py:581
  (5 shorter events, 0.0 us)
Async XLA Ops:
  5.0 13.1 %copy-start.1 = (bf16[128,128]{1,0:T(8,128)(2,1)S(1)}, bf16[128,128]{1,0:T(8,128)(2,1)}, u32[]{:S(2)}) copy-start(bf16[128,128]{1,0:T(8,128)(2,1)} %refs_3_.1) | copy-start | bytes 98308
  5.0 13.1 %copy-start.2 = (bf16[128,128]{1,0:T(8,128)(2,1)S(1)}, bf16[128,128]{1,0:T(8,128)(2,1)}, u32[]{:S(2)}) copy-start(bf16[128,128]{1,0:T(8,128)(2,1)} %refs_4_.1) | copy-start | bytes 98308
  5.0 13.1 %copy-start.3 = (s32[1,1,256,4]{2,3,1,0:T(4,128)S(1)}, s32[1,1,256,4]{2,3,1,0:T(4,128)}, u32[]{:S(2)}) copy-start(s32[1,1,256,4]{2,3,1,0:T(4,128)} %param.18) | copy-start | bytes 12292
  5.0 13.1 %copy-start.4 = (f32[1,1,256,4]{2,3,1,0:T(4,128)S(1)}, f32[1,1,256,4]{2,3,1,0:T(4,128)}, u32[]{:S(2)}) copy-start(f32[1,1,256,4]{2,3,1,0:T(4,128)} %param.19) | copy-start | bytes 12292
  19.1 11.0 %copy-start = (f32[19,1,32,128]{3,2,1,0:T(8,128)S(1)}, f32[19,1,32,128]{3,2,1,0:T(8,128)}, u32[]{:S(2)}) copy-start(f32[19,1,32,128]{3,2,1,0:T(8,128)} %param.11) | copy-start | bytes 933892
  32.2 5.6 %collective-permute-start = (bf16[5,32,128]{2,1,0:T(8,128)(2,1)S(1)}, bf16[5,32,128]{2,1,0:T(8,128)(2,1)S(1)}, u32[]{:S(2)}, u32[]{:S(2)}) collective-permute-start(bf16[5,32,128]{2,1,0:T(8,128)(2,1)S(1)} %get-tuple-element.18), channel_id=1, source_target_pairs={{0,28},{4,8},{8,4},{12,16},{16,12},{20,24},{24,20},{28,0},{1,29},{... | collective-permute-start | bytes 122888 | tf_op jit(solution)/shard_map/ppermute | solution.py:439
  35.1 3.2 %collective-permute-start.1 = (bf16[5,32,128]{2,1,0:T(8,128)(2,1)S(1)}, bf16[5,32,128]{2,1,0:T(8,128)(2,1)S(1)}, u32[]{:S(2)}, u32[]{:S(2)}) collective-permute-start(bf16[5,32,128]{2,1,0:T(8,128)(2,1)S(1)} %get-tuple-element.19), channel_id=1, source_target_pairs={{0,4},{4,0},{8,12},{12,8},{16,20},{20,16},{24,28},{28,24},{1,5},{5... | collective-permute-start | bytes 122888 | tf_op jit(solution)/shard_map/ppermute | solution.py:439
  38.2 5.4 %collective-permute-start.2 = (f32[5,128]{1,0:T(8,128)S(1)}, f32[5,128]{1,0:T(8,128)S(1)}, u32[]{:S(2)}, u32[]{:S(2)}) collective-permute-start(f32[5,128]{1,0:T(8,128)S(1)} %get-tuple-element.29), channel_id=1, source_target_pairs={{0,1},{1,0},{2,3},{3,2},{4,5},{5,4},{6,7},{7,6},{8,9},{9,8},{10,11... | collective-permute-start | bytes 7688 | tf_op jit(solution)/shard_map/ppermute | solution.py:439
  41.4 3.0 %collective-permute-start.3 = (f32[5,128]{1,0:T(8,128)S(1)}, f32[5,128]{1,0:T(8,128)S(1)}, u32[]{:S(2)}, u32[]{:S(2)}) collective-permute-start(f32[5,128]{1,0:T(8,128)S(1)} %get-tuple-element.28), channel_id=1, source_target_pairs={{0,3},{1,2},{2,1},{3,0},{4,7},{5,6},{6,5},{7,4},{8,11},{9,10},{10,... | collective-permute-start | bytes 7688 | tf_op jit(solution)/shard_map/ppermute | solution.py:439

commit v10 on v9

--- a/solution.py
+++ b/solution.py
@@ -37,7 +37,7 @@
 upward_y = [3, 15, 17, 7, 10]
 downward_y = [4, 16, 18, 9, 8]
 mark_rows = 8
-kernel_memory = 16 << 20
+kernel_memory = 12 << 20
 BF = jnp.bfloat16
 F32 = jnp.float32
 PICK = jnp.float8_e4m3fn
@@ -198,10 +198,26 @@
             y_rows = y_all[eight : eight + 8]
             parts = [[], [], []]
             for first in range(0, 8, 2):
-                picks = jnp.concatenate(
-                    [one_hot_rows(z_rows[s : s + 1], depth) for s in (first, first + 1)], axis=1
-                )
-                picked = dot_nn(flow_pair, jnp.concatenate([picks, picks], axis=0))
+                if (eight + first) // 2 % 4 == 3:
+                    picked = []
+                    for s in (first, first + 1):
+                        index = jnp.broadcast_to(z_rows[s : s + 1].astype(jnp.int32), (8, depth))
+                        picked.append(
+                            jnp.concatenate(
+                                [
+                                    jnp.take_along_axis(flow[k : k + 8], index, axis=1)
+                                    for k in range(0, 3 * rows, 8)
+                                ],
+                                axis=0,
+                            )
+                        )
+                    picked = jnp.concatenate(picked, axis=1)
+                else:
+                    picks = jnp.concatenate(
+                        [one_hot_rows(z_rows[s : s + 1], depth) for s in (first, first + 1)],
+                        axis=1,
+                    )
+                    picked = dot_nn(flow_pair, jnp.concatenate([picks, picks], axis=0))
                 for s in (first, first + 1):
                     cut = slice((s - first) * width, (s - first + 1) * width)
                     tall = jnp.broadcast_to(y_rows[s : s + 1], (8, width))

time: 45.6 us -> 45.6 us (level)
  no operation moved by 1% of the time
where the time goes in v10:
time: 45.6 us; the launch traced here: 45.3 us
  blocking collectives  24 us (53%)
  Pallas kernels  8.58 us (19%)
  starting transfers between devices  7.24 us (16%)
  waiting for transfers between devices  4 us (9%)
  between operations  1.36 us (3%)
    all_to_all x2, blocking collectives, exchange(): lax.all_to_all(value, 'slab', split_axis=0, concat_axis=0, tiled=True)  24 us
    ppermute x4, starting transfers between devices, swap(): return lax.ppermute(value, axis, pairs)  7.24 us
    ppermute x4, waiting for transfers between devices, swap(): return lax.ppermute(value, axis, pairs)  4 us
    pallas_call x1, Pallas kernels, per_device(): pl.pallas_call(functools.partial(sample_kernel, slab_count, packed), out_...  3.67 us
    pallas_call x1, Pallas kernels, per_device(): pl.pallas_call(functools.partial(spread_kernel, slab_count, packed), out_...  2.03 us
    pallas_call x1, Pallas kernels, per_device(): pl.pallas_call(functools.partial(owner_kernel, slab_count, packed), out_s...  1.03 us
    pallas_call x1, Pallas kernels, per_device(): pl.pallas_call(functools.partial(finish_kernel, slab_count, packed), out_...  1.02 us
  transfers between devices with their start and end apart: 4, of which 3 were waited for; matrix products, arithmetic and copies ran while one was open for 0% of the time, Pallas kernels for 2%

profile of v10, /device:TPU:1, one launch (start us, length us, event | category | flops | bytes accessed | tf_op | source)
XLA Modules:
  0.0 45.3 jit_solution(17272483731175315199)
XLA Ops:
  1.3 3.7 %sample.1 = (bf16[8,104,128]{2,1,0:T(8,128)(2,1)S(1)}, f32[256,8]{1,0:T(8,128)S(1)}, f32[256,8]{1,0:T(8,128)S(1)}, f32[256,128]{1,0:T(8,128)S(1)}, f32[256,128]{1,0:T(8,128)S(1)}) custom-call(s32[1,256]{1,0:T(1,128)S(1)} %iota_subtract_fusion.refs_0_, s32[8]{0:T(128)} %bitcast.50, s32[1,256]{1,0:T(1,128)} %bitcast.48, s32[1,256]{1,0:T(1,128)} %bitcast.49, ...), custom_call_target="tpu_custom_call" | custom-call | tf_op jit(solution)/shard_map/sample/pallas_call | solution.py:489
  5.0 0.0 copy-start.1
  5.0 0.0 copy-start.2
  5.0 0.0 copy-start.3
  5.0 0.0 copy-start.4
  5.0 13.1 %all_to_all.10.refs_0_ = bf16[8,104,128]{2,1,0:T(8,128)(2,1)S(1)} all-to-all(bf16[8,104,128]{2,1,0:T(8,128)(2,1)S(1)} %get-tuple-element.12), channel_id=1, replica_groups=mesh['slab'=8,'sub'=4] {'slab'}, dimensions={0} | all-to-all | bytes 425984 | tf_op jit(solution)/shard_map/all_to_all | solution.py:522
  18.1 0.0 copy-done.1
  18.1 0.0 copy-done.2
  18.1 0.0 copy-done.3
  18.1 0.0 copy-done.4
  18.1 1.0 %owner.1 = bf16[8,96,128]{2,1,0:T(8,128)(2,1)S(1)} custom-call(bf16[8,104,128]{2,1,0:T(8,128)(2,1)S(1)} %all_to_all.10.refs_0_, s32[4,256]{1,0:T(4,128)S(1)} %bitcast.42, f32[4,256]{1,0:T(4,128)S(1)} %bitcast.43, bf16[128,128]{1,0:T(8,128)(2,1)S(1)} %copy-done.1, bf16[128,128]{1,0:T(8,128)(2,1)S(1)} %copy-done.2), custom_call_target="tpu_custom_call" | custom-call | tf_op jit(solution)/shard_map/owner/pallas_call | solution.py:543
  19.1 0.0 copy-start
  19.1 11.0 %all_to_all.11.back_ref = bf16[8,96,128]{2,1,0:T(8,128)(2,1)S(1)} all-to-all(bf16[8,96,128]{2,1,0:T(8,128)(2,1)S(1)} %owner.1), channel_id=1, replica_groups=mesh['slab'=8,'sub'=4] {'slab'}, dimensions={0} | all-to-all | bytes 393216 | tf_op jit(solution)/shard_map/all_to_all | solution.py:522
  30.1 0.0 copy-done
  30.1 2.0 %spread.1 = (f32[19,32,128]{2,1,0:T(8,128)S(1)}, f32[8,128]{1,0:T(8,128)S(1)}, f32[8,128]{1,0:T(8,128)S(1)}, bf16[5,32,128]{2,1,0:T(8,128)(2,1)S(1)}, bf16[5,32,128]{2,1,0:T(8,128)(2,1)S(1)}) custom-call(bf16[8,96,128]{2,1,0:T(8,128)(2,1)S(1)} %all_to_all.11.back_ref, f32[256,8]{1,0:T(8,128)S(1)} %get-tuple-element.13.sorted_ref, ...), custom_call_target="tpu_custom_call" | custom-call | tf_op jit(solution)/shard_map/spread/pallas_call | solution.py:559
  32.2 2.9 %collective-permute-start = (bf16[5,32,128]{2,1,0:T(8,128)(2,1)S(1)}, bf16[5,32,128]{2,1,0:T(8,128)(2,1)S(1)}, u32[]{:S(2)}, u32[]{:S(2)}) collective-permute-start(bf16[5,32,128]{2,1,0:T(8,128)(2,1)S(1)} %get-tuple-element.18), channel_id=1, source_target_pairs={{0,28},{4,8},{8,4},{12,16},{16,12},{20,24},{24,20},{28,0},{1,29},{... | collective-permute-start | bytes 122888 | tf_op jit(solution)/shard_map/ppermute | solution.py:455
  35.0 0.0 collective-permute-start.1
  35.1 2.8 %collective-permute-done.second_ref = bf16[5,32,128]{2,1,0:T(8,128)(2,1)S(1)} collective-permute-done((bf16[5,32,128]{2,1,0:T(8,128)(2,1)S(1)}, bf16[5,32,128]{2,1,0:T(8,128)(2,1)S(1)}, u32[]{:S(2)}, u32[]{:S(2)}) %collective-permute-start) | collective-permute-done | bytes 40992 | tf_op jit(solution)/shard_map/ppermute | solution.py:455
  37.8 0.4 collective-permute-done.1.first_ref
  38.2 3.2 %collective-permute-start.2 = (f32[5,128]{1,0:T(8,128)S(1)}, f32[5,128]{1,0:T(8,128)S(1)}, u32[]{:S(2)}, u32[]{:S(2)}) collective-permute-start(f32[5,128]{1,0:T(8,128)S(1)} %get-tuple-element.29), channel_id=1, source_target_pairs={{0,1},{1,0},{2,3},{3,2},{4,5},{5,4},{6,7},{7,6},{8,9},{9,8},{10,11... | collective-permute-start | bytes 7688 | tf_op jit(solution)/shard_map/ppermute | solution.py:455
  41.4 1.2 %collective-permute-start.3 = (f32[5,128]{1,0:T(8,128)S(1)}, f32[5,128]{1,0:T(8,128)S(1)}, u32[]{:S(2)}, u32[]{:S(2)}) collective-permute-start(f32[5,128]{1,0:T(8,128)S(1)} %get-tuple-element.28), channel_id=1, source_target_pairs={{0,3},{1,2},{2,1},{3,0},{4,7},{5,6},{6,5},{7,4},{8,11},{9,10},{10,... | collective-permute-start | bytes 7688 | tf_op jit(solution)/shard_map/ppermute | solution.py:455
  42.6 1.0 %finish.1 = bf16[3,256,128]{2,1,0:T(8,128)(2,1)} custom-call(bf16[8,96,128]{2,1,0:T(8,128)(2,1)S(1)} %all_to_all.11.back_ref, f32[256,8]{1,0:T(8,128)S(1)} %get-tuple-element.13.sorted_ref, f32[256,8]{1,0:T(8,128)S(1)} %get-tuple-element.21.send_ref), custom_call_target="tpu_custom_call" | custom-call | flops 50000000 | bytes 400000 | tf_op jit(solution)/shard_map/finish/pallas_call | solution.py:573
  43.6 0.0 collective-permute-done.2.one_ref
  43.6 0.8 %collective-permute-done.3.two_ref = f32[5,128]{1,0:T(8,128)S(1)} collective-permute-done((f32[5,128]{1,0:T(8,128)S(1)}, f32[5,128]{1,0:T(8,128)S(1)}, u32[]{:S(2)}, u32[]{:S(2)}) %collective-permute-start.3) | collective-permute-done | bytes 2592 | tf_op jit(solution)/shard_map/ppermute | solution.py:455
  44.4 0.8 %stream.1 = f32[19,32,128]{2,1,0:T(8,128)} custom-call(f32[19,32,128]{2,1,0:T(8,128)S(1)} %get-tuple-element.16.collided_ref, f32[5,128]{1,0:T(8,128)S(1)} %collective-permute-done.2.one_ref, f32[5,128]{1,0:T(8,128)S(1)} %collective-permute-done.3.two_ref, bf16[5,32,128]{2,1,0:T(8,128)(2,1)S(1)} %collective-permute-done.1.first_ref, ...), custom_call_target="tpu_custom_call" | custom-call | tf_op jit(solution)/shard_map/stream/pallas_call | solution.py:597
  (5 shorter events, 0.0 us)
Async XLA Ops:
  5.0 13.1 %copy-start.1 = (bf16[128,128]{1,0:T(8,128)(2,1)S(1)}, bf16[128,128]{1,0:T(8,128)(2,1)}, u32[]{:S(2)}) copy-start(bf16[128,128]{1,0:T(8,128)(2,1)} %refs_3_.1) | copy-start | bytes 98308
  5.0 13.1 %copy-start.2 = (bf16[128,128]{1,0:T(8,128)(2,1)S(1)}, bf16[128,128]{1,0:T(8,128)(2,1)}, u32[]{:S(2)}) copy-start(bf16[128,128]{1,0:T(8,128)(2,1)} %refs_4_.1) | copy-start | bytes 98308
  5.0 13.1 %copy-start.3 = (s32[1,1,256,4]{2,3,1,0:T(4,128)S(1)}, s32[1,1,256,4]{2,3,1,0:T(4,128)}, u32[]{:S(2)}) copy-start(s32[1,1,256,4]{2,3,1,0:T(4,128)} %param.18) | copy-start | bytes 12292
  5.0 13.1 %copy-start.4 = (f32[1,1,256,4]{2,3,1,0:T(4,128)S(1)}, f32[1,1,256,4]{2,3,1,0:T(4,128)}, u32[]{:S(2)}) copy-start(f32[1,1,256,4]{2,3,1,0:T(4,128)} %param.19) | copy-start | bytes 12292
  19.1 11.0 %copy-start = (f32[19,1,32,128]{3,2,1,0:T(8,128)S(1)}, f32[19,1,32,128]{3,2,1,0:T(8,128)}, u32[]{:S(2)}) copy-start(f32[19,1,32,128]{3,2,1,0:T(8,128)} %param.11) | copy-start | bytes 933892
  32.2 5.6 %collective-permute-start = (bf16[5,32,128]{2,1,0:T(8,128)(2,1)S(1)}, bf16[5,32,128]{2,1,0:T(8,128)(2,1)S(1)}, u32[]{:S(2)}, u32[]{:S(2)}) collective-permute-start(bf16[5,32,128]{2,1,0:T(8,128)(2,1)S(1)} %get-tuple-element.18), channel_id=1, source_target_pairs={{0,28},{4,8},{8,4},{12,16},{16,12},{20,24},{24,20},{28,0},{1,29},{... | collective-permute-start | bytes 122888 | tf_op jit(solution)/shard_map/ppermute | solution.py:455
  35.0 3.2 %collective-permute-start.1 = (bf16[5,32,128]{2,1,0:T(8,128)(2,1)S(1)}, bf16[5,32,128]{2,1,0:T(8,128)(2,1)S(1)}, u32[]{:S(2)}, u32[]{:S(2)}) collective-permute-start(bf16[5,32,128]{2,1,0:T(8,128)(2,1)S(1)} %get-tuple-element.19), channel_id=1, source_target_pairs={{0,4},{4,0},{8,12},{12,8},{16,20},{20,16},{24,28},{28,24},{1,5},{5... | collective-permute-start | bytes 122888 | tf_op jit(solution)/shard_map/ppermute | solution.py:455
  38.2 5.4 %collective-permute-start.2 = (f32[5,128]{1,0:T(8,128)S(1)}, f32[5,128]{1,0:T(8,128)S(1)}, u32[]{:S(2)}, u32[]{:S(2)}) collective-permute-start(f32[5,128]{1,0:T(8,128)S(1)} %get-tuple-element.29), channel_id=1, source_target_pairs={{0,1},{1,0},{2,3},{3,2},{4,5},{5,4},{6,7},{7,6},{8,9},{9,8},{10,11... | collective-permute-start | bytes 7688 | tf_op jit(solution)/shard_map/ppermute | solution.py:455
  41.4 3.0 %collective-permute-start.3 = (f32[5,128]{1,0:T(8,128)S(1)}, f32[5,128]{1,0:T(8,128)S(1)}, u32[]{:S(2)}, u32[]{:S(2)}) collective-permute-start(f32[5,128]{1,0:T(8,128)S(1)} %get-tuple-element.28), channel_id=1, source_target_pairs={{0,3},{1,2},{2,1},{3,0},{4,7},{5,6},{6,5},{7,4},{8,11},{9,10},{10,... | collective-permute-start | bytes 7688 | tf_op jit(solution)/shard_map/ppermute | solution.py:455

commit v11 on v9

--- a/solution.py
+++ b/solution.py
@@ -574,6 +574,7 @@
     two_down = jnp.where(slab_even, first[1, bottom], second[1, bottom])
     up = jnp.concatenate([up[:3], one_up.astype(F32), two_up.astype(F32)])
     down = jnp.concatenate([down[:3], one_down.astype(F32), two_down.astype(F32)])
+    up, down, marker_force = lax.optimization_barrier((up, down, marker_force))
     low_high = (
         swap(jnp.where(sub_even, up, down), "sub", 0),
         swap(jnp.where(sub_even, down, up), "sub", 1),

time: 45.6 us -> 45.6 us (level)
  no operation moved by 1% of the time
where the time goes in v11:
time: 45.6 us; the launch traced here: 45.3 us
  blocking collectives  24 us (53%)
  Pallas kernels  8.59 us (19%)
  starting transfers between devices  7.24 us (16%)
  waiting for transfers between devices  4 us (9%)
  between operations  1.37 us (3%)
    all_to_all x2, blocking collectives, exchange(): lax.all_to_all(value, 'slab', split_axis=0, concat_axis=0, tiled=True)  24 us
    ppermute x4, starting transfers between devices, swap(): return lax.ppermute(value, axis, pairs)  7.24 us
    ppermute x4, waiting for transfers between devices, swap(): return lax.ppermute(value, axis, pairs)  4 us
    pallas_call x1, Pallas kernels, per_device(): pl.pallas_call(functools.partial(sample_kernel, slab_count, packed), out_...  3.68 us
    pallas_call x1, Pallas kernels, per_device(): pl.pallas_call(functools.partial(spread_kernel, slab_count, packed), out_...  2.03 us
    pallas_call x1, Pallas kernels, per_device(): pl.pallas_call(functools.partial(owner_kernel, slab_count, packed), out_s...  1.03 us
    pallas_call x1, Pallas kernels, per_device(): pl.pallas_call(functools.partial(finish_kernel, slab_count, packed), out_...  1.02 us
  transfers between devices with their start and end apart: 4, of which 3 were waited for; matrix products, arithmetic and copies ran while one was open for 0% of the time, Pallas kernels for 2%

profile of v11, /device:TPU:1, one launch (start us, length us, event | category | flops | bytes accessed | tf_op | source)
XLA Modules:
  0.0 45.3 jit_solution(8061032215017070627)
XLA Ops:
  1.3 3.7 %sample.1 = (bf16[8,104,128]{2,1,0:T(8,128)(2,1)S(1)}, f32[256,8]{1,0:T(8,128)S(1)}, f32[256,8]{1,0:T(8,128)S(1)}, f32[256,128]{1,0:T(8,128)S(1)}, f32[256,128]{1,0:T(8,128)S(1)}) custom-call(s32[1,256]{1,0:T(1,128)S(1)} %iota_subtract_fusion.refs_0_, s32[8]{0:T(128)} %bitcast.50, s32[1,256]{1,0:T(1,128)} %bitcast.48, s32[1,256]{1,0:T(1,128)} %bitcast.49, ...), custom_call_target="tpu_custom_call" | custom-call | tf_op jit(solution)/shard_map/sample/pallas_call | solution.py:473
  5.0 0.0 copy-start.1
  5.0 0.0 copy-start.2
  5.0 0.0 copy-start.3
  5.0 0.0 copy-start.4
  5.0 13.1 %all_to_all.10.refs_0_ = bf16[8,104,128]{2,1,0:T(8,128)(2,1)S(1)} all-to-all(bf16[8,104,128]{2,1,0:T(8,128)(2,1)S(1)} %get-tuple-element.15), channel_id=1, replica_groups=mesh['slab'=8,'sub'=4] {'slab'}, dimensions={0} | all-to-all | bytes 425984 | tf_op jit(solution)/shard_map/all_to_all | solution.py:506
  18.1 0.0 copy-done.1
  18.1 0.0 copy-done.2
  18.1 0.0 copy-done.3
  18.1 0.0 copy-done.4
  18.1 1.0 %owner.1 = bf16[8,96,128]{2,1,0:T(8,128)(2,1)S(1)} custom-call(bf16[8,104,128]{2,1,0:T(8,128)(2,1)S(1)} %all_to_all.10.refs_0_, s32[4,256]{1,0:T(4,128)S(1)} %bitcast.42, f32[4,256]{1,0:T(4,128)S(1)} %bitcast.43, bf16[128,128]{1,0:T(8,128)(2,1)S(1)} %copy-done.1, bf16[128,128]{1,0:T(8,128)(2,1)S(1)} %copy-done.2), custom_call_target="tpu_custom_call" | custom-call | tf_op jit(solution)/shard_map/owner/pallas_call | solution.py:527
  19.1 0.0 copy-start
  19.1 11.0 %all_to_all.11.back_ref = bf16[8,96,128]{2,1,0:T(8,128)(2,1)S(1)} all-to-all(bf16[8,96,128]{2,1,0:T(8,128)(2,1)S(1)} %owner.1), channel_id=1, replica_groups=mesh['slab'=8,'sub'=4] {'slab'}, dimensions={0} | all-to-all | bytes 393216 | tf_op jit(solution)/shard_map/all_to_all | solution.py:506
  30.1 0.0 copy-done
  30.1 2.0 %spread.1 = (f32[19,32,128]{2,1,0:T(8,128)S(1)}, f32[8,128]{1,0:T(8,128)S(1)}, f32[8,128]{1,0:T(8,128)S(1)}, bf16[5,32,128]{2,1,0:T(8,128)(2,1)S(1)}, bf16[5,32,128]{2,1,0:T(8,128)(2,1)S(1)}) custom-call(bf16[8,96,128]{2,1,0:T(8,128)(2,1)S(1)} %all_to_all.11.back_ref, f32[256,8]{1,0:T(8,128)S(1)} %get-tuple-element.16.sorted_ref, ...), custom_call_target="tpu_custom_call" | custom-call | tf_op jit(solution)/shard_map/spread/pallas_call | solution.py:543
  32.2 2.9 %collective-permute-start = (bf16[5,32,128]{2,1,0:T(8,128)(2,1)S(1)}, bf16[5,32,128]{2,1,0:T(8,128)(2,1)S(1)}, u32[]{:S(2)}, u32[]{:S(2)}) collective-permute-start(bf16[5,32,128]{2,1,0:T(8,128)(2,1)S(1)} %get-tuple-element.21), channel_id=1, source_target_pairs={{0,28},{4,8},{8,4},{12,16},{16,12},{20,24},{24,20},{28,0},{1,29},{... | collective-permute-start | bytes 122888 | tf_op jit(solution)/shard_map/ppermute | solution.py:439
  35.1 0.0 collective-permute-start.1
  35.1 1.0 %finish.1 = bf16[3,256,128]{2,1,0:T(8,128)(2,1)} custom-call(bf16[8,96,128]{2,1,0:T(8,128)(2,1)S(1)} %all_to_all.11.back_ref, f32[256,8]{1,0:T(8,128)S(1)} %get-tuple-element.16.sorted_ref, f32[256,8]{1,0:T(8,128)S(1)} %get-tuple-element.24.send_ref), custom_call_target="tpu_custom_call" | custom-call | flops 50000000 | bytes 400000 | tf_op jit(solution)/shard_map/finish/pallas_call | solution.py:557
  36.1 1.7 %collective-permute-done.second_ref = bf16[5,32,128]{2,1,0:T(8,128)(2,1)S(1)} collective-permute-done((bf16[5,32,128]{2,1,0:T(8,128)(2,1)S(1)}, bf16[5,32,128]{2,1,0:T(8,128)(2,1)S(1)}, u32[]{:S(2)}, u32[]{:S(2)}) %collective-permute-start) | collective-permute-done | bytes 40992 | tf_op jit(solution)/shard_map/ppermute | solution.py:439
  37.8 0.4 collective-permute-done.1.first_ref
  38.3 3.2 %collective-permute-start.2 = (f32[5,128]{1,0:T(8,128)S(1)}, f32[5,128]{1,0:T(8,128)S(1)}, u32[]{:S(2)}, u32[]{:S(2)}) collective-permute-start(f32[5,128]{1,0:T(8,128)S(1)} %get-tuple-element.35), channel_id=1, source_target_pairs={{0,1},{1,0},{2,3},{3,2},{4,5},{5,4},{6,7},{7,6},{8,9},{9,8},{10,11... | collective-permute-start | bytes 7688 | tf_op jit(solution)/shard_map/ppermute | solution.py:439
  41.4 1.2 %collective-permute-start.3 = (f32[5,128]{1,0:T(8,128)S(1)}, f32[5,128]{1,0:T(8,128)S(1)}, u32[]{:S(2)}, u32[]{:S(2)}) collective-permute-start(f32[5,128]{1,0:T(8,128)S(1)} %get-tuple-element.34), channel_id=1, source_target_pairs={{0,3},{1,2},{2,1},{3,0},{4,7},{5,6},{6,5},{7,4},{8,11},{9,10},{10,... | collective-permute-start | bytes 7688 | tf_op jit(solution)/shard_map/ppermute | solution.py:439
  42.6 0.0 collective-permute-done.2.one_ref
  42.6 1.9 %collective-permute-done.3.two_ref = f32[5,128]{1,0:T(8,128)S(1)} collective-permute-done((f32[5,128]{1,0:T(8,128)S(1)}, f32[5,128]{1,0:T(8,128)S(1)}, u32[]{:S(2)}, u32[]{:S(2)}) %collective-permute-start.3) | collective-permute-done | bytes 2592 | tf_op jit(solution)/shard_map/ppermute | solution.py:439
  44.5 0.8 %stream.1 = f32[19,32,128]{2,1,0:T(8,128)} custom-call(f32[19,32,128]{2,1,0:T(8,128)S(1)} %get-tuple-element.19.collided_ref, f32[5,128]{1,0:T(8,128)S(1)} %collective-permute-done.2.one_ref, f32[5,128]{1,0:T(8,128)S(1)} %collective-permute-done.3.two_ref, bf16[5,32,128]{2,1,0:T(8,128)(2,1)S(1)} %collective-permute-done.1.first_ref, ...), custom_call_target="tpu_custom_call" | custom-call | tf_op jit(solution)/shard_map/stream/pallas_call | solution.py:582
  (6 shorter events, 0.0 us)
Async XLA Ops:
  5.0 13.1 %copy-start.1 = (bf16[128,128]{1,0:T(8,128)(2,1)S(1)}, bf16[128,128]{1,0:T(8,128)(2,1)}, u32[]{:S(2)}) copy-start(bf16[128,128]{1,0:T(8,128)(2,1)} %refs_3_.1) | copy-start | bytes 98308
  5.0 13.1 %copy-start.2 = (bf16[128,128]{1,0:T(8,128)(2,1)S(1)}, bf16[128,128]{1,0:T(8,128)(2,1)}, u32[]{:S(2)}) copy-start(bf16[128,128]{1,0:T(8,128)(2,1)} %refs_4_.1) | copy-start | bytes 98308
  5.0 13.1 %copy-start.3 = (s32[1,1,256,4]{2,3,1,0:T(4,128)S(1)}, s32[1,1,256,4]{2,3,1,0:T(4,128)}, u32[]{:S(2)}) copy-start(s32[1,1,256,4]{2,3,1,0:T(4,128)} %param.18) | copy-start | bytes 12292
  5.0 13.1 %copy-start.4 = (f32[1,1,256,4]{2,3,1,0:T(4,128)S(1)}, f32[1,1,256,4]{2,3,1,0:T(4,128)}, u32[]{:S(2)}) copy-start(f32[1,1,256,4]{2,3,1,0:T(4,128)} %param.19) | copy-start | bytes 12292
  19.1 11.0 %copy-start = (f32[19,1,32,128]{3,2,1,0:T(8,128)S(1)}, f32[19,1,32,128]{3,2,1,0:T(8,128)}, u32[]{:S(2)}) copy-start(f32[19,1,32,128]{3,2,1,0:T(8,128)} %param.11) | copy-start | bytes 933892
  32.2 5.6 %collective-permute-start = (bf16[5,32,128]{2,1,0:T(8,128)(2,1)S(1)}, bf16[5,32,128]{2,1,0:T(8,128)(2,1)S(1)}, u32[]{:S(2)}, u32[]{:S(2)}) collective-permute-start(bf16[5,32,128]{2,1,0:T(8,128)(2,1)S(1)} %get-tuple-element.21), channel_id=1, source_target_pairs={{0,28},{4,8},{8,4},{12,16},{16,12},{20,24},{24,20},{28,0},{1,29},{... | collective-permute-start | bytes 122888 | tf_op jit(solution)/shard_map/ppermute | solution.py:439
  35.1 3.2 %collective-permute-start.1 = (bf16[5,32,128]{2,1,0:T(8,128)(2,1)S(1)}, bf16[5,32,128]{2,1,0:T(8,128)(2,1)S(1)}, u32[]{:S(2)}, u32[]{:S(2)}) collective-permute-start(bf16[5,32,128]{2,1,0:T(8,128)(2,1)S(1)} %get-tuple-element.22), channel_id=1, source_target_pairs={{0,4},{4,0},{8,12},{12,8},{16,20},{20,16},{24,28},{28,24},{1,5},{5... | collective-permute-start | bytes 122888 | tf_op jit(solution)/shard_map/ppermute | solution.py:439
  38.3 4.4 %collective-permute-start.2 = (f32[5,128]{1,0:T(8,128)S(1)}, f32[5,128]{1,0:T(8,128)S(1)}, u32[]{:S(2)}, u32[]{:S(2)}) collective-permute-start(f32[5,128]{1,0:T(8,128)S(1)} %get-tuple-element.35), channel_id=1, source_target_pairs={{0,1},{1,0},{2,3},{3,2},{4,5},{5,4},{6,7},{7,6},{8,9},{9,8},{10,11... | collective-permute-start | bytes 7688 | tf_op jit(solution)/shard_map/ppermute | solution.py:439
  41.4 3.0 %collective-permute-start.3 = (f32[5,128]{1,0:T(8,128)S(1)}, f32[5,128]{1,0:T(8,128)S(1)}, u32[]{:S(2)}, u32[]{:S(2)}) collective-permute-start(f32[5,128]{1,0:T(8,128)S(1)} %get-tuple-element.34), channel_id=1, source_target_pairs={{0,3},{1,2},{2,1},{3,0},{4,7},{5,6},{6,5},{7,4},{8,11},{9,10},{10,... | collective-permute-start | bytes 7688 | tf_op jit(solution)/shard_map/ppermute | solution.py:439
